TPU v7x, 32 devices: a whole 2x2x4 slice. The times are simulated.
32 devices in a mesh: fsdp: 4 (over z), ctx: 2 (over x), tp: 4 (over y, core).
Axes of the slice: x: 2, y: 2, z: 4, core: 2. Of those that a mesh axis runs over, the one named last changes fastest.
Arguments:
- hidden: bfloat16 [1536, 2048], P(('fsdp', 'ctx')), may hold values from -6 to 6
- embeds: bfloat16 [1536, 2048], P(('fsdp', 'ctx')), may hold values from -6 to 6
- cotangent: bfloat16 [1536, 2048], P(('fsdp', 'ctx')), may hold values from -6 to 6
- lengths: int32 [4, 3], P('fsdp'), may hold values from 1 to 192, 384 in all within a row
- attention_norm_gain: float32 [4096], replicated, may hold values from 0.5 to 1.5
- adapter_down_maps: bfloat16 [3, 4096, 128], replicated, may hold values from -0.09375 to 0.09375
- query_key_value_weight: bfloat16 [3, 4096, 4096], P(None, ('fsdp', 'ctx'), 'tp'), may hold values from -0.09375 to 0.09375
- adapter_up_maps: bfloat16 [3, 128, 4096], P(None, None, 'tp'), may hold values from -0.5 to 0.5
- attention_output_weight: bfloat16 [4096, 2048], P('tp', ('fsdp', 'ctx')), may hold values from -0.375 to 0.375
- feedforward_norm_gain: float32 [2048], replicated, may hold values from 0.5 to 1.5
- gate_up_weight: bfloat16 [2, 2048, 8192], P(None, ('fsdp', 'ctx'), 'tp'), may hold values from -0.125 to 0.125
- down_weight: bfloat16 [8192, 2048], P('tp', ('fsdp', 'ctx')), may hold values from -0.0625 to 0.0625
- mixer_norm_gain: float32 [2048], replicated, may hold values from 0.5 to 1.5
- mixer_gate_input_weight: bfloat16 [2, 2048, 4096], P(None, ('fsdp', 'ctx'), 'tp'), may hold values from -0.125 to 0.125
- state_map_weight: bfloat16 [2048, 256], replicated, may hold values from -0.125 to 0.125
- step_size_weight: bfloat16 [2048, 64], P(None, 'tp'), may hold values from -0.0625 to 0.0625
- mixer_input_taps: float32 [4, 4096], P(None, 'tp'), may hold values from -3 to 3
- mixer_input_tap_bias: float32 [4096], P('tp'), may hold values from -0.5 to 0.5
- state_map_taps: float32 [4, 256], replicated, may hold values from -3 to 3
- state_map_tap_bias: float32 [256], replicated, may hold values from -0.5 to 0.5
- step_size_bias: float32 [64], P('tp'), may hold values from -7 to -2
- log_decay_rate: float32 [64], P('tp'), may hold values from 0 to 2.77
- head_skip_weight: float32 [64], P('tp'), may hold values from 0.5 to 2
- gated_norm_gain: float32 [4096], P('tp'), may hold values from 0.5 to 1.5
- mixer_output_weight: bfloat16 [4096, 2048], P('tp', ('fsdp', 'ctx')), may hold values from -0.09375 to 0.09375
Outputs:
- out: bfloat16 [1536, 2048], P(('fsdp', 'ctx'))
- d_hidden: float32 [1536, 2048], P(('fsdp', 'ctx'))
- d_embeds: float32 [1536, 2048], P(('fsdp', 'ctx'))
- grad_g_attn: float32 [4096], replicated
- adapter_down_gradient: float32 [3, 4096, 128], replicated
- grad_w_qkv: float32 [3, 4096, 4096], P(None, ('fsdp', 'ctx'), 'tp')
- adapter_up_gradient: float32 [3, 128, 4096], P(None, None, 'tp')
- grad_w_o: float32 [4096, 2048], P('tp', ('fsdp', 'ctx'))
- grad_g_mlp: float32 [2048], replicated
- grad_w_gu: float32 [2, 2048, 8192], P(None, ('fsdp', 'ctx'), 'tp')
- grad_w_down: float32 [8192, 2048], P('tp', ('fsdp', 'ctx'))
- grad_g_mamba: float32 [2048], replicated
- grad_w_zx: float32 [2, 2048, 4096], P(None, ('fsdp', 'ctx'), 'tp')
- grad_w_bc: float32 [2048, 256], replicated
- grad_w_dt: float32 [2048, 64], P(None, 'tp')
- grad_conv_x: float32 [4, 4096], P(None, 'tp')
- grad_conv_x_bias: float32 [4096], P('tp')
- grad_conv_bc: float32 [4, 256], replicated
- grad_conv_bc_bias: float32 [256], replicated
- grad_dt_bias: float32 [64], P('tp')
- grad_a_log: float32 [64], P('tp')
- grad_d_skip: float32 [64], P('tp')
- grad_g_gate: float32 [4096], P('tp')
- grad_w_out: float32 [4096, 2048], P('tp', ('fsdp', 'ctx'))
Inputs may be any that keep to these rules, and one draw needn't show every extreme that they name: `lengths`: each row lists the 3 sequences of one group of 384 tokens in order; the row sums to 384 and its largest length is exactly 192.
All inputs are finite; a program needn't handle non-finite values.
Results may differ from a plain program's by a relative error of at most 0.035.
Values may be sent and summed in bfloat16 or wider, within the bound.
A program may use at most 384 MiB of HBM per device.

v0:
```python
import jax
import jax.numpy as jnp
from jax import lax
from jax.sharding import PartitionSpec as P

MODEL_WIDTH = 2048
AHD = 128
INNER = 4096
MIXER_HEAD_SIZE = 64
STATE = 128
SPAN = 128


highest = lax.Precision.HIGHEST
epsilon = 1e-05


def matrix_product(left, right):
    return jnp.dot(left, right, preferred_element_type=jnp.float32)


def matrix_product_transposed(left, right):
    return lax.dot_general(
        left, right, (((1,), (1,)), ((), ())), preferred_element_type=jnp.float32
    )


def outer_product_sum(left, right):
    return lax.dot_general(
        left, right, (((0,), (0,)), ((), ())), preferred_element_type=jnp.float32
    )


def rms_scale(values, gain):
    return values * lax.rsqrt(jnp.mean(values * values, axis=-1, keepdims=True) + epsilon) * gain


def gated_gelu(gate_in, up_in):
    return jax.nn.gelu(gate_in, approximate=True) * up_in


def layout(lengths_row, total_rows):
    ends = jnp.cumsum(lengths_row)
    slot_index = jnp.arange(total_rows, dtype=jnp.int32)
    passed = (slot_index[:, None] >= ends[None, :]).astype(jnp.int32)
    segment = jnp.sum(passed, axis=1)
    position = slot_index - jnp.sum(passed * lengths_row[None, :], axis=1)
    return (segment, position, slot_index)


def causal_conv(values, kernel, bias, position):
    total_rows = values.shape[0]
    total = values * kernel[0][None, :] + bias[None, :]
    for lag in range(1, kernel.shape[0]):
        shifted = jnp.concatenate(
            [jnp.zeros((lag, values.shape[1]), values.dtype), values[: total_rows - lag]], axis=0
        )
        keep = (position >= lag).astype(values.dtype)[:, None]
        total = total + shifted * keep * kernel[lag][None, :]
    return jax.nn.silu(total)


def rotate(values, position):
    half_dim = values.shape[-1] // 2
    inverse = 10000.0 ** (-jnp.arange(half_dim, dtype=jnp.float32) / half_dim)
    angle = position.astype(jnp.float32)[:, None] * inverse[None, :]
    cosine = jnp.cos(angle)[:, None, :]
    sine_part = jnp.sin(angle)[:, None, :]
    first_half = values[..., :half_dim]
    second_half = values[..., half_dim:]
    return jnp.concatenate(
        [
            first_half * cosine - second_half * sine_part,
            second_half * cosine + first_half * sine_part,
        ],
        axis=-1,
    )


def attend_core(pair_data, values, segment, slot_index, position, block_rows):
    group_row_block = values.shape[0]
    count_of_heads = values.shape[1] // AHD
    paired = pair_data.reshape(group_row_block, count_of_heads, 2, AHD)
    queries = rotate(paired[:, :, 0], position).astype(jnp.bfloat16)
    keys_all = rotate(paired[:, :, 1], position).astype(jnp.bfloat16)
    vals_all = values.reshape(group_row_block, count_of_heads, AHD).astype(jnp.bfloat16)
    scaling = AHD ** (-0.5)
    block_count = group_row_block // block_rows

    def one_block(inputs):
        query_part, query_seg, query_slot = inputs
        scores = (
            jnp.einsum("qhd,khd->hqk", query_part, keys_all, preferred_element_type=jnp.float32)
            * scaling
        )
        allowed = (query_seg[:, None] == segment[None, :]) & (
            query_slot[:, None] >= slot_index[None, :]
        )
        scores = jnp.where(allowed[None], scores, -1e30)
        weights = jnp.exp(scores)
        weights_low = (weights / jnp.sum(weights, axis=-1, keepdims=True)).astype(jnp.bfloat16)
        return jnp.einsum("hqk,khd->qhd", weights_low, vals_all, preferred_element_type=jnp.float32)

    mapped = lax.map(
        jax.checkpoint(one_block),
        (
            queries.reshape(block_count, block_rows, count_of_heads, AHD),
            segment.reshape(block_count, block_rows),
            slot_index.reshape(block_count, block_rows),
        ),
    )
    return mapped.reshape(group_row_block, count_of_heads * AHD)


def state_scan(inputs_x, step_size, b_mat, c_mat, decay_rate, segment):
    total_rows, count_of_heads, head_dim = inputs_x.shape
    spans = total_rows // SPAN
    log_decay = step_size * decay_rate[None, :]
    weighted = inputs_x * step_size[:, :, None]
    causal = jnp.arange(SPAN)[:, None] >= jnp.arange(SPAN)[None, :]

    def advance(carried_in, inputs):
        memory, last_segment = carried_in
        decay_part, weighted_part, b_part, c_part, seg_part = inputs
        running = jnp.cumsum(decay_part, axis=0)
        same_seq = (seg_part[:, None] == seg_part[None, :]) & causal
        intersection = jnp.dot(c_part, b_part.T, precision=highest)
        log_gap = jnp.where(same_seq[:, :, None], running[:, None, :] - running[None, :, :], 0.0)
        mixing = jnp.where(same_seq[:, :, None], jnp.exp(log_gap), 0.0) * intersection[:, :, None]
        output = jnp.einsum("tsh,shp->thp", mixing, weighted_part, precision=highest)
        carried = (seg_part == last_segment).astype(jnp.float32)
        reach_back = jnp.exp(running) * carried[:, None]
        output = (
            output
            + jnp.einsum("tn,hpn->thp", c_part, memory, precision=highest) * reach_back[:, :, None]
        )
        tail_seg = seg_part[-1]
        toward = (
            jnp.exp(running[-1][None, :] - running)
            * (seg_part == tail_seg).astype(jnp.float32)[:, None]
        )
        next_state = jnp.einsum("sh,shp,sn->hpn", toward, weighted_part, b_part, precision=highest)
        keep_all = jnp.exp(running[-1]) * (tail_seg == last_segment).astype(jnp.float32)
        next_state = next_state + memory * keep_all[:, None, None]
        return ((next_state, tail_seg), output)

    initial = (jnp.zeros((count_of_heads, head_dim, b_mat.shape[1]), jnp.float32), jnp.int32(-1))
    pieces = (
        log_decay.reshape(spans, SPAN, count_of_heads),
        weighted.reshape(spans, SPAN, count_of_heads, head_dim),
        b_mat.reshape(spans, SPAN, -1),
        c_mat.reshape(spans, SPAN, -1),
        segment.reshape(spans, SPAN),
    )
    last_state, outputs = lax.scan(jax.checkpoint(advance), initial, pieces)
    return outputs.reshape(total_rows, count_of_heads, head_dim)


def mamba_core(
    inner_in,
    step_in,
    bc_post,
    bias_in,
    decay_in,
    skip_weight_input,
    kernel_in,
    conv_bias_in,
    position,
    segment,
):
    group_row_block = inner_in.shape[0]
    count_of_heads = step_in.shape[1]
    mixer_result = causal_conv(inner_in, kernel_in, conv_bias_in, position)
    reshaped_tensor = mixer_result.reshape(group_row_block, count_of_heads, MIXER_HEAD_SIZE)
    step_size = jax.nn.softplus(step_in + bias_in[None, :])
    scan_result = state_scan(
        reshaped_tensor,
        step_size,
        bc_post[:, :STATE],
        bc_post[:, STATE:],
        -jnp.exp(decay_in),
        segment,
    )
    return (scan_result + skip_weight_input[None, :, None] * reshaped_tensor).reshape(
        group_row_block, count_of_heads * MIXER_HEAD_SIZE
    )


def collect(first_part, second_part):
    return (
        lax.all_gather(first_part, ("fsdp", "ctx"), axis=1, tiled=True),
        lax.all_gather(second_part, ("fsdp", "ctx"), axis=1, tiled=True),
    )


def collect_again(first_part, second_part):
    return (
        lax.all_gather(first_part, ("fsdp", "ctx"), axis=1, tiled=True),
        lax.all_gather(second_part, ("fsdp", "ctx"), axis=1, tiled=True),
    )


def tensor_sum(partial_sum):
    return lax.psum(partial_sum, "tp")


def tensor_pair(first_part, second_part):
    return (
        lax.psum(first_part.astype(jnp.bfloat16), "tp").astype(jnp.float32),
        lax.psum(second_part.astype(jnp.bfloat16), "tp").astype(jnp.float32),
    )


def heads_pair(first_part, second_part):
    return (
        lax.all_to_all(first_part, "ctx", split_axis=1, concat_axis=0, tiled=True),
        lax.all_to_all(second_part, "ctx", split_axis=1, concat_axis=0, tiled=True),
    )


def heads_one(values):
    return lax.all_to_all(values, "ctx", split_axis=1, concat_axis=0, tiled=True)


def tokens_pair(first_part, second_part):
    return (
        lax.all_to_all(first_part, "ctx", split_axis=0, concat_axis=1, tiled=True),
        lax.all_to_all(second_part, "ctx", split_axis=0, concat_axis=1, tiled=True),
    )


def tokens_one(values):
    return lax.all_to_all(values, "ctx", split_axis=0, concat_axis=1, tiled=True)


def per_device(
    hidden,
    embeds,
    cotangent,
    lengths,
    attention_norm_gain,
    adapter_down_maps,
    query_key_value_weight,
    adapter_up_maps,
    attention_output_weight,
    feedforward_norm_gain,
    gate_up_weight,
    down_weight,
    mixer_norm_gain,
    mixer_gate_input_weight,
    state_map_weight,
    step_size_weight,
    mixer_input_taps,
    mixer_input_tap_bias,
    state_map_taps,
    state_map_tap_bias,
    step_size_bias,
    log_decay_rate,
    head_skip_weight,
    gated_norm_gain,
    mixer_output_weight,
):
    tok_rows = hidden.shape[0]
    ctx_size = lax.axis_size("ctx")
    ctx_index = lax.axis_index("ctx")
    group_row_block = tok_rows * ctx_size
    block_rows = group_row_block // max(1, group_row_block // 1024)
    segment, position, slot_index = layout(lengths[0], group_row_block)
    hidden_f = hidden.astype(jnp.float32)
    embeds_f = embeds.astype(jnp.float32)
    attention_block_full, attn_out = collect(query_key_value_weight, attention_output_weight)
    joined = jnp.concatenate([hidden_f, embeds_f], axis=1)
    normed_a, norm_a_back = jax.vjp(rms_scale, joined, attention_norm_gain)
    attention_input_reduced = normed_a.astype(jnp.bfloat16)
    middle_reduced_precision = [
        matrix_product(attention_input_reduced, adapter_down_maps[group_member]).astype(
            jnp.bfloat16
        )
        for group_member in range(3)
    ]
    projected_input = [
        (
            matrix_product(attention_input_reduced, attention_block_full[group_member])
            + matrix_product(middle_reduced_precision[group_member], adapter_up_maps[group_member])
        ).astype(jnp.bfloat16)
        for group_member in range(3)
    ]
    tp_heads = projected_input[0].shape[1] // AHD
    pair_data = jnp.stack(
        [
            projected_input[0].reshape(tok_rows, tp_heads, AHD),
            projected_input[1].reshape(tok_rows, tp_heads, AHD),
        ],
        axis=2,
    ).reshape(tok_rows, tp_heads * 2 * AHD)
    pair_heads, value_heads = heads_pair(pair_data, projected_input[2])
    attn_core, attn_pull = jax.vjp(
        lambda pairs_in, values_in: attend_core(
            pairs_in, values_in, segment, slot_index, position, block_rows
        ),
        pair_heads.astype(jnp.float32),
        value_heads.astype(jnp.float32),
    )
    attn_tokens = tokens_one(attn_core.astype(jnp.bfloat16))
    after_attn = hidden_f + tensor_sum(matrix_product(attn_tokens, attn_out))
    mlp_big, mlp_down = collect(gate_up_weight, down_weight)
    normed_m, norm_m_back = jax.vjp(rms_scale, after_attn, feedforward_norm_gain)
    xm_low = normed_m.astype(jnp.bfloat16)
    gate_pre = matrix_product(xm_low, mlp_big[0])
    up_pre = matrix_product(xm_low, mlp_big[1])
    activated, act_back = jax.vjp(gated_gelu, gate_pre, up_pre)
    hid_low = activated.astype(jnp.bfloat16)
    after_mlp = after_attn + tensor_sum(matrix_product(hid_low, mlp_down))
    mamba_big, mamba_out = collect(mixer_gate_input_weight, mixer_output_weight)
    normed_n, norm_n_back = jax.vjp(rms_scale, after_mlp, mixer_norm_gain)
    xn_low = normed_n.astype(jnp.bfloat16)
    gate_z = matrix_product(xn_low, mamba_big[0])
    inner_x = matrix_product(xn_low, mamba_big[1]).astype(jnp.bfloat16)
    step_raw = matrix_product(xn_low, step_size_weight).astype(jnp.bfloat16)
    bc_low = matrix_product(xn_low, state_map_weight).astype(jnp.bfloat16)
    x_heads, step_heads = heads_pair(inner_x, step_raw)
    bc_group = lax.all_gather(bc_low, "ctx", axis=0, tiled=True)
    bc_post, bc_conv_pull = jax.vjp(
        lambda values_in, kernel_in, conv_bias_in: causal_conv(
            values_in, kernel_in, conv_bias_in, position
        ),
        bc_group.astype(jnp.float32),
        state_map_taps,
        state_map_tap_bias,
    )
    heads_on_device_share = step_heads.shape[1]
    start_offset = ctx_index * heads_on_device_share
    channel_count_here = heads_on_device_share * MIXER_HEAD_SIZE
    channel_offset_begin = start_offset * MIXER_HEAD_SIZE
    bias_local = lax.dynamic_slice_in_dim(step_size_bias, start_offset, heads_on_device_share)
    decay_local = lax.dynamic_slice_in_dim(log_decay_rate, start_offset, heads_on_device_share)
    skip_local = lax.dynamic_slice_in_dim(head_skip_weight, start_offset, heads_on_device_share)
    kernel_local = lax.dynamic_slice_in_dim(
        mixer_input_taps, channel_offset_begin, channel_count_here, 1
    )
    conv_bias_local = lax.dynamic_slice_in_dim(
        mixer_input_tap_bias, channel_offset_begin, channel_count_here, 0
    )
    scan_out, scan_pull = jax.vjp(
        lambda xs_in, step_in, bcp_in, bias_in, decay_in, skip_weight_input, kernel_in, conv_bias_in: mamba_core(
            xs_in,
            step_in,
            bcp_in,
            bias_in,
            decay_in,
            skip_weight_input,
            kernel_in,
            conv_bias_in,
            position,
            segment,
        ),
        x_heads.astype(jnp.float32),
        step_heads.astype(jnp.float32),
        bc_post,
        bias_local,
        decay_local,
        skip_local,
        kernel_local,
        conv_bias_local,
    )
    y_tokens = tokens_one(scan_out.astype(jnp.bfloat16)).astype(jnp.float32)
    silu_z = jax.nn.silu(gate_z)
    gated = y_tokens * silu_z
    total_sq = tensor_sum(jnp.sum(gated * gated, axis=1))
    inverse = lax.rsqrt(total_sq / INNER + epsilon)[:, None]
    yn_low = (gated * inverse * gated_norm_gain).astype(jnp.bfloat16)
    after_mamba = after_mlp + tensor_sum(matrix_product(yn_low, mamba_out))
    result = after_mamba.astype(jnp.bfloat16)
    grad_out = cotangent.astype(jnp.float32)
    mamba_big, mamba_out = collect_again(mixer_gate_input_weight, mixer_output_weight)
    d_yn = matrix_product_transposed(cotangent, mamba_out)
    grad_w_out = outer_product_sum(yn_low, cotangent)
    gain_part = d_yn * gated_norm_gain
    cross = tensor_sum(jnp.sum(gain_part * gated, axis=1))
    grad_g_gate = jnp.sum(d_yn * gated * inverse, axis=0)
    d_gated = gain_part * inverse - gated * inverse**3 * (cross / INNER)[:, None]
    d_y = (d_gated * silu_z).astype(jnp.bfloat16)
    sigmoid_z = jax.nn.sigmoid(gate_z)
    d_z = (d_gated * y_tokens * sigmoid_z * (1.0 + gate_z * (1.0 - sigmoid_z))).astype(jnp.bfloat16)
    dy_heads = heads_one(d_y)
    (
        d_xs,
        d_step,
        d_bc_post,
        grad_bias_local,
        grad_decay_local,
        grad_skip_local,
        grad_kernel_local,
        grad_conv_bias_local,
    ) = scan_pull(dy_heads.astype(jnp.float32))
    d_xs_tok, d_step_tok = tokens_pair(d_xs.astype(jnp.bfloat16), d_step.astype(jnp.bfloat16))
    d_bc_ctx = lax.psum(d_bc_post.astype(jnp.bfloat16), "ctx").astype(jnp.float32)
    dxn_part = (
        matrix_product_transposed(d_z, mamba_big[0])
        + matrix_product_transposed(d_xs_tok, mamba_big[1])
        + matrix_product_transposed(d_step_tok, step_size_weight)
    )
    grad_w_zx = jnp.stack([outer_product_sum(xn_low, d_z), outer_product_sum(xn_low, d_xs_tok)])
    grad_w_dt = outer_product_sum(xn_low, d_step_tok)
    dxn_sum, d_bc_full = tensor_pair(dxn_part, d_bc_ctx)
    d_bc_pre = bc_conv_pull(d_bc_full)[0]
    d_bc_mine = lax.dynamic_slice_in_dim(d_bc_pre, ctx_index * tok_rows, tok_rows, 0)
    own_rows = (slot_index // tok_rows == ctx_index).astype(jnp.float32)[:, None]
    ignored_part, grad_conv_bc, grad_conv_bc_bias = bc_conv_pull(d_bc_full * own_rows)
    d_bc_low = d_bc_mine.astype(jnp.bfloat16)
    dxn_total = dxn_sum + matrix_product_transposed(d_bc_low, state_map_weight)
    grad_w_bc = outer_product_sum(xn_low, d_bc_low)
    d_norm_n, grad_g_mamba = norm_n_back(dxn_total)
    d_after_mlp = grad_out + d_norm_n
    shard_heads = step_size_bias.shape[0]
    zero_heads = jnp.zeros((shard_heads,), jnp.float32)
    grad_dt_bias = lax.dynamic_update_slice_in_dim(zero_heads, grad_bias_local, start_offset, 0)
    grad_a_log = lax.dynamic_update_slice_in_dim(zero_heads, grad_decay_local, start_offset, 0)
    grad_d_skip = lax.dynamic_update_slice_in_dim(zero_heads, grad_skip_local, start_offset, 0)
    grad_conv_x = lax.dynamic_update_slice_in_dim(
        jnp.zeros(mixer_input_taps.shape, jnp.float32), grad_kernel_local, channel_offset_begin, 1
    )
    grad_conv_x_bias = lax.dynamic_update_slice_in_dim(
        jnp.zeros(mixer_input_tap_bias.shape, jnp.float32),
        grad_conv_bias_local,
        channel_offset_begin,
        0,
    )
    mlp_big, mlp_down = collect_again(gate_up_weight, down_weight)
    d_mlp_low = d_after_mlp.astype(jnp.bfloat16)
    d_hid = matrix_product_transposed(d_mlp_low, mlp_down)
    grad_w_down = outer_product_sum(hid_low, d_mlp_low)
    d_gate, d_up = act_back(d_hid)
    d_gate_low = d_gate.astype(jnp.bfloat16)
    d_up_low = d_up.astype(jnp.bfloat16)
    d_xm = tensor_sum(
        matrix_product_transposed(d_gate_low, mlp_big[0])
        + matrix_product_transposed(d_up_low, mlp_big[1])
    )
    grad_w_gu = jnp.stack(
        [outer_product_sum(xm_low, d_gate_low), outer_product_sum(xm_low, d_up_low)]
    )
    d_norm_m, grad_g_mlp = norm_m_back(d_xm)
    d_after_attn = d_after_mlp + d_norm_m
    attention_block_full, attn_out = collect_again(query_key_value_weight, attention_output_weight)
    d_attn_low = d_after_attn.astype(jnp.bfloat16)
    d_tokens = matrix_product_transposed(d_attn_low, attn_out).astype(jnp.bfloat16)
    grad_w_o = outer_product_sum(attn_tokens, d_attn_low)
    d_core = heads_one(d_tokens)
    d_pairs, d_values = attn_pull(d_core.astype(jnp.float32))
    d_pair_tok, d_value_tok = tokens_pair(
        d_pairs.astype(jnp.bfloat16), d_values.astype(jnp.bfloat16)
    )
    d_paired = d_pair_tok.reshape(tok_rows, tp_heads, 2, AHD)
    projection_gradient = [
        d_paired[:, :, 0].reshape(tok_rows, tp_heads * AHD),
        d_paired[:, :, 1].reshape(tok_rows, tp_heads * AHD),
        d_value_tok,
    ]
    dxa_part = (
        matrix_product_transposed(projection_gradient[0], attention_block_full[0])
        + matrix_product_transposed(projection_gradient[1], attention_block_full[1])
        + matrix_product_transposed(projection_gradient[2], attention_block_full[2])
    )
    dmid_part = jnp.concatenate(
        [
            matrix_product_transposed(
                projection_gradient[group_member], adapter_up_maps[group_member]
            )
            for group_member in range(3)
        ],
        axis=1,
    )
    grad_w_qkv = jnp.stack(
        [
            outer_product_sum(attention_input_reduced, projection_gradient[group_member])
            for group_member in range(3)
        ]
    )
    adapter_up_gradient = jnp.stack(
        [
            outer_product_sum(
                middle_reduced_precision[group_member], projection_gradient[group_member]
            )
            for group_member in range(3)
        ]
    )
    dxa_sum, dmid_sum = tensor_pair(dxa_part, dmid_part)
    dmid_low = dmid_sum.astype(jnp.bfloat16)
    rank_column_block = adapter_down_maps.shape[2]
    middle_gradient_pieces = [
        dmid_low[:, group_member * rank_column_block : (group_member + 1) * rank_column_block]
        for group_member in range(3)
    ]
    dxa_total = (
        dxa_sum
        + matrix_product_transposed(middle_gradient_pieces[0], adapter_down_maps[0])
        + matrix_product_transposed(middle_gradient_pieces[1], adapter_down_maps[1])
        + matrix_product_transposed(middle_gradient_pieces[2], adapter_down_maps[2])
    )
    adapter_down_gradient = jnp.stack(
        [
            outer_product_sum(attention_input_reduced, middle_gradient_pieces[group_member])
            for group_member in range(3)
        ]
    )
    d_joined, grad_g_attn = norm_a_back(dxa_total)
    d_hidden = d_after_attn + d_joined[:, :MODEL_WIDTH]
    d_embeds = d_joined[:, MODEL_WIDTH:]
    grad_w_qkv, grad_w_o, grad_w_gu, grad_w_down, grad_w_zx, grad_w_out = (
        lax.psum_scatter(
            grad_w_qkv.astype(jnp.bfloat16), ("fsdp", "ctx"), scatter_dimension=1, tiled=True
        ).astype(jnp.float32),
        lax.psum_scatter(
            grad_w_o.astype(jnp.bfloat16), ("fsdp", "ctx"), scatter_dimension=1, tiled=True
        ).astype(jnp.float32),
        lax.psum_scatter(
            grad_w_gu.astype(jnp.bfloat16), ("fsdp", "ctx"), scatter_dimension=1, tiled=True
        ).astype(jnp.float32),
        lax.psum_scatter(
            grad_w_down.astype(jnp.bfloat16), ("fsdp", "ctx"), scatter_dimension=1, tiled=True
        ).astype(jnp.float32),
        lax.psum_scatter(
            grad_w_zx.astype(jnp.bfloat16), ("fsdp", "ctx"), scatter_dimension=1, tiled=True
        ).astype(jnp.float32),
        lax.psum_scatter(
            grad_w_out.astype(jnp.bfloat16), ("fsdp", "ctx"), scatter_dimension=1, tiled=True
        ).astype(jnp.float32),
    )
    (
        grad_g_attn,
        adapter_down_gradient,
        adapter_up_gradient,
        grad_g_mlp,
        grad_g_mamba,
        grad_w_bc,
        grad_w_dt,
        grad_conv_x,
        grad_conv_x_bias,
        grad_conv_bc,
        grad_conv_bc_bias,
        grad_dt_bias,
        grad_a_log,
        grad_d_skip,
        grad_g_gate,
    ) = (
        lax.psum(grad_g_attn.astype(jnp.bfloat16), ("fsdp", "ctx")).astype(jnp.float32),
        lax.psum(adapter_down_gradient.astype(jnp.bfloat16), ("fsdp", "ctx")).astype(jnp.float32),
        lax.psum(adapter_up_gradient.astype(jnp.bfloat16), ("fsdp", "ctx")).astype(jnp.float32),
        lax.psum(grad_g_mlp.astype(jnp.bfloat16), ("fsdp", "ctx")).astype(jnp.float32),
        lax.psum(grad_g_mamba.astype(jnp.bfloat16), ("fsdp", "ctx")).astype(jnp.float32),
        lax.psum(grad_w_bc.astype(jnp.bfloat16), ("fsdp", "ctx")).astype(jnp.float32),
        lax.psum(grad_w_dt.astype(jnp.bfloat16), ("fsdp", "ctx")).astype(jnp.float32),
        lax.psum(grad_conv_x.astype(jnp.bfloat16), ("fsdp", "ctx")).astype(jnp.float32),
        lax.psum(grad_conv_x_bias.astype(jnp.bfloat16), ("fsdp", "ctx")).astype(jnp.float32),
        lax.psum(grad_conv_bc.astype(jnp.bfloat16), ("fsdp", "ctx")).astype(jnp.float32),
        lax.psum(grad_conv_bc_bias.astype(jnp.bfloat16), ("fsdp", "ctx")).astype(jnp.float32),
        lax.psum(grad_dt_bias.astype(jnp.bfloat16), ("fsdp", "ctx")).astype(jnp.float32),
        lax.psum(grad_a_log.astype(jnp.bfloat16), ("fsdp", "ctx")).astype(jnp.float32),
        lax.psum(grad_d_skip.astype(jnp.bfloat16), ("fsdp", "ctx")).astype(jnp.float32),
        lax.psum(grad_g_gate.astype(jnp.bfloat16), ("fsdp", "ctx")).astype(jnp.float32),
    )
    return (
        result,
        d_hidden,
        d_embeds,
        grad_g_attn,
        adapter_down_gradient,
        grad_w_qkv,
        adapter_up_gradient,
        grad_w_o,
        grad_g_mlp,
        grad_w_gu,
        grad_w_down,
        grad_g_mamba,
        grad_w_zx,
        grad_w_bc,
        grad_w_dt,
        grad_conv_x,
        grad_conv_x_bias,
        grad_conv_bc,
        grad_conv_bc_bias,
        grad_dt_bias,
        grad_a_log,
        grad_d_skip,
        grad_g_gate,
        grad_w_out,
    )


def solution(mesh):
    placed = (
        P(("fsdp", "ctx"), None),
        P(("fsdp", "ctx"), None),
        P(("fsdp", "ctx"), None),
        P("fsdp", None),
        P(),
        P(),
        P(None, ("fsdp", "ctx"), "tp"),
        P(None, None, "tp"),
        P("tp", ("fsdp", "ctx")),
        P(),
        P(None, ("fsdp", "ctx"), "tp"),
        P("tp", ("fsdp", "ctx")),
        P(),
        P(None, ("fsdp", "ctx"), "tp"),
        P(),
        P(None, "tp"),
        P(None, "tp"),
        P("tp"),
        P(),
        P(),
        P("tp"),
        P("tp"),
        P("tp"),
        P("tp"),
        P("tp", ("fsdp", "ctx")),
    )
    return jax.shard_map(
        per_device,
        mesh=mesh,
        in_specs=placed,
        out_specs=(
            P(("fsdp", "ctx"), None),
            P(("fsdp", "ctx"), None),
            P(("fsdp", "ctx"), None),
            P(),
            P(),
            P(None, ("fsdp", "ctx"), "tp"),
            P(None, None, "tp"),
            P("tp", ("fsdp", "ctx")),
            P(),
            P(None, ("fsdp", "ctx"), "tp"),
            P("tp", ("fsdp", "ctx")),
            P(),
            P(None, ("fsdp", "ctx"), "tp"),
            P(),
            P(None, "tp"),
            P(None, "tp"),
            P("tp"),
            P(),
            P(),
            P("tp"),
            P("tp"),
            P("tp"),
            P("tp"),
            P("tp", ("fsdp", "ctx")),
        ),
        check_vma=False,
    )
```

profile of v0, /device:TPU:0, one launch (start us, length us, event | category | flops | bytes accessed | tf_op | source)
XLA Modules:
  0.0 3048.3 jit_solution(14720691103175746514)
XLA Ops:
  17.3 475.4 %all-gather.7.cloned.1.call-done = bf16[3,4096,1024]{2,1,0:T(8,128)(2,1)} async-done(((bf16[3,512,1024]{2,1,0:T(8,128)(2,1)}), bf16[3,4096,1024]{2,1,0:T(8,128)(2,1)}) %all-gather.7.cloned.1.call-update) | async-done | bytes 25165840 | tf_op jit(solution)/shard_map/all_gather | solution.py:191
  492.7 5.2 fusion.79
  499.9 4.2 all-to-all-start.1
  504.1 5.3 fusion.77
  509.6 5.2 fusion.75
  518.9 3.5 all-to-all-start
  524.7 8.6 all-to-all-done
  542.5 13.9 all_to_all.177
  556.5 20.5 all-gather.9.cloned.1.call-done
  577.0 4.3 fusion.249
  582.8 39.7 %all-reduce.43.cloned.1.call-done = f32[192,2048]{1,0:T(8,128)} async-done(((f32[192,2048]{1,0:T(8,128)}), f32[192,2048]{1,0:T(8,128)}) %all-reduce.43.cloned.1.call-update) | async-done | bytes 1572880 | tf_op jit(solution)/shard_map/psum | solution.py:204
  625.7 226.2 %all-gather.11.cloned.1.call-done = bf16[2,2048,2048]{2,1,0:T(8,128)(2,1)} async-done(((bf16[2,256,2048]{2,1,0:T(8,128)(2,1)}), bf16[2,2048,2048]{2,1,0:T(8,128)(2,1)}) %all-gather.11.cloned.1.call-update) | async-done | bytes 16777232 | tf_op jit(solution)/shard_map/all_gather | solution.py:191
  851.9 5.5 fusion.81
  858.6 7.5 multiply_convert_fusion.3
  866.1 110.9 %all-gather.13.cloned.1.call-done = bf16[2048,2048]{1,0:T(8,128)(2,1)} async-done(((bf16[2048,256]{1,0:T(8,128)(2,1)}), bf16[2048,2048]{1,0:T(8,128)(2,1)}) %all-gather.13.cloned.1.call-update) | async-done | bytes 8388624 | tf_op jit(solution)/shard_map/all_gather | solution.py:192
  977.0 6.6 fusion.250
  988.6 36.2 %all-reduce.45.cloned.1.call-done = f32[192,2048]{1,0:T(8,128)} async-done(((f32[192,2048]{1,0:T(8,128)}), f32[192,2048]{1,0:T(8,128)}) %all-reduce.45.cloned.1.call-update) | async-done | bytes 1572880 | tf_op jit(solution)/shard_map/psum | solution.py:204
  1027.2 5.3 all_gather.32
  1033.5 3.8 all-to-all-start.3
  1038.6 112.9 %all-gather.15.cloned.1.call-done = bf16[2,2048,1024]{2,1,0:T(8,128)(2,1)} async-done(((bf16[2,256,1024]{2,1,0:T(8,128)(2,1)}), bf16[2,2048,1024]{2,1,0:T(8,128)(2,1)}) %all-gather.15.cloned.1.call-update) | async-done | bytes 8388624 | tf_op jit(solution)/shard_map/all_gather | solution.py:191
  1155.7 4.6 all-to-all-start.4
  1162.1 9.6 all-to-all-done.4
  1183.6 39.8 %while.56 = (s32[]{:T(128)}, f32[8,64,128]{2,1,0:T(8,128)S(1)}, s32[]{:T(128)}, f32[3,128,8,64]{1,3,2,0:T(8,128)}, f32[3,8,64,128]{3,2,1,0:T(8,128)}, /*index=5*...) while((s32[]{:T(128)}, f32[8,64,128]{2,1,0:T(8,128)S(1)}, ...), condition=%wide.region_11.12_spmd.clone, body=%wide.region_9.11_spmd.clone.sunk | while | flops 328387072 | bytes 3126145 | solution.py:155
  1231.0 4.2 all-to-all-start.5
  1237.2 3.9 all-to-all-done.5
  1242.3 4.7 multiply_reduce_fusion.18
  1247.1 5.6 psum.184
  1252.8 5.8 multiply_reduce_fusion.12
  1258.6 6.6 psum.186
  1287.8 102.8 %while.57 = (s32[]{:T(128)}, f32[8,64,128]{2,1,0:T(8,128)}, f32[3,128,8]{2,1,0:T(8,128)}, f32[3,128,8,64]{1,3,2,0:T(8,128)}, f32[3,128,128]{2,1,0:T(8,128)}, /*i...) while((s32[]{:T(128)}, f32[8,64,128]{2,1,0:T(8,128)}, ...), condition=%wide.region_26.27_spmd.clone, body=%wide.region_17.26_spmd.clone.sunk | while | flops 783364608 | bytes 9512937 | solution.py:155
  1408.7 5.0 all-to-all-done.7
  1417.0 3.9 fusion.90
  1421.0 3.7 fusion.95
  1426.4 4.4 fusion.236
  1430.8 30.6 %all-reduce.55.cloned.1.call-done = (bf16[384,256]{1,0:T(8,128)(2,1)}, bf16[192,2048]{1,0:T(8,128)(2,1)}) async-done(((bf16[384,256]{1,0:T(8,128)(2,1)}, bf16[192,2048]{1,0:T(8,128)(2,1)}), (bf16[384,256]{1,0:T(8,128)(2,1)}, bf16[192,2048]{1,0:T(8,128)(2,1)})) %all-reduce.55.cloned.1.call-update) | async-done | bytes 983056 | tf_op jit(solution)/shard_map/psum | solution.py:210
  1467.9 7.4 multiply_convert_fusion.1
  1475.3 6.9 fusion.80
  1482.3 4.1 fusion.94
  1486.4 69.0 %all-reduce.49.cloned.1.call-done = (f32[192,2048]{1,0:T(8,128)}, f32[192,2048]{1,0:T(8,128)}) async-done(((f32[192,2048]{1,0:T(8,128)}, f32[192,2048]{1,0:T(8,128)}), (f32[192,2048]{1,0:T(8,128)}, f32[192,2048]{1,0:T(8,128)})) %all-reduce.49.cloned.1.call-update) | async-done | bytes 3145744 | tf_op jit(solution)/shard_map/psum | solution.py:204
  1562.3 9.5 all_to_all.178
  1583.1 4.2 all-to-all-start.11
  1593.2 3.5 all-to-all-start.10
  1599.4 6.0 all-to-all-done.10
  1606.8 4.2 slice_reduce_fusion
  1612.2 6.3 fusion.74
  1618.5 6.3 fusion.85
  1624.8 8.0 fusion.86
  1641.6 36.4 %all-reduce.53.cloned.1.call-done = (bf16[192,4096]{1,0:T(8,128)(2,1)}, bf16[192,384]{1,0:T(8,128)(2,1)}) async-done(((bf16[192,4096]{1,0:T(8,128)(2,1)}, bf16[192,384]{1,0:T(8,128)(2,1)}), (bf16[192,4096]{1,0:T(8,128)(2,1)}, bf16[192,384]{1,0:T(8,128)(2,1)})) %all-reduce.53.cloned.1.call-update) | async-done | bytes 1720336 | tf_op jit(solution)/shard_map/psum | solution.py:209
  1684.3 4.7 convolution_convert_fusion.5
  1696.7 7.6 pad_maximum_fusion.2
  1705.4 7.2 convolution_convert_fusion
  1713.8 3.6 convert_bitcast_fusion
  1719.7 6.8 pad_maximum_fusion.1
  1734.0 10.9 pad_maximum_fusion
  1758.4 38.7 %all-reduce.31 = (bf16[4096]{0:T(1024)(128)(2,1)S(1)}, bf16[2048]{0:T(1024)(128)(2,1)S(1)}, bf16[2048]{0:T(1024)(128)(2,1)S(1)}, bf16[4,1024]{1,0:T(4,128)(2,1)S...) all-reduce(bf16[4096]{0:T(1024)(128)(2,1)S(1)} %get-tuple-element.8, ...), channel_id=1, replica_groups=mesh['fsdp'=4,'ctx'=2,'tp'=4] {'fsdp','ctx'}, use_global_device_ids=true, to_apply=%region_40.41 | all-reduce | flops 15664 | bytes 62656 | tf_op jit(solution)/shard_map/psum | solution.py:547
  1810.8 143.5 %all-reduce.51.cloned.1.call-done = (bf16[3,4096,128]{2,1,0:T(8,128)(2,1)}, bf16[3,128,1024]{2,1,0:T(8,128)(2,1)}, bf16[2048,256]{1,0:T(8,128)(2,1)}, bf16[2048,16]{0,1:T(8,128)(2,1)}) async-done(((bf16[3,4096,128]{2,1,0:T(8,128)(2,1)}, bf16[3,128,1024]{2,1,0:T(8,128)(2,1)}, bf16[2048,256]{1,0:T(8,128)(2,1)}, bf16[2048,16]{0,1:T(8,128)(2,1)}), (bf16[3,4096,128]{2,1,0:T(8,128)(2,1)}, ...) | async-done | bytes 5046288 | tf_op jit(solution)/shard_map/psum | solution.py:548
  1954.3 5.1 convert_element_type.575
  1963.0 83.0 %reduce-scatter.9.cloned.1.call-done = bf16[1024,256]{1,0:T(8,128)(2,1)} async-done(((bf16[1024,2048]{1,0:T(8,128)(2,1)}), bf16[1024,256]{1,0:T(8,128)(2,1)}) %reduce-scatter.9.cloned.1.call-update) | async-done | bytes 524304 | tf_op jit(solution)/shard_map/reduce_scatter | solution.py:514
  2048.1 148.6 %reduce-scatter.15.cloned.1.call-done = bf16[2,256,1024]{2,1,0:T(8,128)(2,1)} async-done(((bf16[2,2048,1024]{2,1,0:T(8,128)(2,1)}), bf16[2,256,1024]{2,1,0:T(8,128)(2,1)}) %reduce-scatter.15.cloned.1.call-update) | async-done | bytes 1048592 | tf_op jit(solution)/shard_map/reduce_scatter | solution.py:523
  2199.5 147.7 %reduce-scatter.13.cloned.1.call-done = bf16[2048,256]{1,0:T(8,128)(2,1)} async-done(((bf16[2048,2048]{1,0:T(8,128)(2,1)}), bf16[2048,256]{1,0:T(8,128)(2,1)}) %reduce-scatter.13.cloned.1.call-update) | async-done | bytes 1048592 | tf_op jit(solution)/shard_map/reduce_scatter | solution.py:520
  2349.9 279.4 %reduce-scatter.11.cloned.1.call-done = bf16[2,256,2048]{2,1,0:T(8,128)(2,1)} async-done(((bf16[2,2048,2048]{2,1,0:T(8,128)(2,1)}), bf16[2,256,2048]{2,1,0:T(8,128)(2,1)}) %reduce-scatter.11.cloned.1.call-update) | async-done | bytes 2097168 | tf_op jit(solution)/shard_map/reduce_scatter | solution.py:517
  2629.3 4.1 convert_element_type.582
  2633.4 402.7 %reduce-scatter.7.cloned.1.call-done = bf16[3,512,1024]{2,1,0:T(8,128)(2,1)} async-done(((bf16[3,4096,1024]{2,1,0:T(8,128)(2,1)}), bf16[3,512,1024]{2,1,0:T(8,128)(2,1)}) %reduce-scatter.7.cloned.1.call-update) | async-done | bytes 3145744 | tf_op jit(solution)/shard_map/reduce_scatter | solution.py:511
  3036.2 5.4 convert_element_type.576
  (839 shorter events, 358.9 us)
Async XLA Ops:
  7.2 1019.5 %copy-start = (bf16[2048,256]{1,0:T(8,128)(2,1)S(1)}, bf16[2048,256]{1,0:T(8,128)(2,1)}, u32[]{:S(2)}) copy-start(bf16[2048,256]{1,0:T(8,128)(2,1)} %param.43) | copy-start | bytes 3145732
  7.2 485.5 %all-gather.7.cloned.1.call-start = ((), (), s32[]{:S(2)}) async-start(), calls=%async_computation.18 | async-start | bytes 28311552 | tf_op jit(solution)/shard_map/all_gather | solution.py:191
  8.0 569.0 %all-gather.9.cloned.1.call-start = ((), (), s32[]{:S(2)}) async-start(), calls=%async_computation.19 | async-start | bytes 4718592 | tf_op jit(solution)/shard_map/all_gather | solution.py:192
  13.2 496.4 %copy-start.2 = (bf16[192,4096]{1,0:T(8,128)(2,1)}, bf16[192,4096]{1,0:T(8,128)(2,1)S(1)}, u32[]{:S(2)}) copy-start(bf16[192,4096]{1,0:T(8,128)(2,1)S(1)} %multiply_convert_fusion) | copy-start | bytes 4718596
  16.1 493.2 %copy-start.88 = (bf16[192,128]{1,0:T(8,128)(2,1)}, bf16[192,128]{1,0:T(8,128)(2,1)S(1)}, u32[]{:S(2)}) copy-start(bf16[192,128]{1,0:T(8,128)(2,1)S(1)} %convolution_convert_fusion.22) | copy-start | bytes 147460
  16.7 498.1 %copy-start.86 = (bf16[192,128]{1,0:T(8,128)(2,1)}, bf16[192,128]{1,0:T(8,128)(2,1)S(1)}, u32[]{:S(2)}) copy-start(bf16[192,128]{1,0:T(8,128)(2,1)S(1)} %convolution_convert_fusion.23) | copy-start | bytes 147460
  17.3 480.6 %copy-start.90 = (bf16[192,128]{1,0:T(8,128)(2,1)}, bf16[192,128]{1,0:T(8,128)(2,1)S(1)}, u32[]{:S(2)}) copy-start(bf16[192,128]{1,0:T(8,128)(2,1)S(1)} %convolution_convert_fusion.21) | copy-start | bytes 147460
  499.9 19.0 all-to-all-start.1
  518.9 14.5 all-to-all-start
  522.4 100.1 %all-reduce.43.cloned.1.call-start = ((), (), s32[]{:S(2)}) async-start(), calls=%async_computation.20 | async-start | bytes 3145728 | tf_op jit(solution)/shard_map/psum | solution.py:204
  556.5 24.9 copy-start.29
  581.3 270.6 %all-gather.11.cloned.1.call-start = ((), (), s32[]{:S(2)}) async-start(), calls=%async_computation.21 | async-start | bytes 18874368 | tf_op jit(solution)/shard_map/all_gather | solution.py:191
  581.9 42.6 %copy-start.108 = (f32[2048]{0:T(1024)S(1)}, f32[2048]{0:T(1024)}, u32[]{:S(2)}) copy-start(f32[2048]{0:T(1024)} %param.38) | copy-start | bytes 24580
  581.9 395.0 %all-gather.13.cloned.1.call-start = ((), (), s32[]{:S(2)}) async-start(), calls=%async_computation.22 | async-start | bytes 9437184 | tf_op jit(solution)/shard_map/all_gather | solution.py:192
  582.5 442.3 %all-reduce.45.cloned.1.call-start = ((), (), s32[]{:S(2)}) async-start(), calls=%async_computation.23 | async-start | bytes 3145728 | tf_op jit(solution)/shard_map/psum | solution.py:204
  624.4 233.0 %copy-start.155 = (f32[192]{0:T(256)}, f32[192]{0:T(256)S(1)}, u32[]{:S(2)}) copy-start(f32[192]{0:T(256)S(1)} %get-tuple-element.953) | copy-start | bytes 2308
  624.4 400.4 %copy-start.4 = (f32[192,2048]{1,0:T(8,128)}, f32[192,2048]{1,0:T(8,128)S(1)}, u32[]{:S(2)}) copy-start(f32[192,2048]{1,0:T(8,128)S(1)} %get-tuple-element.954) | copy-start | bytes 4718596
  624.5 233.0 %copy-start.137 = (f32[192]{0:T(256)}, f32[192]{0:T(256)S(1)}, u32[]{:S(2)}) copy-start(f32[192]{0:T(256)S(1)} %fusion.231) | copy-start | bytes 2308
  983.6 167.9 %all-gather.15.cloned.1.call-start = ((), (), s32[]{:S(2)}) async-start(), calls=%async_computation.24 | async-start | bytes 9437184 | tf_op jit(solution)/shard_map/all_gather | solution.py:191
  984.4 268.4 %all-gather.17.cloned.1.call-start = ((), (), s32[]{:S(2)}) async-start(), calls=%async_computation.25 | async-start | bytes 4718592 | tf_op jit(solution)/shard_map/all_gather | solution.py:192
  985.2 250.0 %copy-start.112 = (f32[384]{0:T(512)}, f32[384]{0:T(512)S(1)}, u32[]{:S(2)}) copy-start(f32[384]{0:T(512)S(1)} %get-tuple-element.1005) | copy-start | bytes 4612
  985.2 250.7 %copy-start.115 = (f32[384]{0:T(512)}, f32[384]{0:T(512)S(1)}, u32[]{:S(2)}) copy-start(f32[384]{0:T(512)S(1)} %get-tuple-element.1006) | copy-start | bytes 4612
  985.2 251.3 %copy-start.118 = (f32[384]{0:T(512)}, f32[384]{0:T(512)S(1)}, u32[]{:S(2)}) copy-start(f32[384]{0:T(512)S(1)} %get-tuple-element.1007) | copy-start | bytes 4612
  986.4 50.9 %copy-start.145 = (f32[1,256]{1,0:T(1,128)}, f32[1,256]{1,0:T(1,128)S(1)}, u32[]{:S(2)}) copy-start(f32[1,256]{1,0:T(1,128)S(1)} %get-tuple-element.999) | copy-start | bytes 3076
  986.5 50.9 %copy-start.147 = (f32[1,256]{1,0:T(1,128)}, f32[1,256]{1,0:T(1,128)S(1)}, u32[]{:S(2)}) copy-start(f32[1,256]{1,0:T(1,128)S(1)} %get-tuple-element.1000) | copy-start | bytes 3076
  986.5 50.9 %copy-start.149 = (f32[1,256]{1,0:T(1,128)}, f32[1,256]{1,0:T(1,128)S(1)}, u32[]{:S(2)}) copy-start(f32[1,256]{1,0:T(1,128)S(1)} %get-tuple-element.1002) | copy-start | bytes 3076
  986.5 50.9 %copy-start.151 = (f32[1,256]{1,0:T(1,128)}, f32[1,256]{1,0:T(1,128)S(1)}, u32[]{:S(2)}) copy-start(f32[1,256]{1,0:T(1,128)S(1)} %get-tuple-element.1001) | copy-start | bytes 3076
  988.6 184.2 %copy-start.124 = (f32[1,512]{1,0:T(1,128)}, f32[1,512]{1,0:T(1,128)S(1)}, u32[]{:S(2)}) copy-start(f32[1,512]{1,0:T(1,128)S(1)} %get-tuple-element.995) | copy-start | bytes 6148
  988.6 37.9 %copy-start.106 = (f32[2048]{0:T(1024)S(1)}, f32[2048]{0:T(1024)}, u32[]{:S(2)}) copy-start(f32[2048]{0:T(1024)} %param.41) | copy-start | bytes 24580
  1026.7 215.6 %copy-start.15 = (bf16[192,2048]{1,0:T(8,128)(2,1)}, bf16[192,2048]{1,0:T(8,128)(2,1)S(1)}, u32[]{:S(2)}) copy-start(bf16[192,2048]{1,0:T(8,128)(2,1)S(1)} %multiply_convert_fusion.2) | copy-start | bytes 2359300
  1032.5 122.3 %copy-start.31 = (f32[381,256]{1,0:T(8,128)}, f32[381,256]{1,0:T(8,128)S(1)}, u32[]{:S(2)}) copy-start(f32[381,256]{1,0:T(8,128)S(1)} %slice.237) | copy-start | bytes 1170436
  1032.5 122.2 %copy-start.33 = (f32[382,256]{1,0:T(8,128)}, f32[382,256]{1,0:T(8,128)S(1)}, u32[]{:S(2)}) copy-start(f32[382,256]{1,0:T(8,128)S(1)} %slice.236) | copy-start | bytes 1173508
  1032.6 122.2 %copy-start.35 = (f32[383,256]{1,0:T(8,128)}, f32[383,256]{1,0:T(8,128)S(1)}, u32[]{:S(2)}) copy-start(f32[383,256]{1,0:T(8,128)S(1)} %slice.235) | copy-start | bytes 1176580
  1033.5 122.1 %all-to-all-start.3 = ((bf16[192,2,8]{0,2,1:T(8,128)(2,1)}), bf16[192,2,8]{0,2,1:T(8,128)(2,1)}, u32[]{:S(2)}, u32[]{:S(2)}) async-start(bf16[192,2,8]{0,2,1:T(8,128)(2,1)} %fusion.127), calls=%async_computation.3 | async-start | bytes 16384 | tf_op jit(solution)/shard_map/all_to_all | solution.py:217
  1155.7 16.0 all-to-all-start.4
  1231.0 10.1 all-to-all-start.5
  1268.8 9.5 all-to-all-start.6
  1272.2 153.8 %all-reduce.47.cloned.1.call-start = ((), (), s32[]{:S(2)}) async-start(), calls=%async_computation.26 | async-start | bytes 393216 | tf_op jit(solution)/shard_map/psum | solution.py:397
  1403.7 10.0 all-to-all-start.7
  1413.7 11.1 all-to-all-start.8
  1416.9 44.5 %all-reduce.55.cloned.1.call-start = ((), (), s32[]{:S(2)}) async-start(), calls=%async_computation.36 | async-start | bytes 1966080 | tf_op jit(solution)/shard_map/psum | solution.py:210
  1426.1 129.3 %all-reduce.49.cloned.1.call-start = ((), (), s32[]{:S(2)}) async-start(), calls=%async_computation.33 | async-start | bytes 6291456 | tf_op jit(solution)/shard_map/psum | solution.py:204
  1426.4 35.1 %copy-start.57 = (f32[384,256]{1,0:T(8,128)S(1)}, f32[384,256]{1,0:T(8,128)}, u32[]{:S(2)}) copy-start(f32[384,256]{1,0:T(8,128)} %get-tuple-element.946) | copy-start | bytes 1179652
  1426.4 37.1 %copy-start.152 = (f32[1,256]{1,0:T(1,128)S(1)}, f32[1,256]{1,0:T(1,128)}, u32[]{:S(2)}) copy-start(f32[1,256]{1,0:T(1,128)} %copy-done.151) | copy-start | bytes 3076
  1426.4 37.2 %copy-start.150 = (f32[1,256]{1,0:T(1,128)S(1)}, f32[1,256]{1,0:T(1,128)}, u32[]{:S(2)}) copy-start(f32[1,256]{1,0:T(1,128)} %copy-done.149) | copy-start | bytes 3076
  1430.8 32.9 %copy-start.148 = (f32[1,256]{1,0:T(1,128)S(1)}, f32[1,256]{1,0:T(1,128)}, u32[]{:S(2)}) copy-start(f32[1,256]{1,0:T(1,128)} %copy-done.147) | copy-start | bytes 3076
  1430.8 33.1 %copy-start.146 = (f32[1,256]{1,0:T(1,128)S(1)}, f32[1,256]{1,0:T(1,128)}, u32[]{:S(2)}) copy-start(f32[1,256]{1,0:T(1,128)} %copy-done.145) | copy-start | bytes 3076
  1486.4 69.0 %copy-start.5 = (f32[192,2048]{1,0:T(8,128)S(1)}, f32[192,2048]{1,0:T(8,128)}, u32[]{:S(2)}) copy-start(f32[192,2048]{1,0:T(8,128)} %copy-done.4) | copy-start | bytes 4718596
  1486.4 69.0 %copy-start.109 = (f32[2048]{0:T(1024)S(1)}, f32[2048]{0:T(1024)}, u32[]{:S(2)}) copy-start(f32[2048]{0:T(1024)} %param.38) | copy-start | bytes 24580
  1486.4 69.0 %copy-start.138 = (f32[192]{0:T(256)S(1)}, f32[192]{0:T(256)}, u32[]{:S(2)}) copy-start(f32[192]{0:T(256)} %copy-done.137) | copy-start | bytes 2308
  1486.4 71.5 %copy-start.156 = (f32[192]{0:T(256)S(1)}, f32[192]{0:T(256)}, u32[]{:S(2)}) copy-start(f32[192]{0:T(256)} %copy-done.155) | copy-start | bytes 2308
  1583.1 10.2 all-to-all-start.11
  1593.2 12.2 all-to-all-start.10
  1596.8 81.3 %all-reduce.53.cloned.1.call-start = ((), (), s32[]{:S(2)}) async-start(), calls=%async_computation.35 | async-start | bytes 3440640 | tf_op jit(solution)/shard_map/psum | solution.py:209
  1598.1 26.8 copy-start.27
  1632.8 175.9 %reduce-scatter.17.cloned.1.call-start = ((), (), s32[]{:S(2)}) async-start(), calls=%async_computation.32 | async-start | bytes 4718592 | tf_op jit(solution)/shard_map/reduce_scatter | solution.py:526
  1636.4 317.9 %all-reduce.51.cloned.1.call-start = ((), (), s32[]{:S(2)}) async-start(), calls=%async_computation.34 | async-start | bytes 10092544 | tf_op jit(solution)/shard_map/psum | solution.py:548
  1638.4 39.7 %copy-start.3 = (bf16[192,4096]{1,0:T(8,128)(2,1)S(1)}, bf16[192,4096]{1,0:T(8,128)(2,1)}, u32[]{:S(2)}) copy-start(bf16[192,4096]{1,0:T(8,128)(2,1)} %copy-done.2) | copy-start | bytes 4718596
  1683.3 362.7 %reduce-scatter.9.cloned.1.call-start = ((), (), s32[]{:S(2)}) async-start(), calls=%async_computation.28 | async-start | bytes 4718592 | tf_op jit(solution)/shard_map/reduce_scatter | solution.py:514
  1689.0 507.7 %reduce-scatter.15.cloned.1.call-start = ((), (), s32[]{:S(2)}) async-start(), calls=%async_computation.31 | async-start | bytes 9437184 | tf_op jit(solution)/shard_map/reduce_scatter | solution.py:523
  1704.3 642.9 %reduce-scatter.13.cloned.1.call-start = ((), (), s32[]{:S(2)}) async-start(), calls=%async_computation.30 | async-start | bytes 9437184 | tf_op jit(solution)/shard_map/reduce_scatter | solution.py:520
  1712.6 916.6 %reduce-scatter.11.cloned.1.call-start = ((), (), s32[]{:S(2)}) async-start(), calls=%async_computation.29 | async-start | bytes 18874368 | tf_op jit(solution)/shard_map/reduce_scatter | solution.py:517
  1726.6 1309.6 %reduce-scatter.7.cloned.1.call-start = ((), (), s32[]{:S(2)}) async-start(), calls=%async_computation.27 | async-start | bytes 28311552 | tf_op jit(solution)/shard_map/reduce_scatter | solution.py:511
  1755.6 47.8 %copy-start.154 = (f32[192]{0:T(256)S(1)}, f32[192]{0:T(256)}, u32[]{:S(2)}) copy-start(f32[192]{0:T(256)} %copy-done.153) | copy-start | bytes 2308
  (170 other events, 811.3 us)
Sparse Core Ops, SparseCore 0:
  9.6 483.0 all-gather.6
  494.7 82.2 all-gather.8
  581.5 41.0 all-reduce.42
  624.6 227.2 all-gather.10
  853.8 123.1 all-gather.12
  983.7 41.0 all-reduce.44
  1027.0 124.5 all-gather.14
  1153.6 76.2 all-gather.16
  1395.8 19.9 all-reduce.46
  1426.2 35.1 all-reduce.54
  1486.5 68.8 all-reduce.48
  1633.0 45.0 all-reduce.52
  1681.7 88.9 reduce-scatter.16
  1775.7 178.5 all-reduce.50
  1958.4 87.6 reduce-scatter.8
  2049.5 147.1 reduce-scatter.14
  2200.2 146.9 reduce-scatter.12
  2350.8 278.4 reduce-scatter.10
  2633.2 402.9 reduce-scatter.6
where the time goes:
time: 3060 us; the launch traced here: 3050 us
  waiting for transfers between devices  2400 us (78%)
  matrix products  224 us (7%)
  other arithmetic  155 us (5%)
  local copies, waits for them, and re-layouts  121 us (4%)
  blocking collectives  79.6 us (3%)
  starting transfers between devices  40.2 us (1%)
    all_gather x3, waiting for transfers between devices, collect(): lax.all_gather(first_part, ('fsdp', 'ctx'), axis=1, tiled=True)  815 us
    reduce_scatter x1, waiting for transfers between devices, per_device(): lax.psum_scatter(grad_w_qkv.astype(jnp.bfloat16), ('fsdp', 'ctx'), scatte...  403 us
    reduce_scatter x1, waiting for transfers between devices, per_device(): lax.psum_scatter(grad_w_gu.astype(jnp.bfloat16), ('fsdp', 'ctx'), scatter...  279 us
    reduce_scatter x1, waiting for transfers between devices, per_device(): lax.psum_scatter(grad_w_zx.astype(jnp.bfloat16), ('fsdp', 'ctx'), scatter...  149 us
    reduce_scatter x1, waiting for transfers between devices, per_device(): lax.psum_scatter(grad_w_down.astype(jnp.bfloat16), ('fsdp', 'ctx'), scatt...  148 us
    psum x3, waiting for transfers between devices, tensor_sum(): return lax.psum(partial_sum, 'tp')  145 us
    psum x1, waiting for transfers between devices, per_device(): lax.psum(adapter_down_gradient.astype(jnp.bfloat16), ('fsdp', 'ctx'))  144 us
    all_gather x3, waiting for transfers between devices, collect(): lax.all_gather(second_part, ('fsdp', 'ctx'), axis=1, tiled=True)  131 us
  transfers between devices with their start and end apart: 29, of which 23 were waited for; matrix products, arithmetic and copies ran while one was open for 9% of the time, Pallas kernels for 0%

commit v1 on v0

--- a/solution.py
+++ b/solution.py
@@ -4,7 +4,9 @@
 from jax.sharding import PartitionSpec as P
 
 MODEL_WIDTH = 2048
+AHEADS = 32
 AHD = 128
+MHEADS = 64
 INNER = 4096
 MIXER_HEAD_SIZE = 64
 STATE = 128
@@ -588,6 +590,345 @@
     )
 
 
+PLANE = ("fsdp", "ctx")
+EVERY = ("fsdp", "ctx", "tp")
+
+
+def gather_rows(values):
+    return lax.all_gather(values, EVERY, axis=0, tiled=True)
+
+
+def scatter_rows(partial_sum):
+    return lax.psum_scatter(partial_sum, EVERY, scatter_dimension=0, tiled=True).astype(jnp.float32)
+
+
+def spread(weight, split, join):
+    return lax.all_to_all(weight, PLANE, split_axis=split, concat_axis=join, tiled=True)
+
+
+def shift_conv(values, kernel, bias, position):
+    total = values * kernel[0][None, :] + bias[None, :]
+    for lag in range(1, kernel.shape[0]):
+        shifted = jnp.pad(values, ((lag, 0), (0, 0)))[: values.shape[0]]
+        keep = (position >= lag).astype(values.dtype)[:, None]
+        total = total + shifted * keep * kernel[lag][None, :]
+    return jax.nn.silu(total)
+
+
+def attend_groups(queries, keys_all, vals_all, segment, position):
+    def rot(values):
+        half_dim = values.shape[-1] // 2
+        inverse = 10000.0 ** (-jnp.arange(half_dim, dtype=jnp.float32) / half_dim)
+        angle = position.astype(jnp.float32)[..., None] * inverse
+        cosine, sine = jnp.cos(angle), jnp.sin(angle)
+        a, b = values[..., :half_dim], values[..., half_dim:]
+        return jnp.concatenate([a * cosine - b * sine, b * cosine + a * sine], axis=-1).astype(
+            jnp.bfloat16
+        )
+
+    rows = queries.shape[1]
+    order = jnp.arange(rows)
+    scores = jnp.einsum(
+        "gqd,gkd->gqk", rot(queries), rot(keys_all), preferred_element_type=jnp.float32
+    ) * AHD ** (-0.5)
+    allowed = (segment[:, :, None] == segment[:, None, :]) & (order[:, None] >= order[None, :])
+    weights = jnp.exp(jnp.where(allowed, scores, -1e30))
+    low = (weights / jnp.sum(weights, axis=-1, keepdims=True)).astype(jnp.bfloat16)
+    return jnp.einsum(
+        "gqk,gkd->gqd", low, vals_all.astype(jnp.bfloat16), preferred_element_type=jnp.float32
+    )
+
+
+def mixer_groups(
+    inner_in, step_in, bc_post, bias_in, decay_in, skip_in, kernel_in, conv_bias_in, position, segment
+):
+    groups, rows = segment.shape
+    heads = step_in.shape[1]
+    xc = shift_conv(inner_in, kernel_in, conv_bias_in, position.reshape(-1))
+    xc = xc.reshape(groups, rows, heads, MIXER_HEAD_SIZE)
+    step = jax.nn.softplus(step_in + bias_in[None, :]).reshape(groups, rows, heads)
+    log_decay = step * -jnp.exp(decay_in)
+    order = jnp.arange(rows)
+    same = (segment[:, :, None] == segment[:, None, :]) & (order[:, None] >= order[None, :])
+    running = jnp.einsum("gts,gsh->gth", same.astype(jnp.float32), log_decay, precision=highest)
+    gap = running.transpose(0, 2, 1)
+    gap = gap[:, :, :, None] - gap[:, :, None, :]
+    decay = jnp.where(same[:, None], jnp.exp(jnp.where(same[:, None], gap, 0.0)), 0.0)
+    b_mat = bc_post[:, :STATE].reshape(groups, rows, STATE)
+    c_mat = bc_post[:, STATE:].reshape(groups, rows, STATE)
+    meet = jnp.einsum("gtn,gsn->gts", c_mat, b_mat, precision=lax.Precision.HIGH)
+    out = jnp.einsum(
+        "ghts,gshp->gthp",
+        decay * meet[:, None],
+        xc * step[..., None],
+        precision=lax.Precision.HIGH,
+    )
+    out = out + skip_in[:, None] * xc
+    return out.reshape(groups * rows, heads * MIXER_HEAD_SIZE)
+
+
+def per_device_split(
+    hidden,
+    embeds,
+    cotangent,
+    lengths,
+    attention_norm_gain,
+    adapter_down_maps,
+    query_key_value_weight,
+    adapter_up_maps,
+    attention_output_weight,
+    feedforward_norm_gain,
+    gate_up_weight,
+    down_weight,
+    mixer_norm_gain,
+    mixer_gate_input_weight,
+    state_map_weight,
+    step_size_weight,
+    mixer_input_taps,
+    mixer_input_tap_bias,
+    state_map_taps,
+    state_map_tap_bias,
+    step_size_bias,
+    log_decay_rate,
+    head_skip_weight,
+    gated_norm_gain,
+    mixer_output_weight,
+):
+    bf16, f32 = jnp.bfloat16, jnp.float32
+    tp_size, ctx_size, groups = (lax.axis_size(name) for name in ("tp", "ctx", "fsdp"))
+    tp_index, ctx_index = lax.axis_index("tp"), lax.axis_index("ctx")
+    plane_index = lax.axis_index("fsdp") * ctx_size + ctx_index
+    plane_size = groups * ctx_size
+    tok_rows = hidden.shape[0]
+    mine = tok_rows // tp_size
+    group_rows = tok_rows * ctx_size
+    start = tp_index * mine
+
+    def own_rows(values):
+        return lax.dynamic_slice_in_dim(values, start, mine, 0)
+
+    def own_part(values, axis=0):
+        width = values.shape[axis] // plane_size
+        return lax.dynamic_slice_in_dim(values, plane_index * width, width, axis)
+
+    hidden_f = own_rows(hidden).astype(f32)
+    embeds_f = own_rows(embeds).astype(f32)
+    cot_low = own_rows(cotangent)
+
+    w_qkv = spread(query_key_value_weight, 2, 1)
+    w_o = spread(attention_output_weight, 0, 1)
+    w_gu = spread(gate_up_weight, 2, 1)
+    w_down = spread(down_weight, 0, 1)
+    w_zx = spread(mixer_gate_input_weight, 2, 1)
+    w_out = spread(mixer_output_weight, 0, 1)
+    up_maps = own_part(adapter_up_maps, 2)
+    w_step = own_part(step_size_weight, 1)
+    taps, tap_bias = own_part(mixer_input_taps, 1), own_part(mixer_input_tap_bias)
+    step_bias, decay_rate = own_part(step_size_bias), own_part(log_decay_rate)
+    skip, gate_gain = own_part(head_skip_weight), own_part(gated_norm_gain)
+
+    rank = adapter_down_maps.shape[2]
+    width_a = adapter_down_maps.shape[1]
+    down_all = jnp.concatenate([adapter_down_maps[j] for j in range(3)], axis=1)
+    joined = jnp.concatenate([hidden_f, embeds_f], axis=1)
+    normed_a, norm_a_back = jax.vjp(rms_scale, joined, attention_norm_gain)
+    xa_mine = normed_a.astype(bf16)
+    mid_mine = matrix_product(xa_mine, down_all).astype(bf16)
+    segment_g, position_g, slot_g = layout(lengths[0], group_rows)
+    first = ctx_index * tok_rows + start
+    marks = jnp.stack(
+        [
+            lax.dynamic_slice_in_dim(segment_g, first, mine),
+            lax.dynamic_slice_in_dim(position_g, first, mine),
+        ],
+        axis=1,
+    ).astype(bf16)
+    marks = jnp.pad(marks, ((0, 0), (0, 126)))
+    gathered = gather_rows(jnp.concatenate([xa_mine, mid_mine, marks], axis=1))
+    xa = gathered[:, :width_a]
+    mid = gathered[:, width_a : width_a + 3 * rank]
+    segment = gathered[:, width_a + 3 * rank].astype(jnp.int32).reshape(groups, group_rows)
+    position = gathered[:, width_a + 3 * rank + 1].astype(jnp.int32).reshape(groups, group_rows)
+    position_flat = position.reshape(-1)
+    cot = gather_rows(cot_low)
+    proj = [
+        (
+            matrix_product(xa, w_qkv[j])
+            + matrix_product(mid[:, j * rank : (j + 1) * rank], up_maps[j])
+        ).astype(bf16)
+        for j in range(3)
+    ]
+    ao, attend_back = jax.vjp(
+        lambda q, k, v: attend_groups(q, k, v, segment, position),
+        *[piece.astype(f32).reshape(groups, group_rows, AHD) for piece in proj],
+    )
+    ao_low = ao.astype(bf16).reshape(groups * group_rows, AHD)
+    after_attn = hidden_f + scatter_rows(matrix_product(ao_low, w_o).astype(bf16))
+
+    normed_m, norm_m_back = jax.vjp(rms_scale, after_attn, feedforward_norm_gain)
+    xm = gather_rows(normed_m.astype(bf16))
+    gate_pre, up_pre = matrix_product(xm, w_gu[0]), matrix_product(xm, w_gu[1])
+    activated, act_back = jax.vjp(gated_gelu, gate_pre, up_pre)
+    hid_low = activated.astype(bf16)
+    after_mlp = after_attn + scatter_rows(matrix_product(hid_low, w_down).astype(bf16))
+
+    normed_n, norm_n_back = jax.vjp(rms_scale, after_mlp, mixer_norm_gain)
+    xn = gather_rows(normed_n.astype(bf16))
+    gate_z = matrix_product(xn, w_zx[0])
+    inner_x = matrix_product(xn, w_zx[1]).astype(bf16)
+    step_raw = matrix_product(xn, w_step).astype(bf16)
+    bc_low = matrix_product(xn, state_map_weight).astype(bf16)
+    bc_post, bc_conv_back = jax.vjp(
+        lambda v, k, b: shift_conv(v, k, b, position_flat),
+        bc_low.astype(f32),
+        state_map_taps,
+        state_map_tap_bias,
+    )
+    scan_out, scan_back = jax.vjp(
+        lambda *parts: mixer_groups(*parts, position, segment),
+        inner_x.astype(f32),
+        step_raw.astype(f32),
+        bc_post,
+        step_bias,
+        decay_rate,
+        skip,
+        taps,
+        tap_bias,
+    )
+    y = scan_out.astype(bf16).astype(f32)
+    silu_z = jax.nn.silu(gate_z)
+    gated = y * silu_z
+    d_yn = matrix_product_transposed(cot, w_out)
+    gain_part = d_yn * gate_gain
+    sums = lax.psum(
+        jnp.stack([jnp.sum(gated * gated, axis=1), jnp.sum(gain_part * gated, axis=1)]), EVERY
+    )
+    inverse = lax.rsqrt(sums[0] / INNER + epsilon)[:, None]
+    cross = (sums[1] / INNER)[:, None]
+    yn_low = (gated * inverse * gate_gain).astype(bf16)
+    out_mine = after_mlp + scatter_rows(matrix_product(yn_low, w_out).astype(bf16))
+    result = lax.all_gather(out_mine.astype(bf16), "tp", axis=0, tiled=True)
+
+    grad_w_out = outer_product_sum(yn_low, cot)
+    grad_g_gate = jnp.sum(d_yn * gated * inverse, axis=0)
+    d_gated = gain_part * inverse - gated * inverse**3 * cross
+    d_y = (d_gated * silu_z).astype(bf16)
+    sigmoid_z = jax.nn.sigmoid(gate_z)
+    d_z = (d_gated * y * sigmoid_z * (1.0 + gate_z * (1.0 - sigmoid_z))).astype(bf16)
+    (
+        d_xs,
+        d_step,
+        d_bc_post,
+        grad_dt_bias,
+        grad_a_log,
+        grad_d_skip,
+        grad_conv_x,
+        grad_conv_x_bias,
+    ) = scan_back(d_y.astype(f32))
+    d_xs, d_step = d_xs.astype(bf16), d_step.astype(bf16)
+    d_bc_part, grad_conv_bc, grad_conv_bc_bias = bc_conv_back(d_bc_post)
+    dxn_part = (
+        matrix_product_transposed(d_z, w_zx[0])
+        + matrix_product_transposed(d_xs, w_zx[1])
+        + matrix_product_transposed(d_step, w_step)
+    )
+    sent = scatter_rows(jnp.concatenate([dxn_part, d_bc_part], axis=1).astype(bf16))
+    width = hidden.shape[1]
+    d_bc_mine = sent[:, width:].astype(bf16)
+    dxn_mine = sent[:, :width] + matrix_product_transposed(d_bc_mine, state_map_weight)
+    grad_w_zx = jnp.stack([outer_product_sum(xn, d_z), outer_product_sum(xn, d_xs)])
+    grad_w_dt = outer_product_sum(xn, d_step)
+    d_norm_n, grad_g_mamba = norm_n_back(dxn_mine)
+    d_after_mlp = cot_low.astype(f32) + d_norm_n
+
+    gathered = gather_rows(jnp.concatenate([d_after_mlp.astype(bf16), d_bc_mine], axis=1))
+    d_mlp, d_bc = gathered[:, :width], gathered[:, width:]
+    grad_w_bc = outer_product_sum(xn, d_bc)
+    grad_w_down = outer_product_sum(hid_low, d_mlp)
+    d_gate, d_up = act_back(matrix_product_transposed(d_mlp, w_down))
+    d_gate, d_up = d_gate.astype(bf16), d_up.astype(bf16)
+    d_xm = scatter_rows(
+        (
+            matrix_product_transposed(d_gate, w_gu[0]) + matrix_product_transposed(d_up, w_gu[1])
+        ).astype(bf16)
+    )
+    grad_w_gu = jnp.stack([outer_product_sum(xm, d_gate), outer_product_sum(xm, d_up)])
+    d_norm_m, grad_g_mlp = norm_m_back(d_xm)
+    d_after_attn = d_after_mlp + d_norm_m
+
+    d_attn = gather_rows(d_after_attn.astype(bf16))
+    grad_w_o = outer_product_sum(ao_low, d_attn)
+    d_ao = matrix_product_transposed(d_attn, w_o).astype(bf16)
+    d_proj = [
+        piece.reshape(groups * group_rows, AHD).astype(bf16)
+        for piece in attend_back(d_ao.astype(f32).reshape(groups, group_rows, AHD))
+    ]
+    dxa_part = sum(matrix_product_transposed(d_proj[j], w_qkv[j]) for j in range(3))
+    dmid_part = jnp.concatenate(
+        [matrix_product_transposed(d_proj[j], up_maps[j]) for j in range(3)], axis=1
+    )
+    sent = scatter_rows(jnp.concatenate([dxa_part, dmid_part], axis=1).astype(bf16))
+    dmid_mine = sent[:, width_a:].astype(bf16)
+    dxa_mine = sent[:, :width_a] + matrix_product_transposed(dmid_mine, down_all)
+    dmid = gather_rows(dmid_mine)
+    adapter_down_gradient = jnp.stack(
+        [outer_product_sum(xa, dmid[:, j * rank : (j + 1) * rank]) for j in range(3)]
+    )
+    grad_w_qkv = jnp.stack([outer_product_sum(xa, d_proj[j]) for j in range(3)])
+    adapter_up_gradient = jnp.stack(
+        [outer_product_sum(mid[:, j * rank : (j + 1) * rank], d_proj[j]) for j in range(3)]
+    )
+    d_joined, grad_g_attn = norm_a_back(dxa_mine)
+    back = jnp.concatenate(
+        [d_after_attn + d_joined[:, :width], d_joined[:, width:]], axis=1
+    ).astype(bf16)
+    back = lax.all_gather(back, "tp", axis=0, tiled=True).astype(f32)
+    d_hidden, d_embeds = back[:, :width], back[:, width:]
+
+    def home(grad, split, join):
+        return spread(grad.astype(bf16), split, join).astype(f32)
+
+    grad_w_qkv = home(grad_w_qkv, 1, 2)
+    grad_w_o = home(grad_w_o, 1, 0)
+    grad_w_gu = home(grad_w_gu, 1, 2)
+    grad_w_down = home(grad_w_down, 1, 0)
+    grad_w_zx = home(grad_w_zx, 1, 2)
+    grad_w_out = home(grad_w_out, 1, 0)
+
+    def whole(part, axis):
+        return lax.all_gather(part.astype(bf16), PLANE, axis=axis, tiled=True).astype(f32)
+
+    def total(part):
+        return lax.psum(part, EVERY)
+
+    return (
+        result,
+        d_hidden,
+        d_embeds,
+        total(grad_g_attn),
+        adapter_down_gradient,
+        grad_w_qkv,
+        whole(adapter_up_gradient, 2),
+        grad_w_o,
+        total(grad_g_mlp),
+        grad_w_gu,
+        grad_w_down,
+        total(grad_g_mamba),
+        grad_w_zx,
+        grad_w_bc,
+        whole(grad_w_dt, 1),
+        whole(grad_conv_x, 1),
+        whole(grad_conv_x_bias, 0),
+        total(grad_conv_bc),
+        total(grad_conv_bc_bias),
+        whole(grad_dt_bias, 0),
+        whole(grad_a_log, 0),
+        whole(grad_d_skip, 0),
+        whole(grad_g_gate, 0),
+        grad_w_out,
+    )
+
+
 def solution(mesh):
     placed = (
         P(("fsdp", "ctx"), None),
@@ -616,8 +957,10 @@
         P("tp"),
         P("tp", ("fsdp", "ctx")),
     )
+    devices = mesh.shape["fsdp"] * mesh.shape["ctx"] * mesh.shape["tp"]
+    one_head_each = devices == AHEADS and MHEADS % devices == 0
     return jax.shard_map(
-        per_device,
+        per_device_split if one_head_each else per_device,
         mesh=mesh,
         in_specs=placed,
         out_specs=(

time: 3060 us -> 2080 us (0.68)
  waiting for transfers between devices: 2400 us -> 1160 us
  blocking collectives: 79.6 us -> 299 us
  other arithmetic: 155 us -> 87.4 us
  matrix products: 224 us -> 277 us
  local copies, waits for them, and re-layouts: 121 us -> 172 us
    all_gather x6 -> x8, waiting for transfers between devices: 946 us -> 193 us  [the longest x7 193 us: gather_rows(): return lax.all_gather(values, EVERY, axis=0, tiled=True)]
    reduce_scatter x6, waiting for transfers between devices: 1060 us -> 574 us  [scatter_rows(): lax.psum_scatter(partial_sum, EVERY, scatter_dimension=0, tiled=True)]
    psum x7 -> x0, waiting for transfers between devices: 355 us -> none  [the longest x3 145 us: tensor_sum(): return lax.psum(partial_sum, 'tp')]
    all_to_all x10 -> x12, waiting for transfers between devices: 37.2 us -> 391 us  [spread(): lax.all_to_all(weight, PLANE, split_axis=split, concat_axis=join, tiled=T...]
    all_gather x1 -> x6, blocking collectives: 5.29 us -> 139 us  [the longest x5 131 us: whole(): lax.all_gather(part.astype(bf16), PLANE, axis=axis, tiled=True).astype(f32)]
    unnamed x0 -> x1, blocking collectives: none -> 80.7 us
    dot_general x18, matrix products: 41.4 us -> 85.9 us  [outer_product_sum(): lax.dot_general(left, right, (((0,), (0,)), ((), ())), preferred_element_...]
    convert_element_type x54 -> x26, other arithmetic: 65.7 us -> 26.1 us  [the longest x6 11.8 us: home(): return spread(grad.astype(bf16), split, join).astype(f32)]
  transfers between devices with their start and end apart: 29 -> 26, of which waited for: 23 -> 20; matrix products, arithmetic and copies ran while one was open for 9% -> 14% of each run, Pallas kernels for 0% -> 0%
where the time goes in v1:
time: 2080 us; the launch traced here: 2070 us
  waiting for transfers between devices  1160 us (56%)
  blocking collectives  299 us (14%)
  matrix products  277 us (13%)
  local copies, waits for them, and re-layouts  172 us (8%)
  other arithmetic  87.4 us (4%)
  starting transfers between devices  57.9 us (3%)
    reduce_scatter x6, waiting for transfers between devices, scatter_rows(): lax.psum_scatter(partial_sum, EVERY, scatter_dimension=0, tiled=True)  574 us
    all_to_all x12, waiting for transfers between devices, spread(): lax.all_to_all(weight, PLANE, split_axis=split, concat_axis=join, tiled=T...  391 us
    all_gather x7, waiting for transfers between devices, gather_rows(): return lax.all_gather(values, EVERY, axis=0, tiled=True)  193 us
    all_gather x5, blocking collectives, whole(): lax.all_gather(part.astype(bf16), PLANE, axis=axis, tiled=True).astype(f32)  131 us
    dot_general x16, matrix products, matrix_product_transposed(): lax.dot_general(left, right, (((1,), (1,)), ((), ())), preferred_element_...  102 us
    dot_general x18, matrix products, outer_product_sum(): lax.dot_general(left, right, (((0,), (0,)), ((), ())), preferred_element_...  85.9 us
    unnamed x1, blocking collectives  80.7 us
    dot_general x16, matrix products, matrix_product(): return jnp.dot(left, right, preferred_element_type=jnp.float32)  59.8 us
  transfers between devices with their start and end apart: 26, of which 20 were waited for; matrix products, arithmetic and copies ran while one was open for 14% of the time, Pallas kernels for 0%

profile of v1, /device:TPU:0, one launch (start us, length us, event | category | flops | bytes accessed | tf_op | source)
XLA Modules:
  0.0 2068.2 jit_solution(12604824943490700468)
XLA Ops:
  15.7 7.3 all-to-all-start.1
  23.0 7.7 copy.233
  30.6 15.5 all-to-all-done.1
  51.8 147.6 %all-to-all-done = bf16[3,512,1024]{1,0,2:T(4,128)(2,1)} async-done(((bf16[3,512,1024]{1,0,2:T(4,128)(2,1)}), bf16[3,512,1024]{1,0,2:T(4,128)(2,1)}, u32[]{:S(2)}, u32[]{:S(2)}) %all-to-all-start) | async-done | bytes 3145760 | tf_op jit(solution)/shard_map/all_to_all | solution.py:606
  213.1 6.4 fusion.139
  221.1 6.6 fusion.141
  248.6 114.0 %reduce-scatter.7.cloned.1.call-done = bf16[48,2048]{1,0:T(8,128)(2,1)} async-done(((bf16[1536,2048]{1,0:T(8,128)(2,1)}), bf16[48,2048]{1,0:T(8,128)(2,1)}) %reduce-scatter.7.cloned.1.call-update) | async-done | bytes 196624 | tf_op jit(solution)/shard_map/reduce_scatter | solution.py:602
  369.8 6.2 copy.240
  376.0 22.4 %all-to-all-done.3 = bf16[8,256,256]{2,1,0:T(8,128)(2,1)S(1)} async-done(((bf16[8,256,256]{2,1,0:T(8,128)(2,1)}), bf16[8,256,256]{2,1,0:T(8,128)(2,1)S(1)}, u32[]{:S(2)}, u32[]{:S(2)}) %all-to-all-start.3) | async-done | bytes 1048608 | tf_op jit(solution)/shard_map/all_to_all | solution.py:606
  405.8 66.3 %all-to-all-done.2 = bf16[2,256,2048]{1,0,2:T(2,128)(2,1)S(1)} async-done(((bf16[2,256,2048]{1,0,2:T(2,128)(2,1)}), bf16[2,256,2048]{1,0,2:T(2,128)(2,1)S(1)}, u32[]{:S(2)}, u32[]{:S(2)}) %all-to-all-start.2) | async-done | bytes 2097184 | tf_op jit(solution)/shard_map/all_to_all | solution.py:606
  476.0 5.0 fusion.220
  489.9 113.6 %reduce-scatter.9.cloned.1.call-done = bf16[48,2048]{1,0:T(8,128)(2,1)} async-done(((bf16[1536,2048]{1,0:T(8,128)(2,1)}), bf16[48,2048]{1,0:T(8,128)(2,1)}) %reduce-scatter.9.cloned.1.call-update) | async-done | bytes 196624 | tf_op jit(solution)/shard_map/reduce_scatter | solution.py:602
  615.4 13.3 all-to-all-done.5
  639.6 26.0 %all-to-all-done.4 = bf16[2,256,1024]{1,0,2:T(2,128)(2,1)S(1)} async-done(((bf16[2,256,1024]{1,0,2:T(2,128)(2,1)}), bf16[2,256,1024]{1,0,2:T(2,128)(2,1)S(1)}, u32[]{:S(2)}, u32[]{:S(2)}) %all-to-all-start.4) | async-done | bytes 1048608 | tf_op jit(solution)/shard_map/all_to_all | solution.py:606
  670.6 18.0 all-gather.16.cloned.1.call-done
  702.0 5.3 compare_select_fusion.2
  725.6 5.5 fusion.222
  731.1 28.1 %all-gather.18.cloned.1.call-done = bf16[1536,2048]{1,0:T(8,128)(2,1)} async-done(((bf16[48,2048]{1,0:T(8,128)(2,1)}), bf16[1536,2048]{1,0:T(8,128)(2,1)}) %all-gather.18.cloned.1.call-update) | async-done | bytes 6291472 | tf_op jit(solution)/shard_map/all_gather | solution.py:598
  759.2 6.1 multiply_reduce_fusion.15
  765.3 39.8 %psum.42 = f32[2,1536]{1,0:T(2,128)S(1)} all-reduce(f32[2,1536]{1,0:T(2,128)S(1)} %pad_maximum_fusion.21), channel_id=1, replica_groups=mesh['fsdp'=4,'ctx'=2,'tp'=4] {'fsdp','ctx','tp'}, use_global_device_ids=true, to_apply=%region_11.12 | all-reduce | flops 3072 | bytes 24576 | tf_op jit(solution)/shard_map/psum | solution.py:803
  811.0 6.1 fusion.14
  846.3 6.4 fusion.224
  852.7 6.4 fusion.223
  862.4 12.7 add_convert_fusion.2
  875.1 6.4 pad_maximum_fusion.1
  881.6 119.9 %reduce-scatter.13.cloned.1.call-done = bf16[48,2304]{1,0:T(8,128)(2,1)} async-done(((bf16[1536,2304]{1,0:T(8,128)(2,1)}), bf16[48,2304]{1,0:T(8,128)(2,1)}) %reduce-scatter.13.cloned.1.call-update) | async-done | bytes 221200 | tf_op jit(solution)/shard_map/reduce_scatter | solution.py:602
  1006.3 70.8 %all-gather.20.cloned.1.call-done = bf16[1536,2304]{1,0:T(8,128)(2,1)} async-done(((bf16[48,2304]{1,0:T(8,128)(2,1)}), bf16[1536,2304]{1,0:T(8,128)(2,1)}) %all-gather.20.cloned.1.call-update) | async-done | bytes 7077904 | tf_op jit(solution)/shard_map/all_gather | solution.py:598
  1077.1 6.6 multiply_convert_fusion
  1095.8 108.0 %reduce-scatter.15.cloned.1.call-done = bf16[48,2048]{1,0:T(8,128)(2,1)} async-done(((bf16[1536,2048]{1,0:T(8,128)(2,1)}), bf16[48,2048]{1,0:T(8,128)(2,1)}) %reduce-scatter.15.cloned.1.call-update) | async-done | bytes 196624 | tf_op jit(solution)/shard_map/reduce_scatter | solution.py:602
  1205.5 118.3 %reduce-scatter.11.cloned.1.call-done = bf16[48,2048]{1,0:T(8,128)(2,1)} async-done(((bf16[1536,2048]{1,0:T(8,128)(2,1)}), bf16[48,2048]{1,0:T(8,128)(2,1)}) %reduce-scatter.11.cloned.1.call-update) | async-done | bytes 196624 | tf_op jit(solution)/shard_map/reduce_scatter | solution.py:602
  1326.5 69.1 %all-gather.22.cloned.1.call-done = bf16[1536,2048]{1,0:T(8,128)(2,1)} async-done(((bf16[48,2048]{1,0:T(8,128)(2,1)}), bf16[1536,2048]{1,0:T(8,128)(2,1)}) %all-gather.22.cloned.1.call-update) | async-done | bytes 6291472 | tf_op jit(solution)/shard_map/all_gather | solution.py:598
  1410.9 10.1 fusion.228
  1423.2 10.1 fusion.229
  1435.1 21.9 %add_convert_fusion = bf16[1536,4096]{1,0:T(8,128)(2,1)} fusion(f32[1536,4096]{1,0:T(8,128)} %fusion.228, f32[1536,4096]{1,0:T(8,128)} %fusion.229, bf16[1536,128]{1,0:T(8,128)(2,1)S(1)} %bitcast.267, bf16[4096,128]{1,0:T(8,128)(2,1)S(1)} %bitcast.277), kind=kOutput, calls=%fused_computation | convolution fusion | flops 1629487104 | bytes 64356352 | tf_op jit(solution)/shard_map/dot_general | solution.py:25
  1456.9 12.7 pad_maximum_fusion
  1478.6 5.1 fusion.41
  1483.7 5.0 fusion.42
  1488.8 9.5 copy.286
  1499.1 6.0 all-to-all-start.10
  1505.1 5.0 fusion.15
  1511.1 32.3 %all-to-all-done.10 = bf16[2,2048,128]{2,0,1:T(2,128)(2,1)S(1)} async-done(((bf16[2,2048,128]{2,0,1:T(2,128)(2,1)}), bf16[2,2048,128]{2,0,1:T(2,128)(2,1)S(1)}, u32[]{:S(2)}, u32[]{:S(2)}) %all-to-all-start.10) | async-done | bytes 1048608 | tf_op jit(solution)/shard_map/all_to_all | solution.py:606
  1547.1 5.0 fusion.20
  1557.1 14.0 copy.283
  1571.1 19.1 all-to-all-done.9
  1600.0 9.2 fusion.12
  1613.6 48.1 %all-to-all-done.8 = bf16[2,2048,256]{2,0,1:T(2,128)(2,1)S(1)} async-done(((bf16[2,2048,256]{2,0,1:T(2,128)(2,1)}), bf16[2,2048,256]{2,0,1:T(2,128)(2,1)S(1)}, u32[]{:S(2)}, u32[]{:S(2)}) %all-to-all-start.8) | async-done | bytes 2097184 | tf_op jit(solution)/shard_map/all_to_all | solution.py:606
  1661.7 5.0 all-to-all-start.7
  1666.7 8.3 fusion.10
  1675.5 20.4 copy.280
  1696.0 6.1 all-to-all-start.6
  1704.4 80.7 %all-reduce.31 = (bf16[16]{0:T(256)(128)(2,1)S(1)}, bf16[16]{0:T(256)(128)(2,1)S(1)}, bf16[16]{0:T(256)(128)(2,1)S(1)}) all-reduce(bf16[16]{0:T(256)(128)(2,1)S(1)} %dynamic-update-slice, bf16[16]{0:T(256)(128)(2,1)S(1)} %dynamic-update-slice.1, ...), channel_id=1, replica_groups=mesh['fsdp'=4,'ctx'=2,'tp'=4] {'fsdp','ctx'}, use_global_device_ids=true, to_apply=%add.27 | all-reduce | flops 48 | bytes 192
  1785.0 36.6 %all-gather.2 = bf16[8,1,128]{2,1,0:T(2,128)(2,1)S(1)} all-gather(bf16[1,1,128]{2,1,0:T(2,128)(2,1)S(1)} %bitcast.350), channel_id=1, replica_groups=mesh['fsdp'=4,'ctx'=2,'tp'=4] {'fsdp','ctx'}, dimensions={0}, use_global_device_ids=true | all-gather | bytes 2304 | tf_op jit(solution)/shard_map/all_gather | solution.py:899
  1827.5 30.5 %all-gather = bf16[8,2,2048]{2,1,0:T(2,128)(2,1)S(1)} all-gather(bf16[1,2,2048]{2,1,0:T(2,128)(2,1)S(1)} %fusion.45), channel_id=1, replica_groups=mesh['fsdp'=4,'ctx'=2,'tp'=4] {'fsdp','ctx'}, dimensions={0}, use_global_device_ids=true | all-gather | bytes 73728 | tf_op jit(solution)/shard_map/all_gather | solution.py:899
  1858.8 16.3 all-gather.1
  1875.6 18.5 all_gather.62
  1904.1 6.3 fusion.124
  1922.7 7.5 all_gather.55
  1934.1 29.4 %all_gather.60 = bf16[3,128,1024]{2,1,0:T(8,128)(2,1)S(1)} all-gather(bf16[3,128,128]{2,1,0:T(8,128)(2,1)S(1)} %pad_maximum_fusion.16), channel_id=1, replica_groups=mesh['fsdp'=4,'ctx'=2,'tp'=4] {'fsdp','ctx'}, dimensions={2}, use_global_device_ids=true | all-gather | bytes 884736 | tf_op jit(solution)/shard_map/all_gather | solution.py:899
  1969.7 6.3 copy.281
  1976.0 7.2 reshape.440
  1989.5 39.8 %all-reduce.30 = (f32[4096]{0:T(1024)}, f32[2048]{0:T(1024)}, f32[2048]{0:T(1024)}, f32[4,256]{1,0:T(4,128)}, f32[256]{0:T(256)}) all-reduce(f32[4096]{0:T(1024)S(1)} %get-tuple-element.40, f32[2048]{0:T(1024)S(1)} %copy-done.109, f32[2048]{0:T(1024)S(1)} %copy-done.108, ...), channel_id=1, replica_groups=mesh['fsdp'=4,'ctx'=2,'tp'=4] {'fsdp','ctx','tp'}, use_global_device_ids=true, to_apply=%region_25.26 | all-reduce | flops 9472 | bytes 75776 | tf_op jit(solution)/shard_map/psum | solution.py:902
  2029.3 7.1 all-gather.26.cloned.1.call-done
  2036.4 6.8 convolution_bitcast_fusion
  2043.2 7.1 convolution_bitcast_fusion.1
  (611 shorter events, 307.1 us)
Async XLA Ops:
  7.2 701.1 %copy-start = (bf16[2048,256]{1,0:T(8,128)(2,1)S(1)}, bf16[2048,256]{1,0:T(8,128)(2,1)}, u32[]{:S(2)}) copy-start(bf16[2048,256]{1,0:T(8,128)(2,1)} %param.39) | copy-start | bytes 3145732
  7.2 202.0 %all-gather.12.cloned.1.call-start = ((), (), s32[]{:S(2)}) async-start(), calls=%async_computation.18 | async-start | bytes 14598144 | tf_op jit(solution)/shard_map/all_gather | solution.py:598
  15.7 30.4 %all-to-all-start.1 = ((bf16[8,128,256]{2,1,0:T(8,128)(2,1)}), bf16[8,128,256]{2,1,0:T(8,128)(2,1)S(1)}, u32[]{:S(2)}, u32[]{:S(2)}) async-start(bf16[8,128,256]{2,1,0:T(8,128)(2,1)} %bitcast.23), calls=%async_computation.1 | async-start | bytes 1048576 | tf_op jit(solution)/shard_map/all_to_all | solution.py:606
  46.1 153.3 %all-to-all-start = ((bf16[3,512,1024]{1,0,2:T(4,128)(2,1)}), bf16[3,512,1024]{1,0,2:T(4,128)(2,1)}, u32[]{:S(2)}, u32[]{:S(2)}) async-start(bf16[3,512,1024]{1,0,2:T(4,128)(2,1)} %copy.233), calls=%async_computation | async-start | bytes 8388608 | tf_op jit(solution)/shard_map/all_to_all | solution.py:606
  50.7 311.8 %reduce-scatter.7.cloned.1.call-start = ((), (), s32[]{:S(2)}) async-start(), calls=%async_computation.19 | async-start | bytes 6488064 | tf_op jit(solution)/shard_map/reduce_scatter | solution.py:602
  50.8 180.0 %copy-start.150 = (f32[64]{0:T(128)}, f32[64]{0:T(128)S(1)}, u32[]{:S(2)}) copy-start(f32[64]{0:T(128)S(1)} %multiply_power_fusion) | copy-start | bytes 772
  50.8 184.0 %copy-start.79 = (pred[384,384]{0,1:T(8,128)(4,1)}, pred[384,384]{0,1:T(8,128)(4,1)S(1)}, u32[]{:S(2)}) copy-start(pred[384,384]{0,1:T(8,128)(4,1)S(1)} %iota_compare_fusion.1) | copy-start | bytes 442372
  204.6 33.2 %copy-start.28 = (bf16[1,8,512,128]{3,2,1,0:T(8,128)(2,1)}, bf16[1,8,512,128]{3,2,1,0:T(8,128)(2,1)S(1)}, u32[]{:S(2)}) copy-start(bf16[1,8,512,128]{3,2,1,0:T(8,128)(2,1)S(1)} %copy.237) | copy-start | bytes 3145732
  248.5 114.0 %copy-start.60 = (bf16[192,2048]{1,0:T(8,128)(2,1)S(1)}, bf16[192,2048]{1,0:T(8,128)(2,1)}, u32[]{:S(2)}) copy-start(bf16[192,2048]{1,0:T(8,128)(2,1)} %param.25) | copy-start | bytes 2359300
  248.5 115.2 %copy-start.96 = (f32[2048]{0:T(1024)S(1)}, f32[2048]{0:T(1024)}, u32[]{:S(2)}) copy-start(f32[2048]{0:T(1024)} %param.34) | copy-start | bytes 24580
  248.5 227.4 %all-gather.14.cloned.1.call-start = ((), (), s32[]{:S(2)}) async-start(), calls=%async_computation.20 | async-start | bytes 6488064 | tf_op jit(solution)/shard_map/all_gather | solution.py:598
  365.4 32.9 %all-to-all-start.3 = ((bf16[8,256,256]{2,1,0:T(8,128)(2,1)}), bf16[8,256,256]{2,1,0:T(8,128)(2,1)S(1)}, u32[]{:S(2)}, u32[]{:S(2)}) async-start(bf16[8,256,256]{2,1,0:T(8,128)(2,1)} %bitcast.31), calls=%async_computation.4 | async-start | bytes 2097152 | tf_op jit(solution)/shard_map/all_to_all | solution.py:606
  399.3 72.8 %all-to-all-start.2 = ((bf16[2,256,2048]{1,0,2:T(2,128)(2,1)}), bf16[2,256,2048]{1,0,2:T(2,128)(2,1)S(1)}, u32[]{:S(2)}, u32[]{:S(2)}) async-start(bf16[2,256,2048]{1,0,2:T(2,128)(2,1)} %copy.240), calls=%async_computation.3 | async-start | bytes 4194304 | tf_op jit(solution)/shard_map/all_to_all | solution.py:606
  403.0 200.6 %reduce-scatter.9.cloned.1.call-start = ((), (), s32[]{:S(2)}) async-start(), calls=%async_computation.21 | async-start | bytes 6488064 | tf_op jit(solution)/shard_map/reduce_scatter | solution.py:602
  489.9 113.7 %copy-start.22 = (bf16[48,2048]{1,0:T(8,128)(2,1)S(1)}, bf16[48,2048]{1,0:T(8,128)(2,1)}, u32[]{:S(2)}) copy-start(bf16[48,2048]{1,0:T(8,128)(2,1)} %reduce-scatter.7.cloned.1.call-done) | copy-start | bytes 589828
  489.9 114.9 %copy-start.94 = (f32[2048]{0:T(1024)S(1)}, f32[2048]{0:T(1024)}, u32[]{:S(2)}) copy-start(f32[2048]{0:T(1024)} %param.37) | copy-start | bytes 24580
  489.9 198.7 %all-gather.16.cloned.1.call-start = ((), (), s32[]{:S(2)}) async-start(), calls=%async_computation.22 | async-start | bytes 6488064 | tf_op jit(solution)/shard_map/all_gather | solution.py:598
  605.6 153.6 %all-gather.18.cloned.1.call-start = ((), (), s32[]{:S(2)}) async-start(), calls=%async_computation.23 | async-start | bytes 6488064 | tf_op jit(solution)/shard_map/all_gather | solution.py:598
  607.3 21.5 %all-to-all-start.5 = ((bf16[8,128,256]{2,1,0:T(8,128)(2,1)}), bf16[8,128,256]{2,1,0:T(8,128)(2,1)S(1)}, u32[]{:S(2)}, u32[]{:S(2)}) async-start(bf16[8,128,256]{2,1,0:T(8,128)(2,1)} %bitcast.52), calls=%async_computation.7 | async-start | bytes 1048576 | tf_op jit(solution)/shard_map/all_to_all | solution.py:606
  611.7 24.5 %copy-start.160 = (f32[16]{0:T(128)S(1)}, f32[16]{0:T(128)}, u32[]{:S(2)}) copy-start(f32[16]{0:T(128)} %param.46) | copy-start | bytes 196
  611.7 26.3 %copy-start.141 = (f32[4,256]{1,0:T(4,128)S(1)}, f32[4,256]{1,0:T(4,128)}, u32[]{:S(2)}) copy-start(f32[4,256]{1,0:T(4,128)} %param.43) | copy-start | bytes 12292
  628.7 36.9 %all-to-all-start.4 = ((bf16[2,256,1024]{1,0,2:T(2,128)(2,1)}), bf16[2,256,1024]{1,0,2:T(2,128)(2,1)S(1)}, u32[]{:S(2)}, u32[]{:S(2)}) async-start(bf16[2,256,1024]{1,0,2:T(2,128)(2,1)} %copy.245), calls=%async_computation.6 | async-start | bytes 2097152 | tf_op jit(solution)/shard_map/all_to_all | solution.py:606
  632.3 369.2 %reduce-scatter.13.cloned.1.call-start = ((), (), s32[]{:S(2)}) async-start(), calls=%async_computation.25 | async-start | bytes 7299072 | tf_op jit(solution)/shard_map/reduce_scatter | solution.py:602
  667.2 26.0 %copy-start.26 = (bf16[1,8,256,128]{3,2,1,0:T(8,128)(2,1)}, bf16[1,8,256,128]{3,2,1,0:T(8,128)(2,1)S(1)}, u32[]{:S(2)}) copy-start(bf16[1,8,256,128]{3,2,1,0:T(8,128)(2,1)S(1)} %copy.247) | copy-start | bytes 1572868
  725.6 33.6 %copy-start.124 = (f32[128]{0:T(128)S(1)}, f32[128]{0:T(128)}, u32[]{:S(2)}) copy-start(f32[128]{0:T(128)} %dynamic_slice.51) | copy-start | bytes 1540
  759.2 46.0 %copy-start.8 = (f32[1536,128]{1,0:T(8,128)S(1)}, f32[1536,128]{1,0:T(8,128)}, u32[]{:S(2)}) copy-start(f32[1536,128]{1,0:T(8,128)} %get-tuple-element.70) | copy-start | bytes 2359300
  759.2 46.0 %copy-start.125 = (f32[128]{0:T(128)S(1)}, f32[128]{0:T(128)}, u32[]{:S(2)}) copy-start(f32[128]{0:T(128)} %dynamic_slice.51) | copy-start | bytes 1540
  881.5 120.0 %copy-start.95 = (f32[2048]{0:T(1024)S(1)}, f32[2048]{0:T(1024)}, u32[]{:S(2)}) copy-start(f32[2048]{0:T(1024)} %param.37) | copy-start | bytes 24580
  881.5 120.0 %copy-start.123 = (f32[48]{0:T(128)S(1)}, f32[48]{0:T(128)}, u32[]{:S(2)}) copy-start(f32[48]{0:T(128)} %copy-done.122) | copy-start | bytes 580
  881.5 122.0 %copy-start.158 = (f32[48]{0:T(128)S(1)}, f32[48]{0:T(128)}, u32[]{:S(2)}) copy-start(f32[48]{0:T(128)} %copy-done.157) | copy-start | bytes 580
  881.6 195.5 %copy-start.35 = (bf16[256,8,256]{0,2,1:T(8,128)(2,1)S(1)}, bf16[256,8,256]{0,2,1:T(8,128)(2,1)}, u32[]{:S(2)}) copy-start(bf16[256,8,256]{0,2,1:T(8,128)(2,1)} %copy.244) | copy-start | bytes 3145732
  881.6 195.5 %all-gather.20.cloned.1.call-start = ((), (), s32[]{:S(2)}) async-start(), calls=%async_computation.26 | async-start | bytes 7299072 | tf_op jit(solution)/shard_map/all_gather | solution.py:598
  1006.1 197.8 %reduce-scatter.15.cloned.1.call-start = ((), (), s32[]{:S(2)}) async-start(), calls=%async_computation.27 | async-start | bytes 6488064 | tf_op jit(solution)/shard_map/reduce_scatter | solution.py:602
  1090.1 233.7 %reduce-scatter.11.cloned.1.call-start = ((), (), s32[]{:S(2)}) async-start(), calls=%async_computation.24 | async-start | bytes 6488064 | tf_op jit(solution)/shard_map/reduce_scatter | solution.py:602
  1095.7 108.1 %copy-start.23 = (bf16[48,2048]{1,0:T(8,128)(2,1)S(1)}, bf16[48,2048]{1,0:T(8,128)(2,1)}, u32[]{:S(2)}) copy-start(bf16[48,2048]{1,0:T(8,128)(2,1)} %reduce-scatter.7.cloned.1.call-done) | copy-start | bytes 589828
  1095.7 108.1 %copy-start.61 = (bf16[192,2048]{1,0:T(8,128)(2,1)S(1)}, bf16[192,2048]{1,0:T(8,128)(2,1)}, u32[]{:S(2)}) copy-start(bf16[192,2048]{1,0:T(8,128)(2,1)} %param.25) | copy-start | bytes 2359300
  1095.7 108.1 %copy-start.97 = (f32[2048]{0:T(1024)S(1)}, f32[2048]{0:T(1024)}, u32[]{:S(2)}) copy-start(f32[2048]{0:T(1024)} %param.34) | copy-start | bytes 24580
  1095.7 108.1 %copy-start.133 = (f32[48]{0:T(128)S(1)}, f32[48]{0:T(128)}, u32[]{:S(2)}) copy-start(f32[48]{0:T(128)} %copy-done.132) | copy-start | bytes 580
  1095.7 109.8 %copy-start.154 = (f32[48]{0:T(128)S(1)}, f32[48]{0:T(128)}, u32[]{:S(2)}) copy-start(f32[48]{0:T(128)} %copy-done.153) | copy-start | bytes 580
  1095.7 228.1 %copy-start.45 = (f32[48,2048]{1,0:T(8,128)S(1)}, f32[48,2048]{1,0:T(8,128)}, u32[]{:S(2)}) copy-start(f32[48,2048]{1,0:T(8,128)} %copy-done.44) | copy-start | bytes 1179652
  1095.8 230.7 %copy-start.111 = (f32[4,384]{1,0:T(4,128)S(1)}, f32[4,384]{1,0:T(4,128)}, u32[]{:S(2)}) copy-start(f32[4,384]{1,0:T(4,128)} %copy-done.110) | copy-start | bytes 18436
  1095.8 299.8 %all-gather.22.cloned.1.call-start = ((), (), s32[]{:S(2)}) async-start(), calls=%async_computation.28 | async-start | bytes 6488064 | tf_op jit(solution)/shard_map/all_gather | solution.py:598
  1326.2 657.1 %reduce-scatter.17.cloned.1.call-start = ((), (), s32[]{:S(2)}) async-start(), calls=%async_computation.29 | async-start | bytes 14192640 | tf_op jit(solution)/shard_map/reduce_scatter | solution.py:602
  1326.5 73.9 %copy-start.3 = (bf16[4,384,384]{1,2,0:T(8,128)(2,1)S(1)}, bf16[4,384,384]{1,2,0:T(8,128)(2,1)}, u32[]{:S(2)}) copy-start(bf16[4,384,384]{1,2,0:T(8,128)(2,1)} %copy-done.2) | copy-start | bytes 3538948
  1326.5 74.4 %copy-start.47 = (bf16[1536,128]{1,0:T(8,128)(2,1)S(1)}, bf16[1536,128]{1,0:T(8,128)(2,1)}, u32[]{:S(2)}) copy-start(bf16[1536,128]{1,0:T(8,128)(2,1)} %copy-done.46) | copy-start | bytes 1179652
  1474.4 23.9 %all-to-all-start.11 = ((bf16[128,8,256]{2,0,1:T(8,128)(2,1)}), bf16[128,8,256]{2,0,1:T(8,128)(2,1)S(1)}, u32[]{:S(2)}, u32[]{:S(2)}) async-start(bf16[128,8,256]{2,0,1:T(8,128)(2,1)} %bitcast.255), calls=%async_computation.17 | async-start | bytes 1048576 | tf_op jit(solution)/shard_map/all_to_all | solution.py:606
  1499.1 44.3 %all-to-all-start.10 = ((bf16[2,2048,128]{2,0,1:T(2,128)(2,1)}), bf16[2,2048,128]{2,0,1:T(2,128)(2,1)S(1)}, u32[]{:S(2)}, u32[]{:S(2)}) async-start(bf16[2,2048,128]{2,0,1:T(2,128)(2,1)} %copy.286), calls=%async_computation.16 | async-start | bytes 2097152 | tf_op jit(solution)/shard_map/all_to_all | solution.py:606
  1543.3 46.8 %all-to-all-start.9 = ((bf16[256,8,256]{2,0,1:T(8,128)(2,1)}), bf16[256,8,256]{2,0,1:T(8,128)(2,1)S(1)}, u32[]{:S(2)}, u32[]{:S(2)}) async-start(bf16[256,8,256]{2,0,1:T(8,128)(2,1)} %bitcast.289), calls=%async_computation.15 | async-start | bytes 2097152 | tf_op jit(solution)/shard_map/all_to_all | solution.py:606
  1591.1 70.6 %all-to-all-start.8 = ((bf16[2,2048,256]{2,0,1:T(2,128)(2,1)}), bf16[2,2048,256]{2,0,1:T(2,128)(2,1)S(1)}, u32[]{:S(2)}, u32[]{:S(2)}) async-start(bf16[2,2048,256]{2,0,1:T(2,128)(2,1)} %copy.283), calls=%async_computation.14 | async-start | bytes 4194304 | tf_op jit(solution)/shard_map/all_to_all | solution.py:606
  1661.7 34.2 %all-to-all-start.7 = ((bf16[128,8,256]{2,0,1:T(8,128)(2,1)}), bf16[128,8,256]{2,0,1:T(8,128)(2,1)}, u32[]{:S(2)}, u32[]{:S(2)}) async-start(bf16[128,8,256]{2,0,1:T(8,128)(2,1)} %bitcast.313), calls=%async_computation.13 | async-start | bytes 1048576 | tf_op jit(solution)/shard_map/all_to_all | solution.py:606
  1695.9 89.1 %copy-start.144 = (bf16[128]{0:T(256)(128)(2,1)S(1)}, bf16[128]{0:T(256)(128)(2,1)}, u32[]{:S(2)}) copy-start(bf16[128]{0:T(256)(128)(2,1)} %get-tuple-element.87) | copy-start | bytes 772
  1695.9 127.8 %copy-start.107 = (bf16[1536,2]{0,1:T(2,128)(2,1)S(1)}, bf16[1536,2]{0,1:T(2,128)(2,1)}, u32[]{:S(2)}) copy-start(bf16[1536,2]{0,1:T(2,128)(2,1)} %copy-done.106) | copy-start | bytes 18436
  1696.0 270.9 %all-to-all-start.6 = ((bf16[3,4096,128]{2,0,1:T(4,128)(2,1)}), bf16[3,4096,128]{2,0,1:T(4,128)(2,1)}, u32[]{:S(2)}, u32[]{:S(2)}) async-start(bf16[3,4096,128]{2,0,1:T(4,128)(2,1)} %copy.280), calls=%async_computation.12 | async-start | bytes 8388608 | tf_op jit(solution)/shard_map/all_to_all | solution.py:606
  1702.1 334.3 %all-gather.26.cloned.1.call-start = ((), (), s32[]{:S(2)}) async-start(), calls=%async_computation.31 | async-start | bytes 1216512 | tf_op jit(solution)/shard_map/all_gather | solution.py:598
  1823.8 35.0 %copy-start.145 = (bf16[128]{0:T(256)(128)(2,1)S(1)}, bf16[128]{0:T(256)(128)(2,1)}, u32[]{:S(2)}) copy-start(bf16[128]{0:T(256)(128)(2,1)} %get-tuple-element.44) | copy-start | bytes 772
  1823.8 51.9 %copy-start.146 = (f32[128]{0:T(128)S(1)}, f32[128]{0:T(128)}, u32[]{:S(2)}) copy-start(f32[128]{0:T(128)} %get-tuple-element.36) | copy-start | bytes 1540
  1823.8 51.9 %copy-start.147 = (f32[128]{0:T(128)S(1)}, f32[128]{0:T(128)}, u32[]{:S(2)}) copy-start(f32[128]{0:T(128)} %get-tuple-element.37) | copy-start | bytes 1540
  1823.8 51.9 %copy-start.148 = (f32[128]{0:T(128)S(1)}, f32[128]{0:T(128)}, u32[]{:S(2)}) copy-start(f32[128]{0:T(128)} %get-tuple-element.38) | copy-start | bytes 1540
  1823.8 51.8 %copy-start.149 = (f32[128]{0:T(128)S(1)}, f32[128]{0:T(128)}, u32[]{:S(2)}) copy-start(f32[128]{0:T(128)} %get-tuple-element.39) | copy-start | bytes 1540
  1823.8 71.0 %copy-start.137 = (f32[256]{0:T(256)S(1)}, f32[256]{0:T(256)}, u32[]{:S(2)}) copy-start(f32[256]{0:T(256)} %get-tuple-element.31) | copy-start | bytes 3076
  1823.8 71.0 %copy-start.138 = (f32[256]{0:T(256)S(1)}, f32[256]{0:T(256)}, u32[]{:S(2)}) copy-start(f32[256]{0:T(256)} %get-tuple-element.32) | copy-start | bytes 3076
  1823.8 71.0 %copy-start.139 = (f32[256]{0:T(256)S(1)}, f32[256]{0:T(256)}, u32[]{:S(2)}) copy-start(f32[256]{0:T(256)} %get-tuple-element.33) | copy-start | bytes 3076
  1823.8 71.0 %copy-start.140 = (f32[256]{0:T(256)S(1)}, f32[256]{0:T(256)}, u32[]{:S(2)}) copy-start(f32[256]{0:T(256)} %get-tuple-element.34) | copy-start | bytes 3076
  1984.7 72.5 %all-gather.24.cloned.1.call-start = ((), (), s32[]{:S(2)}) async-start(), calls=%async_computation.30 | async-start | bytes 1966080 | tf_op jit(solution)/shard_map/all_gather | solution.py:885
  (154 other events, 873.4 us)
Sparse Core Ops, SparseCore 0:
  15.8 183.2 all-gather.11
  248.6 113.8 reduce-scatter.6
  366.0 105.8 all-gather.13
  490.0 113.4 reduce-scatter.8
  606.8 81.7 all-gather.15
  691.3 67.7 all-gather.17
  881.7 119.7 reduce-scatter.12
  1006.2 70.8 all-gather.19
  1090.3 113.5 reduce-scatter.14
  1209.9 113.9 reduce-scatter.10
  1327.3 68.1 all-gather.21
  1469.7 207.1 reduce-scatter.16
  1984.8 51.6 all-gather.25
  2038.4 18.6 all-gather.23

commit v2 on v1

--- a/solution.py
+++ b/solution.py
@@ -1,12 +1,13 @@
 import jax
 import jax.numpy as jnp
 from jax import lax
+from jax.experimental import pallas as pl
+from jax.experimental.pallas import tpu as pltpu
 from jax.sharding import PartitionSpec as P
 
 MODEL_WIDTH = 2048
 AHEADS = 32
 AHD = 128
-MHEADS = 64
 INNER = 4096
 MIXER_HEAD_SIZE = 64
 STATE = 128
@@ -594,16 +595,680 @@
 EVERY = ("fsdp", "ctx", "tp")
 
 
-def gather_rows(values):
-    return lax.all_gather(values, EVERY, axis=0, tiled=True)
-
-
-def scatter_rows(partial_sum):
-    return lax.psum_scatter(partial_sum, EVERY, scatter_dimension=0, tiled=True).astype(jnp.float32)
-
-
-def spread(weight, split, join):
-    return lax.all_to_all(weight, PLANE, split_axis=split, concat_axis=join, tiled=True)
+MESH = pl.DeviceIdType.MESH
+IN_VMEM = pl.BlockSpec(memory_space=pltpu.VMEM)
+IN_HBM = pl.BlockSpec(memory_space=pltpu.HBM)
+IN_SMEM = pl.BlockSpec(memory_space=pltpu.SMEM)
+DMA = pltpu.SemaphoreType.DMA
+
+
+class Place:
+    def __init__(self, sizes):
+        self.groups, self.ctx, self.tp = sizes
+        g, c, t = (lax.axis_index(name) for name in EVERY)
+        y, k = t // 2, lax.rem(t, 2)
+        self.g, self.c, self.t, self.y, self.k = g, c, t, y, k
+        self.core = (g, c, y * 2 + 1 - k)
+        self.side_y = (g, c, (1 - y) * 2 + k)
+        self.side_x = (g, 1 - c, t)
+        self.line = [(lax.rem(g + d, self.groups), c, t) for d in range(1, self.groups)]
+        self.plane = self.groups * self.ctx
+        self.index = g * self.ctx + c
+
+    def plane_peer(self, d):
+        other = lax.rem(self.index + d, self.plane)
+        return other, (other // self.ctx, lax.rem(other, self.ctx), self.t)
+
+    def plane_source(self, d):
+        return lax.rem(self.index + self.plane - d, self.plane)
+
+
+def greet(devices):
+    barrier = pltpu.get_barrier_semaphore()
+    for device in devices:
+        pl.semaphore_signal(barrier, inc=1, device_id=device, device_id_type=MESH)
+    pl.semaphore_wait(barrier, len(devices))
+
+
+def remote(src, dst, send_sem, recv_sem, device):
+    return pltpu.make_async_remote_copy(
+        src_ref=src,
+        dst_ref=dst,
+        send_sem=send_sem,
+        recv_sem=recv_sem,
+        device_id=device,
+        device_id_type=MESH,
+    )
+
+
+def cut(ref, axis, index, width):
+    if axis is None:
+        return ref
+    at = [slice(None)] * len(ref.shape)
+    start = index * width
+    if width % 128 == 0:
+        start = pl.multiple_of(start, 128)
+    at[axis] = pl.ds(start, width)
+    return ref.at[tuple(at)]
+
+
+class Moves:
+    def __init__(self, place, specs, sources, targets, stages, send, recv, local):
+        self.sent = []
+        self.place, self.specs = place, specs
+        self.sources, self.targets = sources, targets
+        self.stages, self.send, self.recv, self.local = stages, send, recv, local
+
+    def part(self, i, to, origin):
+        split, join = self.specs[i]
+        src, dst = self.sources[i], self.targets[i]
+        n = self.place.plane
+        if split is None:
+            return src, dst.at[origin]
+        return (
+            cut(src, split, to, src.shape[split] // n),
+            cut(dst, join, origin, dst.shape[join] // n),
+        )
+
+    def start(self):
+        place = self.place
+        self.loads, self.queue = [], []
+        for i in range(len(self.specs)):
+            self.queue += [(i, d) for d in range(1, place.plane)]
+            src, _ = self.part(i, place.index, place.index)
+            load = pltpu.make_async_copy(src, self.stages[i], self.local.at[i, 0])
+            load.start()
+            self.loads.append(load)
+
+    def issue(self, count):
+        for i, d in self.queue[:count]:
+            other, device = self.place.plane_peer(d)
+            src, dst = self.part(i, other, self.place.index)
+            copy = remote(src, dst, self.send.at[i, d], self.recv.at[i, d], device)
+            copy.start()
+            self.sent.append(copy)
+        self.queue = self.queue[count:]
+
+    def settle(self):
+        self.stores = []
+        for i, load in enumerate(self.loads):
+            load.wait()
+            _, dst = self.part(i, self.place.index, self.place.index)
+            store = pltpu.make_async_copy(self.stages[i], dst, self.local.at[i, 1])
+            store.start()
+            self.stores.append(store)
+
+    def finish(self):
+        place = self.place
+        for i in range(len(self.specs)):
+            for d in range(1, place.plane):
+                _, device = place.plane_peer(d)
+                src, dst = self.part(i, place.index, place.plane_source(d))
+                remote(src, dst, self.send.at[i, d], self.recv.at[i, d], device).wait_recv()
+        for copy in self.sent:
+            copy.wait_send()
+        for store in self.stores:
+            store.wait()
+
+
+def moves_setup(moves, plane):
+    outs, scratch = [], []
+    for array, split, join in moves:
+        shape = list(array.shape)
+        part = list(array.shape)
+        if split is None:
+            shape = [plane] + shape
+        else:
+            part[split] //= plane
+            shape[split] //= plane
+            shape[join] *= plane
+        outs.append(jax.ShapeDtypeStruct(tuple(shape), array.dtype))
+        scratch.append(pltpu.VMEM(tuple(part), array.dtype))
+    n = len(moves)
+    if n:
+        scratch += [DMA((n, plane)), DMA((n, plane)), DMA((n, 2))]
+    return outs, scratch
+
+
+def spans(width, extra, count):
+    step = width // count
+    found = [(i * step, step) for i in range(count)]
+    if extra:
+        found.append((width, extra))
+    return found
+
+
+def gather_stage(place, x, o, pieces, sems, between):
+    zs, zr, s2, r2, s3, r3, s4, r4, own_sem = sems
+    g, c, y, k = place.g, place.c, place.y, place.k
+    n = len(pieces)
+    lines = place.groups - 1
+    own = pltpu.make_async_copy(x, o.at[g, c, y, k], own_sem)
+    own.start()
+    first = []
+    for q, (at, width) in enumerate(pieces):
+        cols = pl.ds(at, width)
+        for d in range(lines):
+            copy = remote(
+                x.at[:, cols], o.at[g, c, y, k, :, cols], zs.at[q, d], zr.at[q, d], place.line[d]
+            )
+            copy.start()
+            first.append(copy)
+    own.wait()
+    second, third, fourth = [None] * n, [None] * n, [None] * n
+
+    def to_side(q):
+        cols = pl.ds(*pieces[q])
+        for d in range(lines):
+            src = lax.rem(g + place.groups - d - 1, place.groups)
+            remote(
+                x.at[:, cols], o.at[src, c, y, k, :, cols], zs.at[q, d], zr.at[q, d], place.line[d]
+            ).wait_recv()
+        part = o.at[:, c, y, k, :, cols]
+        device = place.side_y if q % 2 == 0 else place.side_x
+        second[q] = remote(part, part, s2.at[q], r2.at[q], device)
+        second[q].start()
+
+    def to_other_side(q):
+        cols = pl.ds(*pieces[q])
+        second[q].wait_recv()
+        if q % 2 == 0:
+            part, device = o.at[:, c, :, k, :, cols], place.side_x
+        else:
+            part, device = o.at[:, :, y, k, :, cols], place.side_y
+        third[q] = remote(part, part, s3.at[q], r3.at[q], device)
+        third[q].start()
+
+    def to_core(q):
+        cols = pl.ds(*pieces[q])
+        third[q].wait_recv()
+        part = o.at[:, :, :, k, :, cols]
+        fourth[q] = remote(part, part, s4.at[q], r4.at[q], place.core)
+        fourth[q].start()
+
+    for step in range(n + 2):
+        between()
+        if step < n:
+            to_side(step)
+        if 0 <= step - 1 < n:
+            to_other_side(step - 1)
+        if 0 <= step - 2 < n:
+            to_core(step - 2)
+    for q in range(n):
+        fourth[q].wait_recv()
+    for copy in first + second + third + fourth:
+        copy.wait_send()
+
+
+def gather_sems(n, groups):
+    return [DMA((n, groups - 1)), DMA((n, groups - 1))] + [DMA((n,))] * 6 + [DMA]
+
+
+def scatter_stage(place, make, pieces, bufs, acc, sems, between):
+    theirs, mine, b1, b2, b3, b4 = bufs
+    sa, ra, sb, rb, sc, rc, sd, rd = sems
+    g, c, y, k = place.g, place.c, place.y, place.k
+    n = len(pieces)
+    lines = place.groups - 1
+    f32, bf16 = jnp.float32, jnp.bfloat16
+    c1, c2, c3, c4 = [None] * n, [None] * n, [None] * n, [None] * n
+
+    def to_core(q):
+        cols = pl.ds(*pieces[q])
+        make(q, theirs, 1 - k)
+        c1[q] = remote(theirs.at[..., cols], b1.at[..., cols], sa.at[q], ra.at[q], place.core)
+        c1[q].start()
+        make(q, mine, k)
+
+    def to_side(q):
+        cols = pl.ds(*pieces[q])
+        c1[q].wait_recv()
+        b1[..., cols] = (b1[..., cols].astype(f32) + mine[..., cols].astype(f32)).astype(bf16)
+        if q % 2 == 0:
+            part, device = b1.at[:, :, 1 - y, :, cols], place.side_y
+        else:
+            part, device = b1.at[:, 1 - c, :, :, cols], place.side_x
+        c2[q] = remote(part, b2.at[:, :, :, cols], sb.at[q], rb.at[q], device)
+        c2[q].start()
+
+    def to_other_side(q):
+        cols = pl.ds(*pieces[q])
+        c2[q].wait_recv()
+        own = b1[:, :, y, :, cols] if q % 2 == 0 else b1[:, c, :, :, cols]
+        b2[:, :, :, cols] = (b2[:, :, :, cols].astype(f32) + own.astype(f32)).astype(bf16)
+        if q % 2 == 0:
+            part, device = b2.at[:, 1 - c, :, cols], place.side_x
+        else:
+            part, device = b2.at[:, 1 - y, :, cols], place.side_y
+        c3[q] = remote(part, b3.at[:, :, cols], sc.at[q], rc.at[q], device)
+        c3[q].start()
+
+    def along_line(q):
+        cols = pl.ds(*pieces[q])
+        c3[q].wait_recv()
+        own = b2[:, c, :, cols] if q % 2 == 0 else b2[:, y, :, cols]
+        b3[:, :, cols] = (b3[:, :, cols].astype(f32) + own.astype(f32)).astype(bf16)
+        c4[q] = []
+        for d in range(lines):
+            to = lax.rem(g + d + 1, place.groups)
+            copy = remote(
+                b3.at[to, :, cols], b4.at[d, :, cols], sd.at[q, d], rd.at[q, d], place.line[d]
+            )
+            copy.start()
+            c4[q].append(copy)
+
+    def land(q):
+        cols = pl.ds(*pieces[q])
+        total = b3[g, :, cols].astype(f32)
+        for d in range(lines):
+            c4[q][d].wait_recv()
+            total = total + b4[d, :, cols].astype(f32)
+        acc[:, cols] = total
+
+    for step in range(n + 4):
+        for lag, stage in enumerate((to_core, to_side, to_other_side, along_line, land)):
+            if 0 <= step - lag < n:
+                stage(step - lag)
+        between()
+    for q in range(n):
+        for copy in [c1[q], c2[q], c3[q]] + c4[q]:
+            copy.wait_send()
+
+
+def scatter_scratch(n, groups, rows, width):
+    bf16 = jnp.bfloat16
+    bufs = [
+        pltpu.VMEM((groups, 2, 2, rows, width), bf16),
+        pltpu.VMEM((groups, 2, 2, rows, width), bf16),
+        pltpu.VMEM((groups, 2, 2, rows, width), bf16),
+        pltpu.VMEM((groups, 2, rows, width), bf16),
+        pltpu.VMEM((groups, rows, width), bf16),
+        pltpu.VMEM((groups - 1, rows, width), bf16),
+        pltpu.VMEM((rows, width), jnp.float32),
+    ]
+    sems = [DMA((n,))] * 6 + [DMA((n, groups - 1))] * 2
+    return bufs, sems
+
+
+def rms_rows(x, gain):
+    return x * lax.rsqrt(jnp.mean(x * x, axis=-1, keepdims=True) + epsilon) * gain
+
+
+def rms_back(x, gain, grad):
+    inverse = lax.rsqrt(jnp.mean(x * x, axis=-1, keepdims=True) + epsilon)
+    scaled = grad * gain
+    along = jnp.mean(scaled * x, axis=-1, keepdims=True)
+    d_gain = jnp.sum(grad * x * inverse, axis=0, keepdims=True)
+    return scaled * inverse - x * inverse**3 * along, d_gain
+
+
+NT = (((1,), (1,)), ((), ()))
+NN = (((1,), (0,)), ((), ()))
+
+
+def exchange(
+    sizes,
+    number,
+    products,
+    extra,
+    finish,
+    finish_args,
+    finish_outs,
+    gathered,
+    moves,
+    early_share=60,
+    tail=0,
+):
+    groups, ctx, tp = sizes
+    f32, bf16 = jnp.float32, jnp.bfloat16
+    total_rows = products[0][0].shape[0]
+    rows = total_rows // (groups * ctx * tp)
+    width = products[0][1].shape[-2 if products[0][3] else -1]
+    rights_all, places = [], []
+    for _, right, _, _ in products:
+        found = [i for i, other in enumerate(rights_all) if other is right]
+        places.append(found[0] if found else len(rights_all))
+        if not found:
+            rights_all.append(right)
+    more = 0 if extra is None else extra.shape[1]
+    pieces = spans(width, more, 4)
+    out_pieces = spans(gathered, 0, 1) if gathered < 1024 else spans(2048, gathered - 2048, 4)
+    move_outs, move_scratch = moves_setup(moves, groups * ctx)
+    bufs, sems = scatter_scratch(len(pieces), groups, rows, width + more)
+    n_prod, n_args, n_outs, n_moves = len(products), len(finish_args), len(finish_outs), len(moves)
+    move_specs = [(split, join) for _, split, join in moves]
+
+    def kernel(*refs):
+        refs = list(refs)
+
+        def take(count):
+            head = refs[:count]
+            del refs[:count]
+            return head
+
+        lefts, rights = take(n_prod), take(len(rights_all))
+        extra_ref = take(1)[0] if more else None
+        args, sources = take(n_args), take(n_moves)
+        o = take(1)[0]
+        o_tail = take(1)[0] if tail else None
+        outs, targets = take(n_outs), take(n_moves)
+        b = take(len(bufs))
+        acc = b.pop()
+        s = take(len(sems))
+        low = take(1)[0]
+        gs = take(9)
+        if tail:
+            low_tail, ts = take(1)[0], take(5)
+        place = Place(sizes)
+        devices = [place.core, place.side_y]
+        if n_moves:
+            devices += [place.plane_peer(d)[1] for d in range(1, place.plane)]
+        else:
+            devices += [place.side_x] + place.line
+        greet(devices)
+        carried = None
+        if n_moves:
+            stages = take(n_moves)
+            send, recv, local = take(3)
+            carried = Moves(place, move_specs, sources, targets, stages, send, recv, local)
+
+        def make(q, into, core):
+            at, size = pieces[q]
+            if at >= width:
+                into[..., pl.ds(at, size)] = extra_ref[:, :, :, core]
+                return
+
+            def block(i, _):
+                total = None
+                for left, where, (_, _, lead, transposed) in zip(lefts, places, products):
+                    right = rights[where] if lead is None else rights[where].at[lead]
+                    a = left[i, :, :, core]
+                    a = a.reshape(-1, a.shape[-1])
+                    if transposed:
+                        part = lax.dot_general(
+                            a, right[pl.ds(at, size), :], NT, preferred_element_type=f32
+                        )
+                    else:
+                        part = lax.dot_general(
+                            a, right[:, pl.ds(at, size)], NN, preferred_element_type=f32
+                        )
+                    total = part if total is None else total + part
+                into[i, :, :, :, pl.ds(at, size)] = total.astype(bf16).reshape(
+                    ctx, tp // 2, rows, size
+                )
+                return 0
+
+            lax.fori_loop(0, groups, block, 0)
+
+        def between(count):
+            return lambda: carried.issue(count) if carried is not None else None
+
+        if carried is not None:
+            carried.start()
+        steps = len(pieces) + 4
+        early = -(-(n_moves * (groups * ctx - 1) * early_share) // (100 * steps))
+        scatter_stage(place, make, pieces, b, acc, s, between(early))
+        if carried is not None:
+            carried.settle()
+        finish(place, acc, args, outs, low, low_tail if tail else None)
+        if tail:
+            ys, yr, ks, kr, own_sem = ts
+            y, k = place.y, place.k
+            own = pltpu.make_async_copy(low_tail, o_tail.at[y, k], own_sem)
+            own.start()
+            to_y = remote(low_tail, o_tail.at[y, k], ys, yr, place.side_y)
+            to_y.start()
+            own.wait()
+        late = -(-n_moves * (groups * ctx - 1) // max(1, len(out_pieces)))
+        gather_stage(place, low, o, out_pieces, gs, between(late))
+        if tail:
+            to_y.wait_recv()
+            part = o_tail.at[:, k]
+            to_k = remote(part, part, ks, kr, place.core)
+            to_k.start()
+            to_k.wait_recv()
+            to_y.wait_send()
+            to_k.wait_send()
+        if carried is not None:
+            carried.issue(10**6)
+            carried.finish()
+
+    S = jax.ShapeDtypeStruct
+    out_shape = [S((groups, ctx, tp // 2, 2, rows, gathered), bf16)]
+    out_specs = [IN_VMEM]
+    if tail:
+        out_shape.append(S((tp // 2, 2, rows, tail), bf16))
+        out_specs.append(IN_VMEM)
+    out_shape += [S(shape, f32) for shape in finish_outs] + move_outs
+    out_specs += [IN_VMEM] * n_outs + [IN_HBM] * n_moves
+    scratch = bufs + sems + [pltpu.VMEM((rows, gathered), bf16)]
+    scratch += gather_sems(len(out_pieces), groups)
+    if tail:
+        scratch += [pltpu.VMEM((rows, tail), bf16)] + [DMA] * 5
+    scratch += move_scratch
+    split = (groups, ctx, tp // 2, 2, rows)
+    operands = [product[0].reshape(*split, product[0].shape[1]) for product in products]
+    operands += rights_all
+    if more:
+        operands.append(extra.reshape(*split, more))
+    operands += list(finish_args)
+    in_specs = [IN_VMEM] * len(operands) + [IN_HBM] * n_moves
+    operands += [array for array, _, _ in moves]
+    results = pl.pallas_call(
+        kernel,
+        out_shape=out_shape,
+        in_specs=in_specs,
+        out_specs=out_specs,
+        scratch_shapes=scratch,
+        name=f"exchange_{number}",
+        compiler_params=pltpu.CompilerParams(
+            collective_id=number, has_side_effects=True, vmem_limit_bytes=62 * 2**20
+        ),
+    )(*operands)
+    results = list(results)
+    spread_out = results.pop(0).reshape(total_rows, gathered)
+    tail_out = [results.pop(0).reshape(tp * rows, tail)] if tail else []
+    return [spread_out] + tail_out + results
+
+
+def opening(sizes, number, hidden, embeds, lengths, gain, down_all, moves):
+    groups, ctx, tp = sizes
+    f32, bf16 = jnp.float32, jnp.bfloat16
+    rows = hidden.shape[0] // tp
+    half = hidden.shape[1]
+    mids = down_all.shape[1]
+    width = 2 * half + mids + 128
+    out_pieces = spans(4096, width - 4096, 4)
+    move_outs, move_scratch = moves_setup(moves, groups * ctx)
+    move_specs = [(split, join) for _, split, join in moves]
+    n_moves = len(moves)
+
+    def kernel(*refs):
+        hid, emb, lens, gain_ref, down_ref = refs[:5]
+        refs = list(refs[5:])
+        sources = refs[:n_moves]
+        o = refs[n_moves]
+        targets = refs[n_moves + 1 : 2 * n_moves + 1]
+        rest = refs[2 * n_moves + 1 :]
+        low, gs = rest[0], rest[1:10]
+        stages = rest[10 : 10 + n_moves]
+        send, recv, local = rest[10 + n_moves :]
+        place = Place(sizes)
+        greet(
+            [place.core, place.side_y]
+            + [place.plane_peer(d)[1] for d in range(1, place.plane)]
+        )
+        carried = Moves(place, move_specs, sources, targets, stages, send, recv, local)
+        carried.start()
+        carried.issue(2)
+        mine = pl.ds(pl.multiple_of(place.t * rows, 16), rows)
+        a, b = hid[mine, :].astype(f32), emb[mine, :].astype(f32)
+        squares = jnp.sum(a * a, axis=1, keepdims=True) + jnp.sum(b * b, axis=1, keepdims=True)
+        inverse = lax.rsqrt(squares / (2 * half) + epsilon)
+        low[:, :half] = (a * inverse * gain_ref[:, :half]).astype(bf16)
+        low[:, half : 2 * half] = (b * inverse * gain_ref[:, half:]).astype(bf16)
+        low[:, 2 * half : 2 * half + mids] = lax.dot_general(
+            low[:, : 2 * half], down_ref[...], NN, preferred_element_type=f32
+        ).astype(bf16)
+        slot = lax.broadcasted_iota(jnp.int32, (rows, 128), 0)
+        slot = slot + (place.c * tp + place.t) * rows
+        lane = lax.broadcasted_iota(jnp.int32, (rows, 128), 1)
+        segment, position, end = jnp.zeros_like(slot), slot, 0
+        for i in range(lengths.shape[1]):
+            length = lens[0, i]
+            end = end + length
+            passed = (slot >= end).astype(jnp.int32)
+            segment = segment + passed
+            position = position - passed * length
+        marks = jnp.where(lane == 0, segment, position)
+        low[:, 2 * half + mids :] = marks.astype(f32).astype(bf16)
+        gather_stage(place, low, o, out_pieces, gs, lambda: carried.issue(4))
+        carried.issue(10**6)
+        carried.settle()
+        carried.finish()
+
+    S = jax.ShapeDtypeStruct
+    results = pl.pallas_call(
+        kernel,
+        out_shape=[S((groups, ctx, tp // 2, 2, rows, width), bf16)] + move_outs,
+        in_specs=[IN_VMEM, IN_VMEM, IN_SMEM, IN_VMEM, IN_VMEM] + [IN_HBM] * n_moves,
+        out_specs=[IN_VMEM] + [IN_HBM] * n_moves,
+        scratch_shapes=[pltpu.VMEM((rows, width), bf16)]
+        + gather_sems(len(out_pieces), groups)
+        + move_scratch,
+        name=f"opening_{number}",
+        compiler_params=pltpu.CompilerParams(
+            collective_id=number, has_side_effects=True, vmem_limit_bytes=62 * 2**20
+        ),
+    )(hidden, embeds, lengths, gain.reshape(1, -1), down_all, *[array for array, _, _ in moves])
+    return [results[0].reshape(-1, width)] + list(results[1:])
+
+
+def sum_small(sizes, number, values):
+    groups, ctx, tp = sizes
+    f32 = jnp.float32
+
+    def kernel(x, o, zbuf, buf, zs, zr, ss, rs):
+        place = Place(sizes)
+        greet([place.core, place.side_y, place.side_x] + place.line)
+        copies = []
+        for d, device in enumerate(place.line):
+            copy = remote(x, zbuf.at[d], zs.at[d], zr.at[d], device)
+            copy.start()
+            copies.append(copy)
+        total = x[...]
+        for d in range(groups - 1):
+            copies[d].wait_recv()
+        order = [zbuf[d] for d in range(groups - 1)]
+        parts = []
+        for g in range(groups):
+            part = total
+            for d in range(groups - 1):
+                src = lax.rem(place.g + groups - d - 1, groups)
+                part = jnp.where(src == g, order[d], part)
+            parts.append(part)
+        total = parts[0]
+        for part in parts[1:]:
+            total = total + part
+        for i, device in enumerate((place.side_x, place.side_y, place.core)):
+            o[...] = total
+            copy = remote(o, buf.at[i], ss.at[i], rs.at[i], device)
+            copy.start()
+            copy.wait_recv()
+            copy.wait_send()
+            total = total + buf[i]
+        o[...] = total
+        for copy in copies:
+            copy.wait_send()
+
+    shape = values.shape
+    return pl.pallas_call(
+        kernel,
+        out_shape=jax.ShapeDtypeStruct(shape, f32),
+        in_specs=[IN_VMEM],
+        out_specs=IN_VMEM,
+        scratch_shapes=[
+            pltpu.VMEM((groups - 1, *shape), f32),
+            pltpu.VMEM((3, *shape), f32),
+            DMA((groups - 1,)),
+            DMA((groups - 1,)),
+            DMA((3,)),
+            DMA((3,)),
+        ],
+        name=f"sum_small_{number}",
+        compiler_params=pltpu.CompilerParams(collective_id=number, has_side_effects=True),
+    )(values)
+
+
+def finish_forward(place, acc, args, outs, low, low_tail):
+    rest, gain = args
+    outs[0][...] = rest[...] + acc[...]
+    low[...] = rms_rows(outs[0][...], gain[...]).astype(jnp.bfloat16)
+
+
+def finish_mixer_back(place, acc, args, outs, low, low_tail):
+    after_mlp, gain, cot, state_map = args
+    width = after_mlp.shape[1]
+    low[:, width:] = acc[:, width:].astype(jnp.bfloat16)
+    d_normed = acc[:, :width] + lax.dot_general(
+        low[:, width:], state_map[...], NT, preferred_element_type=jnp.float32
+    )
+    d_rows, d_gain = rms_back(after_mlp[...], gain[...], d_normed)
+    outs[1][...] = d_gain
+    d_rows = cot[...].astype(jnp.float32) + d_rows
+    outs[0][...] = d_rows
+    low[:, :width] = d_rows.astype(jnp.bfloat16)
+
+
+def finish_mlp_back(place, acc, args, outs, low, low_tail):
+    after_attn, gain, d_after_mlp = args
+    d_rows, d_gain = rms_back(after_attn[...], gain[...], acc[...])
+    outs[1][...] = d_gain
+    d_rows = d_after_mlp[...] + d_rows
+    outs[0][...] = d_rows
+    low[...] = d_rows.astype(jnp.bfloat16)
+
+
+def finish_attention_back(place, acc, args, outs, low, low_tail):
+    hidden, embeds, gain, d_after_attn, down_all, out_mine = args
+    half = hidden.shape[1]
+    bf16, f32 = jnp.bfloat16, jnp.float32
+    low[...] = acc[:, 2 * half :].astype(bf16)
+    inputs = (hidden, embeds)
+    squares = sum(jnp.sum(part[...] * part[...], axis=1, keepdims=True) for part in inputs)
+    inverse = lax.rsqrt(squares / (2 * half) + epsilon)
+    along = jnp.zeros_like(squares)
+    for i, part in enumerate(inputs):
+        cols = slice(i * half, (i + 1) * half)
+        grad = acc[:, cols] + lax.dot_general(
+            low[...], down_all[cols, :], NT, preferred_element_type=f32
+        )
+        acc[:, cols] = grad
+        along = along + jnp.sum(grad * gain[:, cols] * part[...], axis=1, keepdims=True)
+    along = along / (2 * half)
+    low_tail[:, :half] = out_mine[...]
+    for i, part in enumerate(inputs):
+        cols = slice(i * half, (i + 1) * half)
+        grad = acc[:, cols]
+        outs[0][:, cols] = jnp.sum(grad * part[...] * inverse, axis=0, keepdims=True)
+        d_rows = grad * gain[:, cols] * inverse - part[...] * inverse**3 * along
+        if i == 0:
+            d_rows = d_rows + d_after_attn[...]
+        low_tail[:, (i + 1) * half : (i + 2) * half] = d_rows.astype(bf16)
+
+
+def pack(parts, dtype):
+    flat = jnp.concatenate([part.reshape(-1).astype(dtype) for part in parts])
+    count = -(-flat.shape[0] // 2048) * 2048
+    return jnp.pad(flat, (0, count - flat.shape[0])).reshape(-1, 128)
+
+
+def unpack(packed, parts):
+    flat, at, found = packed.reshape(-1), 0, []
+    for part in parts:
+        found.append(flat[at : at + part.size].reshape(part.shape))
+        at += part.size
+    return found
 
 
 def shift_conv(values, kernel, bias, position):
@@ -704,6 +1369,8 @@
     group_rows = tok_rows * ctx_size
     start = tp_index * mine
 
+    sizes = (groups, ctx_size, tp_size)
+
     def own_rows(values):
         return lax.dynamic_slice_in_dim(values, start, mine, 0)
 
@@ -711,16 +1378,11 @@
         width = values.shape[axis] // plane_size
         return lax.dynamic_slice_in_dim(values, plane_index * width, width, axis)
 
+    width = hidden.shape[1]
     hidden_f = own_rows(hidden).astype(f32)
     embeds_f = own_rows(embeds).astype(f32)
     cot_low = own_rows(cotangent)
 
-    w_qkv = spread(query_key_value_weight, 2, 1)
-    w_o = spread(attention_output_weight, 0, 1)
-    w_gu = spread(gate_up_weight, 2, 1)
-    w_down = spread(down_weight, 0, 1)
-    w_zx = spread(mixer_gate_input_weight, 2, 1)
-    w_out = spread(mixer_output_weight, 0, 1)
     up_maps = own_part(adapter_up_maps, 2)
     w_step = own_part(step_size_weight, 1)
     taps, tap_bias = own_part(mixer_input_taps, 1), own_part(mixer_input_tap_bias)
@@ -730,27 +1392,23 @@
     rank = adapter_down_maps.shape[2]
     width_a = adapter_down_maps.shape[1]
     down_all = jnp.concatenate([adapter_down_maps[j] for j in range(3)], axis=1)
-    joined = jnp.concatenate([hidden_f, embeds_f], axis=1)
-    normed_a, norm_a_back = jax.vjp(rms_scale, joined, attention_norm_gain)
-    xa_mine = normed_a.astype(bf16)
-    mid_mine = matrix_product(xa_mine, down_all).astype(bf16)
-    segment_g, position_g, slot_g = layout(lengths[0], group_rows)
-    first = ctx_index * tok_rows + start
-    marks = jnp.stack(
-        [
-            lax.dynamic_slice_in_dim(segment_g, first, mine),
-            lax.dynamic_slice_in_dim(position_g, first, mine),
-        ],
-        axis=1,
-    ).astype(bf16)
-    marks = jnp.pad(marks, ((0, 0), (0, 126)))
-    gathered = gather_rows(jnp.concatenate([xa_mine, mid_mine, marks], axis=1))
+    gathered, w_qkv, w_o = opening(
+        sizes,
+        1,
+        hidden,
+        embeds,
+        lengths,
+        attention_norm_gain,
+        down_all,
+        [(query_key_value_weight, 2, 1), (attention_output_weight, 0, 1)],
+    )
     xa = gathered[:, :width_a]
     mid = gathered[:, width_a : width_a + 3 * rank]
     segment = gathered[:, width_a + 3 * rank].astype(jnp.int32).reshape(groups, group_rows)
     position = gathered[:, width_a + 3 * rank + 1].astype(jnp.int32).reshape(groups, group_rows)
     position_flat = position.reshape(-1)
-    cot = gather_rows(cot_low)
+    late_cot, _ = lax.optimization_barrier((cot_low, w_o))
+    cot = lax.all_gather(late_cot, EVERY, axis=0, tiled=True)
     proj = [
         (
             matrix_product(xa, w_qkv[j])
@@ -763,17 +1421,35 @@
         *[piece.astype(f32).reshape(groups, group_rows, AHD) for piece in proj],
     )
     ao_low = ao.astype(bf16).reshape(groups * group_rows, AHD)
-    after_attn = hidden_f + scatter_rows(matrix_product(ao_low, w_o).astype(bf16))
-
-    normed_m, norm_m_back = jax.vjp(rms_scale, after_attn, feedforward_norm_gain)
-    xm = gather_rows(normed_m.astype(bf16))
+
+    gain_m = feedforward_norm_gain.reshape(1, -1)
+    xm, after_attn, w_gu, w_down = exchange(
+        sizes,
+        2,
+        [(ao_low, w_o, None, False)],
+        None,
+        finish_forward,
+        [hidden_f, gain_m],
+        [hidden_f.shape],
+        width,
+        [(gate_up_weight, 2, 1), (down_weight, 0, 1)],
+    )
     gate_pre, up_pre = matrix_product(xm, w_gu[0]), matrix_product(xm, w_gu[1])
     activated, act_back = jax.vjp(gated_gelu, gate_pre, up_pre)
     hid_low = activated.astype(bf16)
-    after_mlp = after_attn + scatter_rows(matrix_product(hid_low, w_down).astype(bf16))
-
-    normed_n, norm_n_back = jax.vjp(rms_scale, after_mlp, mixer_norm_gain)
-    xn = gather_rows(normed_n.astype(bf16))
+
+    gain_n = mixer_norm_gain.reshape(1, -1)
+    xn, after_mlp, w_zx, w_out = exchange(
+        sizes,
+        3,
+        [(hid_low, w_down, None, False)],
+        None,
+        finish_forward,
+        [after_attn, gain_n],
+        [hidden_f.shape],
+        width,
+        [(mixer_gate_input_weight, 2, 1), (mixer_output_weight, 0, 1)],
+    )
     gate_z = matrix_product(xn, w_zx[0])
     inner_x = matrix_product(xn, w_zx[1]).astype(bf16)
     step_raw = matrix_product(xn, w_step).astype(bf16)
@@ -800,14 +1476,14 @@
     gated = y * silu_z
     d_yn = matrix_product_transposed(cot, w_out)
     gain_part = d_yn * gate_gain
-    sums = lax.psum(
-        jnp.stack([jnp.sum(gated * gated, axis=1), jnp.sum(gain_part * gated, axis=1)]), EVERY
-    )
+    sums = jnp.stack([jnp.sum(gated * gated, axis=1), jnp.sum(gain_part * gated, axis=1)])
+    sums = sum_small(sizes, 4, sums.reshape(-1, 128)).reshape(2, -1)
     inverse = lax.rsqrt(sums[0] / INNER + epsilon)[:, None]
     cross = (sums[1] / INNER)[:, None]
     yn_low = (gated * inverse * gate_gain).astype(bf16)
-    out_mine = after_mlp + scatter_rows(matrix_product(yn_low, w_out).astype(bf16))
-    result = lax.all_gather(out_mine.astype(bf16), "tp", axis=0, tiled=True)
+    out_part = matrix_product(yn_low, w_out).astype(bf16)
+    out_mine = lax.psum_scatter(out_part, EVERY, scatter_dimension=0, tiled=True)
+    out_mine = (after_mlp + out_mine.astype(f32)).astype(bf16)
 
     grad_w_out = outer_product_sum(yn_low, cot)
     grad_g_gate = jnp.sum(d_yn * gated * inverse, axis=0)
@@ -827,105 +1503,142 @@
     ) = scan_back(d_y.astype(f32))
     d_xs, d_step = d_xs.astype(bf16), d_step.astype(bf16)
     d_bc_part, grad_conv_bc, grad_conv_bc_bias = bc_conv_back(d_bc_post)
-    dxn_part = (
-        matrix_product_transposed(d_z, w_zx[0])
-        + matrix_product_transposed(d_xs, w_zx[1])
-        + matrix_product_transposed(d_step, w_step)
-    )
-    sent = scatter_rows(jnp.concatenate([dxn_part, d_bc_part], axis=1).astype(bf16))
-    width = hidden.shape[1]
-    d_bc_mine = sent[:, width:].astype(bf16)
-    dxn_mine = sent[:, :width] + matrix_product_transposed(d_bc_mine, state_map_weight)
-    grad_w_zx = jnp.stack([outer_product_sum(xn, d_z), outer_product_sum(xn, d_xs)])
+    grad_w_zx = jnp.stack(
+        [outer_product_sum(xn, d_z).astype(bf16), outer_product_sum(xn, d_xs).astype(bf16)]
+    )
     grad_w_dt = outer_product_sum(xn, d_step)
-    d_norm_n, grad_g_mamba = norm_n_back(dxn_mine)
-    d_after_mlp = cot_low.astype(f32) + d_norm_n
-
-    gathered = gather_rows(jnp.concatenate([d_after_mlp.astype(bf16), d_bc_mine], axis=1))
+    lanes = ((0, 0), (0, 128 - d_step.shape[1]))
+    gathered, d_after_mlp, grad_g_mamba, grad_w_zx, grad_w_out = exchange(
+        sizes,
+        5,
+        [
+            (d_z, w_zx, 0, True),
+            (d_xs, w_zx, 1, True),
+            (jnp.pad(d_step, lanes), jnp.pad(w_step, lanes), None, True),
+        ],
+        d_bc_part.astype(bf16),
+        finish_mixer_back,
+        [after_mlp, gain_n, cot_low, state_map_weight],
+        [hidden_f.shape, gain_n.shape],
+        width + d_bc_part.shape[1],
+        [(grad_w_zx, 1, 2), (grad_w_out.astype(bf16), 1, 0)],
+    )
+
     d_mlp, d_bc = gathered[:, :width], gathered[:, width:]
     grad_w_bc = outer_product_sum(xn, d_bc)
     grad_w_down = outer_product_sum(hid_low, d_mlp)
     d_gate, d_up = act_back(matrix_product_transposed(d_mlp, w_down))
     d_gate, d_up = d_gate.astype(bf16), d_up.astype(bf16)
-    d_xm = scatter_rows(
-        (
-            matrix_product_transposed(d_gate, w_gu[0]) + matrix_product_transposed(d_up, w_gu[1])
-        ).astype(bf16)
-    )
-    grad_w_gu = jnp.stack([outer_product_sum(xm, d_gate), outer_product_sum(xm, d_up)])
-    d_norm_m, grad_g_mlp = norm_m_back(d_xm)
-    d_after_attn = d_after_mlp + d_norm_m
-
-    d_attn = gather_rows(d_after_attn.astype(bf16))
+    grad_w_gu = jnp.stack(
+        [outer_product_sum(xm, d_gate).astype(bf16), outer_product_sum(xm, d_up).astype(bf16)]
+    )
+
+    d_attn, d_after_attn, grad_g_mlp, grad_w_gu, grad_w_down = exchange(
+        sizes,
+        6,
+        [(d_gate, w_gu, 0, True), (d_up, w_gu, 1, True)],
+        None,
+        finish_mlp_back,
+        [after_attn, gain_m, d_after_mlp],
+        [hidden_f.shape, gain_m.shape],
+        width,
+        [(grad_w_gu, 1, 2), (grad_w_down.astype(bf16), 1, 0)],
+    )
     grad_w_o = outer_product_sum(ao_low, d_attn)
     d_ao = matrix_product_transposed(d_attn, w_o).astype(bf16)
     d_proj = [
         piece.reshape(groups * group_rows, AHD).astype(bf16)
         for piece in attend_back(d_ao.astype(f32).reshape(groups, group_rows, AHD))
     ]
-    dxa_part = sum(matrix_product_transposed(d_proj[j], w_qkv[j]) for j in range(3))
     dmid_part = jnp.concatenate(
-        [matrix_product_transposed(d_proj[j], up_maps[j]) for j in range(3)], axis=1
-    )
-    sent = scatter_rows(jnp.concatenate([dxa_part, dmid_part], axis=1).astype(bf16))
-    dmid_mine = sent[:, width_a:].astype(bf16)
-    dxa_mine = sent[:, :width_a] + matrix_product_transposed(dmid_mine, down_all)
-    dmid = gather_rows(dmid_mine)
+        [matrix_product_transposed(d_proj[j], up_maps[j]).astype(bf16) for j in range(3)], axis=1
+    )
+    grad_w_qkv = jnp.stack([outer_product_sum(xa, d_proj[j]).astype(bf16) for j in range(3)])
+    adapter_up_gradient = jnp.stack(
+        [outer_product_sum(mid[:, j * rank : (j + 1) * rank], d_proj[j]) for j in range(3)]
+    )
+    shares = [
+        adapter_up_gradient,
+        grad_w_dt,
+        grad_conv_x,
+        grad_conv_x_bias,
+        grad_g_gate,
+        grad_dt_bias,
+        grad_a_log,
+        grad_d_skip,
+    ]
+    joins = (2, 1, 1, 0, 0, 0, 0, 0)
+    dmid, back, grad_g_attn, grad_w_qkv, grad_w_o, shared = exchange(
+        sizes,
+        7,
+        [(d_proj[j], w_qkv, j, True) for j in range(3)],
+        dmid_part,
+        finish_attention_back,
+        [
+            hidden_f,
+            embeds_f,
+            attention_norm_gain.reshape(1, -1),
+            d_after_attn,
+            down_all,
+            out_mine,
+        ],
+        [(1, width_a)],
+        3 * rank,
+        [(grad_w_qkv, 1, 2), (grad_w_o.astype(bf16), 1, 0), (pack(shares, bf16), None, 0)],
+        early_share=100,
+        tail=3 * width,
+    )
     adapter_down_gradient = jnp.stack(
         [outer_product_sum(xa, dmid[:, j * rank : (j + 1) * rank]) for j in range(3)]
     )
-    grad_w_qkv = jnp.stack([outer_product_sum(xa, d_proj[j]) for j in range(3)])
-    adapter_up_gradient = jnp.stack(
-        [outer_product_sum(mid[:, j * rank : (j + 1) * rank], d_proj[j]) for j in range(3)]
-    )
-    d_joined, grad_g_attn = norm_a_back(dxa_mine)
-    back = jnp.concatenate(
-        [d_after_attn + d_joined[:, :width], d_joined[:, width:]], axis=1
-    ).astype(bf16)
-    back = lax.all_gather(back, "tp", axis=0, tiled=True).astype(f32)
-    d_hidden, d_embeds = back[:, :width], back[:, width:]
-
-    def home(grad, split, join):
-        return spread(grad.astype(bf16), split, join).astype(f32)
-
-    grad_w_qkv = home(grad_w_qkv, 1, 2)
-    grad_w_o = home(grad_w_o, 1, 0)
-    grad_w_gu = home(grad_w_gu, 1, 2)
-    grad_w_down = home(grad_w_down, 1, 0)
-    grad_w_zx = home(grad_w_zx, 1, 2)
-    grad_w_out = home(grad_w_out, 1, 0)
-
-    def whole(part, axis):
-        return lax.all_gather(part.astype(bf16), PLANE, axis=axis, tiled=True).astype(f32)
-
-    def total(part):
-        return lax.psum(part, EVERY)
+    result = back[:, :width]
+    d_hidden = back[:, width : 2 * width].astype(f32)
+    d_embeds = back[:, 2 * width :].astype(f32)
+    (
+        adapter_up_gradient,
+        grad_w_dt,
+        grad_conv_x,
+        grad_conv_x_bias,
+        grad_g_gate,
+        grad_dt_bias,
+        grad_a_log,
+        grad_d_skip,
+    ) = [
+        jnp.concatenate(parts, axis=join).astype(f32)
+        for parts, join in zip(
+            zip(*[unpack(shared[i], shares) for i in range(plane_size)]), joins
+        )
+    ]
+    sums = [grad_g_attn, grad_g_mlp, grad_g_mamba, grad_conv_bc, grad_conv_bc_bias]
+    grad_g_attn, grad_g_mlp, grad_g_mamba, grad_conv_bc, grad_conv_bc_bias = unpack(
+        sum_small(sizes, 8, pack(sums, f32)), sums
+    )
 
     return (
         result,
         d_hidden,
         d_embeds,
-        total(grad_g_attn),
+        grad_g_attn[0],
         adapter_down_gradient,
-        grad_w_qkv,
-        whole(adapter_up_gradient, 2),
-        grad_w_o,
-        total(grad_g_mlp),
-        grad_w_gu,
-        grad_w_down,
-        total(grad_g_mamba),
-        grad_w_zx,
+        grad_w_qkv.astype(f32),
+        adapter_up_gradient,
+        grad_w_o.astype(f32),
+        grad_g_mlp[0],
+        grad_w_gu.astype(f32),
+        grad_w_down.astype(f32),
+        grad_g_mamba[0],
+        grad_w_zx.astype(f32),
         grad_w_bc,
-        whole(grad_w_dt, 1),
-        whole(grad_conv_x, 1),
-        whole(grad_conv_x_bias, 0),
-        total(grad_conv_bc),
-        total(grad_conv_bc_bias),
-        whole(grad_dt_bias, 0),
-        whole(grad_a_log, 0),
-        whole(grad_d_skip, 0),
-        whole(grad_g_gate, 0),
-        grad_w_out,
+        grad_w_dt,
+        grad_conv_x,
+        grad_conv_x_bias,
+        grad_conv_bc,
+        grad_conv_bc_bias,
+        grad_dt_bias,
+        grad_a_log,
+        grad_d_skip,
+        grad_g_gate,
+        grad_w_out.astype(f32),
     )
 
 
@@ -958,7 +1671,7 @@
         P("tp", ("fsdp", "ctx")),
     )
     devices = mesh.shape["fsdp"] * mesh.shape["ctx"] * mesh.shape["tp"]
-    one_head_each = devices == AHEADS and MHEADS % devices == 0
+    one_head_each = devices == AHEADS and mesh.shape["ctx"] == 2 and mesh.shape["tp"] == 4
     return jax.shard_map(
         per_device_split if one_head_each else per_device,
         mesh=mesh,

time: 2080 us -> 1340 us (0.64)
  waiting for transfers between devices: 1160 us -> 66.5 us
  Pallas kernels: 0 us -> 916 us
  blocking collectives: 299 us -> 0 us
  matrix products: 277 us -> 178 us
  local copies, waits for them, and re-layouts: 172 us -> 79.7 us
  starting transfers between devices: 57.9 us -> 0.29 us
    pallas_call x0 -> x8, Pallas kernels: none -> 916 us  [the longest x5 738 us: exchange(): pl.pallas_call(kernel, out_shape=out_shape, in_specs=in_specs, out_specs=...]
    reduce_scatter x6 -> x1, waiting for transfers between devices: 574 us -> 66.5 us  [per_device_split(): lax.psum_scatter(out_part, EVERY, scatter_dimension=0, tiled=True)]
    all_to_all x12 -> x0, waiting for transfers between devices: 391 us -> none  [spread(): lax.all_to_all(weight, PLANE, split_axis=split, concat_axis=join, tiled=T...]
    all_gather x8 -> x1, waiting for transfers between devices: 193 us -> 0.01 us  [per_device_split(): cot = lax.all_gather(late_cot, EVERY, axis=0, tiled=True)]
    all_gather x6 -> x0, blocking collectives: 139 us -> none  [the longest x5 131 us: whole(): lax.all_gather(part.astype(bf16), PLANE, axis=axis, tiled=True).astype(f32)]
    dot_general x16 -> x6, matrix products: 102 us -> 16.3 us  [matrix_product_transposed(): lax.dot_general(left, right, (((1,), (1,)), ((), ())), preferred_element_...]
    unnamed x1 -> x0, blocking collectives: 80.7 us -> none
    psum x2 -> x0, blocking collectives: 79.6 us -> none  [the longest x1 39.8 us: per_device_split(): lax.psum(jnp.stack([jnp.sum(gated * gated, axis=1), jnp.sum(gain_part * g...]
  transfers between devices with their start and end apart: 26 -> 2, of which waited for: 20 -> 1; matrix products, arithmetic and copies ran while one was open for 14% -> 11% of each run, Pallas kernels for 0% -> 21%
where the time goes in v2:
time: 1340 us; the launch traced here: 1330 us
  Pallas kernels  916 us (68%)
  matrix products  178 us (13%)
  local copies, waits for them, and re-layouts  79.7 us (6%)
  other arithmetic  74.7 us (6%)
  waiting for transfers between devices  66.5 us (5%)
  between operations  16.7 us (1%)
    pallas_call x5, Pallas kernels, exchange(): pl.pallas_call(kernel, out_shape=out_shape, in_specs=in_specs, out_specs=...  738 us
    pallas_call x1, Pallas kernels, opening(): pl.pallas_call(kernel, out_shape=[S((groups, ctx, tp // 2, 2, rows, width...  146 us
    dot_general x18, matrix products, outer_product_sum(): lax.dot_general(left, right, (((0,), (0,)), ((), ())), preferred_element_...  76.8 us
    reduce_scatter x1, waiting for transfers between devices, per_device_split(): lax.psum_scatter(out_part, EVERY, scatter_dimension=0, tiled=True)  66.5 us
    dot_general x13, matrix products, matrix_product(): return jnp.dot(left, right, preferred_element_type=jnp.float32)  52.7 us
    pallas_call x2, Pallas kernels, sum_small(): pl.pallas_call(kernel, out_shape=jax.ShapeDtypeStruct(shape, f32), in_spe...  31.5 us
  transfers between devices with their start and end apart: 2, of which 1 were waited for; matrix products, arithmetic and copies ran while one was open for 11% of the time, Pallas kernels for 21%

profile of v2, /device:TPU:0, one launch (start us, length us, event | category | flops | bytes accessed | tf_op | source)
XLA Modules:
  0.0 1332.0 jit_solution(6363260161315315360)
XLA Ops:
  7.3 3.1 slice_bitcast_fusion.2
  10.4 3.3 pad_maximum_fusion.1.refs_4_.refs_9_
  15.5 146.4 %opening_1.1 = (bf16[4,2,2,2,48,4608]{5,4,3,2,1,0:T(8,128)(2,1)}, bf16[3,4096,128]{2,1,0:T(8,128)(2,1)}, bf16[128,2048]{1,0:T(8,128)(2,1)}) custom-call(bf16[192,2048]{1,0:T(8,128)(2,1)} %refs_0_.1, bf16[192,2048]{1,0:T(8,128)(2,1)} %refs_1_.1, s32[1,3]{1,0:T(1,128)} %refs_2_.1, f32[1,4096]{1,0:T(1,128)} %bitcast.373, ...), custom_call_target="tpu_custom_call" | custom-call | tf_op jit(solution)/shard_map/opening_1/pallas_call | solution.py:1131
  162.2 6.9 fusion.104
  169.1 2.1 copy-done.65
  171.2 4.8 fusion.106
  183.6 6.8 fusion.102
  191.7 3.8 fusion.121
  199.5 166.4 %exchange_2.1 = (bf16[4,2,2,2,48,2048]{5,4,3,2,1,0:T(8,128)(2,1)}, f32[48,2048]{1,0:T(8,128)}, bf16[2,2048,256]{2,1,0:T(8,128)(2,1)}, bf16[256,2048]{1,0:T(8,128)(2,1)}) custom-call(bf16[4,2,2,2,48,128]{5,4,3,2,1,0:T(8,128)(2,1)} %bitcast.312, bf16[128,2048]{1,0:T(8,128)(2,1)} %get-tuple-element.53.refs_1_, f32[48,2048]{1,0:T(8,128)} %get-tuple-element.255.refs_2_.refs_5_, ...), custom_call_target="tpu_custom_call" | custom-call | tf_op jit(solution)/shard_map/exchange_2/pallas_call | solution.py:1057
  366.0 5.1 fusion.100
  371.5 3.6 multiply_convert_fusion.1
  375.1 113.2 %exchange_3.1 = (bf16[4,2,2,2,48,2048]{5,4,3,2,1,0:T(8,128)(2,1)}, f32[48,2048]{1,0:T(8,128)}, bf16[2,2048,128]{2,1,0:T(8,128)(2,1)}, bf16[128,2048]{1,0:T(8,128)(2,1)}) custom-call(bf16[4,2,2,2,48,256]{5,4,3,2,1,0:T(8,128)(2,1)} %bitcast.341, bf16[256,2048]{1,0:T(8,128)(2,1)} %get-tuple-element.58.refs_1_, f32[48,2048]{1,0:T(8,128)} %get-tuple-element.59.refs_2_.refs_3_, ...), custom_call_target="tpu_custom_call" | custom-call | tf_op jit(solution)/shard_map/exchange_3/pallas_call | solution.py:1057
  489.1 4.7 fusion.24
  498.5 2.4 compare_and_fusion
  500.9 2.9 copy.124
  507.8 5.3 compare_select_fusion.2
  516.0 2.6 fusion.61
  522.2 4.5 fusion.74
  526.7 3.3 copy.174
  530.0 3.2 reshape.595
  537.7 5.5 fusion.150
  543.2 6.1 multiply_reduce_fusion.13
  551.3 16.7 %sum_small_4.1 = f32[24,128]{1,0:T(8,128)} custom-call(f32[24,128]{1,0:T(8,128)} %reshape.525.x), custom_call_target="tpu_custom_call" | custom-call | tf_op jit(solution)/shard_map/sum_small_4/pallas_call | solution.py:1185
  569.5 3.5 multiply_reduce_fusion.5
  573.0 3.1 reshape.593
  577.4 6.9 fusion.14
  584.3 2.0 fusion.216
  586.3 3.0 fusion.217
  589.3 2.7 copy.132
  592.0 5.9 multiply_reduce_fusion.11
  597.9 2.4 copy.175
  602.1 5.6 fusion.41
  610.8 2.7 fusion.42
  613.5 2.4 multiply_reduce_fusion.4
  616.0 3.1 multiply_multiply_fusion.2
  624.8 2.3 pad_maximum_fusion.5.refs_10_
  627.0 3.3 fusion.51
  630.4 4.7 convolution_convert_fusion.11.refs_11_
  635.0 124.3 %exchange_5.1 = (bf16[4,2,2,2,48,2304]{5,4,3,2,1,0:T(8,128)(2,1)}, f32[48,2048]{1,0:T(8,128)}, f32[1,2048]{1,0:T(1,128)}, bf16[2,256,1024]{2,1,0:T(8,128)(2,1)}, bf16[1024,256]{1,0:T(8,128)(2,1)}) custom-call(bf16[4,2,2,2,48,128]{5,4,3,2,1,0:T(8,128)(2,1)} %bitcast.338, bf16[4,2,2,2,48,128]{5,4,3,2,1,0:T(8,128)(2,1)} %bitcast.333, ...), custom_call_target="tpu_custom_call" | custom-call | tf_op jit(solution)/shard_map/exchange_5/pallas_call | solution.py:1057
  759.4 6.0 fusion.15.refs_7_
  765.4 4.6 multiply_convert_fusion
  770.0 2.0 fusion.19
  772.0 2.0 fusion.20
  775.5 154.7 %exchange_6.1 = (bf16[4,2,2,2,48,2048]{5,4,3,2,1,0:T(8,128)(2,1)}, f32[48,2048]{1,0:T(8,128)}, f32[1,2048]{1,0:T(1,128)}, bf16[2,256,2048]{2,1,0:T(8,128)(2,1)}, bf16[2048,256]{1,0:T(8,128)(2,1)}) custom-call(bf16[4,2,2,2,48,256]{5,4,3,2,1,0:T(8,128)(2,1)} %bitcast.340, bf16[4,2,2,2,48,256]{5,4,3,2,1,0:T(8,128)(2,1)} %bitcast.339, ...), custom_call_target="tpu_custom_call" | custom-call | tf_op jit(solution)/shard_map/exchange_6/pallas_call | solution.py:1057
  930.2 4.8 convolution_convert_fusion.14
  941.2 4.6 convolution_convert_fusion
  947.6 3.5 fusion.130
  955.5 4.3 convert_element_type.418
  969.7 4.9 convolution_convert_fusion.7.refs_12_
  974.7 8.6 fusion.10
  983.4 3.5 fusion.11
  986.9 3.5 fusion.12
  990.3 2.2 pad_maximum_fusion.2.refs_11_
  992.5 4.4 fusion.134
  996.9 66.5 %reduce-scatter.2.cloned.1.call-done = bf16[48,2048]{1,0:T(8,128)(2,1)} async-done(((bf16[1536,2048]{1,0:T(8,128)(2,1)}), bf16[48,2048]{1,0:T(8,128)(2,1)}) %reduce-scatter.2.cloned.1.call-update) | async-done | bytes 196624 | tf_op jit(solution)/shard_map/reduce_scatter | solution.py:1485
  1065.0 179.4 %exchange_7.1 = (bf16[4,2,2,2,48,384]{5,4,3,2,1,0:T(8,128)(2,1)}, bf16[2,2,48,6144]{3,2,1,0:T(8,128)(2,1)}, f32[1,4096]{1,0:T(1,128)}, bf16[3,512,1024]{2,1,0:T(...) custom-call(bf16[4,2,2,2,48,128]{5,4,3,2,1,0:T(8,128)(2,1)} %bitcast.317, ...), custom_call_target="tpu_custom_call" | custom-call | tf_op jit(solution)/shard_map/exchange_7/pallas_call | solution.py:1057
  1248.3 9.6 convolution_bitcast_fusion.2
  1257.9 9.5 convolution_bitcast_fusion.1
  1267.5 5.0 convolution_bitcast_fusion
  1273.2 14.8 %sum_small_8.1 = f32[80,128]{1,0:T(8,128)} custom-call(f32[80,128]{1,0:T(8,128)} %pad_bitcast_fusion.1.x), custom_call_target="tpu_custom_call" | custom-call | tf_op jit(solution)/shard_map/sum_small_8/pallas_call | solution.py:1185
  1312.5 3.5 convert_element_type.415
  1316.6 2.2 slice_convert_fusion
  1318.8 2.9 convert_element_type.417
  1321.7 3.1 pad_maximum_fusion
  (485 shorter events, 105.3 us)
Async XLA Ops:
  7.2 168.8 %copy-start = (bf16[3,128,1024]{2,1,0:T(8,128)(2,1)S(1)}, bf16[3,128,1024]{2,1,0:T(8,128)(2,1)}, u32[]{:S(2)}) copy-start(bf16[3,128,1024]{2,1,0:T(8,128)(2,1)} %param.32) | copy-start | bytes 2359300
  7.2 536.0 %all-gather.2.cloned.1.call-start = ((), (), s32[]{:S(2)}) async-start(), calls=%async_computation.1 | async-start | bytes 6488064 | tf_op jit(solution)/shard_map/all_gather | solution.py:1411
  162.0 901.4 %reduce-scatter.2.cloned.1.call-start = ((), (), s32[]{:S(2)}) async-start(), calls=%async_computation.2 | async-start | bytes 6488064 | tf_op jit(solution)/shard_map/reduce_scatter | solution.py:1485
  162.2 8.9 copy-start.65
  183.5 8.1 copy-start.114
  183.6 11.9 copy-start.45
  183.6 8.1 copy-start.71
  366.0 5.1 copy-start.27
  366.0 5.5 copy-start.123
  498.5 9.1 copy-start.119
  498.5 9.1 copy-start.104
  498.5 15.5 %slice-start = ((s8[6291456]{0:T(1024)(128)(4,1)}), s8[2097152]{0:T(1024)(128)(4,1)S(1)}, s32[]{:S(2)}) async-start(s8[6291456]{0:T(1024)(128)(4,1)} %bitcast.293), calls=%async_computation.3 | async-start | bytes 4194304
  507.7 5.4 copy-start.125
  507.7 8.3 copy-start.80
  507.7 8.3 copy-start.82
  507.7 8.3 copy-start.84
  507.7 8.3 copy-start.86
  507.7 5.3 copy-start.46
  507.7 5.3 copy-start.68
  507.7 6.3 slice-start.1
  507.8 6.3 copy-start.36
  513.0 7.7 copy-start.77
  514.0 6.7 copy-start.129
  526.7 7.8 copy-start.28
  526.7 8.7 copy-start.75
  543.2 26.3 %copy-start.6 = (f32[1536,128]{1,0:T(8,128)S(1)}, f32[1536,128]{1,0:T(8,128)}, u32[]{:S(2)}) copy-start(f32[1536,128]{1,0:T(8,128)} %copy-done.5) | copy-start | bytes 2359300
  577.4 6.9 copy-start.54
  577.4 6.9 copy-start.8
  586.3 5.7 copy-start.43
  602.1 5.6 copy-start.20
  602.1 5.6 copy-start.21
  602.1 5.6 copy-start.24
  602.1 5.6 copy-start.53
  602.1 8.6 slice-start.2
  616.0 5.1 copy-start.66
  759.4 6.0 copy-start.39
  759.4 6.0 copy-start.122
  759.4 10.6 slice-start.17
  941.2 5.5 copy-start.117
  951.3 23.3 %copy-start.14 = (bf16[4,384,128]{2,1,0:T(8,128)(2,1)}, bf16[4,384,128]{2,1,0:T(8,128)(2,1)S(1)}, u32[]{:S(2)}) copy-start(bf16[4,384,128]{2,1,0:T(8,128)(2,1)S(1)} %add_convert_fusion.1) | copy-start | bytes 1179652
  952.5 30.8 %copy-start.15 = (bf16[4,384,128]{2,1,0:T(8,128)(2,1)}, bf16[4,384,128]{2,1,0:T(8,128)(2,1)S(1)}, u32[]{:S(2)}) copy-start(bf16[4,384,128]{2,1,0:T(8,128)(2,1)S(1)} %add_convert_fusion) | copy-start | bytes 1179652
  953.0 33.8 %copy-start.16 = (bf16[4,384,128]{2,1,0:T(8,128)(2,1)}, bf16[4,384,128]{2,1,0:T(8,128)(2,1)S(1)}, u32[]{:S(2)}) copy-start(bf16[4,384,128]{2,1,0:T(8,128)(2,1)S(1)} %convolution_convert_fusion.19) | copy-start | bytes 1179652
  963.0 5.2 copy-start.120
  963.0 5.2 copy-start.121
  963.0 5.3 copy-start.105
  963.0 5.3 copy-start.106
  963.0 5.3 copy-start.107
  963.0 6.8 copy-start.13
  969.7 13.6 %slice-start.8 = ((s8[14155776]{0:T(1024)(128)(4,1)}), s8[4194304]{0:T(1024)(128)(4,1)S(1)}, s32[]{:S(2)}) async-start(s8[14155776]{0:T(1024)(128)(4,1)} %bitcast.366), calls=%async_computation.11 | async-start | bytes 8388608
  969.7 13.6 %slice-start.9 = ((s8[14155776]{0:T(1024)(128)(4,1)}), s8[4194304]{0:T(1024)(128)(4,1)S(1)}, s32[]{:S(2)}) async-start(s8[14155776]{0:T(1024)(128)(4,1)} %bitcast.366), calls=%async_computation.12 | async-start | bytes 8388608
  974.7 8.6 slice-start.10
  974.7 8.6 slice-start.11
  983.3 9.2 slice-start.6
  986.9 5.7 slice-start.7
  992.5 70.9 %copy-start.32 = (f32[48,2048]{1,0:T(8,128)S(1)}, f32[48,2048]{1,0:T(8,128)}, u32[]{:S(2)}) copy-start(f32[48,2048]{1,0:T(8,128)} %get-tuple-element.63.refs_6_) | copy-start | bytes 1179652
  1248.3 19.2 %slice-start.12 = ((s8[14155776]{0:T(1024)(128)(4,1)}), s8[4194304]{0:T(1024)(128)(4,1)S(1)}, s32[]{:S(2)}) async-start(s8[14155776]{0:T(1024)(128)(4,1)} %bitcast.370), calls=%async_computation.15 | async-start | bytes 8388608
  1248.3 19.2 %slice-start.13 = ((s8[14155776]{0:T(1024)(128)(4,1)}), s8[4194304]{0:T(1024)(128)(4,1)S(1)}, s32[]{:S(2)}) async-start(s8[14155776]{0:T(1024)(128)(4,1)} %bitcast.370), calls=%async_computation.16 | async-start | bytes 8388608
  1257.9 9.6 slice-start.14
  1257.9 9.6 slice-start.15
  1267.5 24.3 %copy-start.113 = (bf16[1024]{0:T(1024)(128)(2,1)S(1)}, bf16[1024]{0:T(1024)(128)(2,1)}, u32[]{:S(2)}) copy-start(bf16[1024]{0:T(1024)(128)(2,1)} %custom-call) | copy-start | bytes 6148
  1267.5 29.2 %copy-start.112 = (bf16[1024]{0:T(1024)(128)(2,1)S(1)}, bf16[1024]{0:T(1024)(128)(2,1)}, u32[]{:S(2)}) copy-start(bf16[1024]{0:T(1024)(128)(2,1)} %custom-call.1) | copy-start | bytes 6148
  1316.6 5.1 copy-start.29
  1316.6 5.1 copy-start.30
  1316.6 5.1 copy-start.31
  (90 other events, 239.3 us)
Sparse Core Ops, SparseCore 0:
  162.1 111.1 all-gather.1
  947.0 116.3 reduce-scatter.1

commit v3 on v2

--- a/solution.py
+++ b/solution.py
@@ -1,3 +1,5 @@
+import functools
+
 import jax
 import jax.numpy as jnp
 from jax import lax
@@ -600,6 +602,8 @@
 IN_HBM = pl.BlockSpec(memory_space=pltpu.HBM)
 IN_SMEM = pl.BlockSpec(memory_space=pltpu.SMEM)
 DMA = pltpu.SemaphoreType.DMA
+GATHER_SHARES = (4, 4, 4, 4)
+SUM_SHARES = (4, 4, 4, 4)
 
 
 class Place:
@@ -664,7 +668,7 @@
         src, dst = self.sources[i], self.targets[i]
         n = self.place.plane
         if split is None:
-            return src, dst.at[origin]
+            return src, cut(dst, join, origin, src.shape[join])
         return (
             cut(src, split, to, src.shape[split] // n),
             cut(dst, join, origin, dst.shape[join] // n),
@@ -716,12 +720,10 @@
     for array, split, join in moves:
         shape = list(array.shape)
         part = list(array.shape)
-        if split is None:
-            shape = [plane] + shape
-        else:
+        if split is not None:
             part[split] //= plane
             shape[split] //= plane
-            shape[join] *= plane
+        shape[join] *= plane
         outs.append(jax.ShapeDtypeStruct(tuple(shape), array.dtype))
         scratch.append(pltpu.VMEM(tuple(part), array.dtype))
     n = len(moves)
@@ -730,149 +732,241 @@
     return outs, scratch
 
 
-def spans(width, extra, count):
-    step = width // count
-    found = [(i * step, step) for i in range(count)]
-    if extra:
-        found.append((width, extra))
-    return found
-
-
-def gather_stage(place, x, o, pieces, sems, between):
-    zs, zr, s2, r2, s3, r3, s4, r4, own_sem = sems
-    g, c, y, k = place.g, place.c, place.y, place.k
-    n = len(pieces)
-    lines = place.groups - 1
-    own = pltpu.make_async_copy(x, o.at[g, c, y, k], own_sem)
-    own.start()
-    first = []
-    for q, (at, width) in enumerate(pieces):
-        cols = pl.ds(at, width)
-        for d in range(lines):
+class Gather:
+    def __init__(self, place, x, o, pieces, sems):
+        self.place, self.x, self.o, self.pieces, self.sems = place, x, o, pieces, sems
+        self.n = len(pieces)
+        self.first, self.second = [], [None] * self.n
+        self.third, self.fourth = [None] * self.n, [None] * self.n
+
+    def line_copy(self, q, d, owner):
+        place, cols = self.place, pl.ds(*self.pieces[q])
+        return remote(
+            self.x.at[:, cols],
+            self.o.at[owner, place.c, place.y, place.k, :, cols],
+            self.sems[0].at[q, d],
+            self.sems[1].at[q, d],
+            place.line[d],
+        )
+
+    def begin(self):
+        place = self.place
+        own_at = self.o.at[place.g, place.c, place.y, place.k]
+        own = pltpu.make_async_copy(self.x, own_at, self.sems[8])
+        own.start()
+        for q in range(self.n):
+            for d in range(place.groups - 1):
+                copy = self.line_copy(q, d, place.g)
+                copy.start()
+                self.first.append(copy)
+        own.wait()
+
+    def to_side(self, q):
+        place = self.place
+        for d in range(place.groups - 1):
+            source = lax.rem(place.g + place.groups - d - 1, place.groups)
+            self.line_copy(q, d, source).wait_recv()
+        part = self.o.at[:, place.c, place.y, place.k, :, pl.ds(*self.pieces[q])]
+        device = place.side_y if q % 2 == 0 else place.side_x
+        self.second[q] = remote(part, part, self.sems[2].at[q], self.sems[3].at[q], device)
+        self.second[q].start()
+
+    def to_other_side(self, q):
+        place, cols = self.place, pl.ds(*self.pieces[q])
+        self.second[q].wait_recv()
+        if q % 2 == 0:
+            part, device = self.o.at[:, place.c, :, place.k, :, cols], place.side_x
+        else:
+            part, device = self.o.at[:, :, place.y, place.k, :, cols], place.side_y
+        self.third[q] = remote(part, part, self.sems[4].at[q], self.sems[5].at[q], device)
+        self.third[q].start()
+
+    def to_core(self, q):
+        place = self.place
+        self.third[q].wait_recv()
+        part = self.o.at[:, :, :, place.k, :, pl.ds(*self.pieces[q])]
+        self.fourth[q] = remote(part, part, self.sems[6].at[q], self.sems[7].at[q], place.core)
+        self.fourth[q].start()
+
+    def steps(self):
+        return pipelined(self.n, (self.to_side, self.to_other_side, self.to_core))
+
+    def end(self):
+        for copy in self.fourth:
+            copy.wait_recv()
+        for copy in self.first + self.second + self.third + self.fourth:
+            copy.wait_send()
+
+
+def pipelined(count, stages):
+    def step(at):
+        for lag, stage in enumerate(stages):
+            if 0 <= at - lag < count:
+                stage(at - lag)
+
+    return [functools.partial(step, at) for at in range(count + len(stages) - 1)]
+
+
+def gather_sems(n, groups):
+    return [DMA((n, groups - 1)), DMA((n, groups - 1))] + [DMA((n,))] * 6 + [DMA]
+
+
+class Scatter:
+    def __init__(self, place, make, pieces, bufs, acc, sems):
+        self.place, self.make, self.pieces, self.bufs, self.acc = place, make, pieces, bufs, acc
+        self.sems = sems
+        n = len(pieces)
+        self.n = n
+        self.c1, self.c2, self.c3, self.c4 = [None] * n, [None] * n, [None] * n, [None] * n
+
+    def to_core(self, q):
+        theirs, mine, b1 = self.bufs[:3]
+        cols, k = pl.ds(*self.pieces[q]), self.place.k
+        self.make(q, theirs, 1 - k)
+        self.c1[q] = remote(
+            theirs.at[..., cols],
+            b1.at[..., cols],
+            self.sems[0].at[q],
+            self.sems[1].at[q],
+            self.place.core,
+        )
+        self.c1[q].start()
+        self.make(q, mine, k)
+
+    def to_side(self, q):
+        _, mine, b1, b2, _, _ = self.bufs
+        place, cols = self.place, pl.ds(*self.pieces[q])
+        f32 = jnp.float32
+        self.c1[q].wait_recv()
+        b1[..., cols] = (b1[..., cols].astype(f32) + mine[..., cols].astype(f32)).astype(b1.dtype)
+        if q % 2 == 0:
+            part, device = b1.at[:, :, 1 - place.y, :, cols], place.side_y
+        else:
+            part, device = b1.at[:, 1 - place.c, :, :, cols], place.side_x
+        self.c2[q] = remote(
+            part, b2.at[:, :, :, cols], self.sems[2].at[q], self.sems[3].at[q], device
+        )
+        self.c2[q].start()
+
+    def to_other_side(self, q):
+        _, _, b1, b2, b3, _ = self.bufs
+        place, cols = self.place, pl.ds(*self.pieces[q])
+        f32 = jnp.float32
+        self.c2[q].wait_recv()
+        own = b1[:, :, place.y, :, cols] if q % 2 == 0 else b1[:, place.c, :, :, cols]
+        b2[:, :, :, cols] = (b2[:, :, :, cols].astype(f32) + own.astype(f32)).astype(b2.dtype)
+        if q % 2 == 0:
+            part, device = b2.at[:, 1 - place.c, :, cols], place.side_x
+        else:
+            part, device = b2.at[:, 1 - place.y, :, cols], place.side_y
+        self.c3[q] = remote(part, b3.at[:, :, cols], self.sems[4].at[q], self.sems[5].at[q], device)
+        self.c3[q].start()
+
+    def along_line(self, q):
+        _, _, _, b2, b3, b4 = self.bufs
+        place, cols = self.place, pl.ds(*self.pieces[q])
+        f32 = jnp.float32
+        self.c3[q].wait_recv()
+        own = b2[:, place.c, :, cols] if q % 2 == 0 else b2[:, place.y, :, cols]
+        b3[:, :, cols] = (b3[:, :, cols].astype(f32) + own.astype(f32)).astype(b3.dtype)
+        self.c4[q] = []
+        for d in range(place.groups - 1):
+            to = lax.rem(place.g + d + 1, place.groups)
             copy = remote(
-                x.at[:, cols], o.at[g, c, y, k, :, cols], zs.at[q, d], zr.at[q, d], place.line[d]
+                b3.at[to, :, cols],
+                b4.at[d, :, cols],
+                self.sems[6].at[q, d],
+                self.sems[7].at[q, d],
+                place.line[d],
             )
             copy.start()
-            first.append(copy)
-    own.wait()
-    second, third, fourth = [None] * n, [None] * n, [None] * n
-
-    def to_side(q):
-        cols = pl.ds(*pieces[q])
-        for d in range(lines):
-            src = lax.rem(g + place.groups - d - 1, place.groups)
-            remote(
-                x.at[:, cols], o.at[src, c, y, k, :, cols], zs.at[q, d], zr.at[q, d], place.line[d]
-            ).wait_recv()
-        part = o.at[:, c, y, k, :, cols]
-        device = place.side_y if q % 2 == 0 else place.side_x
-        second[q] = remote(part, part, s2.at[q], r2.at[q], device)
-        second[q].start()
-
-    def to_other_side(q):
-        cols = pl.ds(*pieces[q])
-        second[q].wait_recv()
-        if q % 2 == 0:
-            part, device = o.at[:, c, :, k, :, cols], place.side_x
-        else:
-            part, device = o.at[:, :, y, k, :, cols], place.side_y
-        third[q] = remote(part, part, s3.at[q], r3.at[q], device)
-        third[q].start()
-
-    def to_core(q):
-        cols = pl.ds(*pieces[q])
-        third[q].wait_recv()
-        part = o.at[:, :, :, k, :, cols]
-        fourth[q] = remote(part, part, s4.at[q], r4.at[q], place.core)
-        fourth[q].start()
-
-    for step in range(n + 2):
-        between()
-        if step < n:
-            to_side(step)
-        if 0 <= step - 1 < n:
-            to_other_side(step - 1)
-        if 0 <= step - 2 < n:
-            to_core(step - 2)
-    for q in range(n):
-        fourth[q].wait_recv()
-    for copy in first + second + third + fourth:
-        copy.wait_send()
-
-
-def gather_sems(n, groups):
-    return [DMA((n, groups - 1)), DMA((n, groups - 1))] + [DMA((n,))] * 6 + [DMA]
-
-
-def scatter_stage(place, make, pieces, bufs, acc, sems, between):
-    theirs, mine, b1, b2, b3, b4 = bufs
-    sa, ra, sb, rb, sc, rc, sd, rd = sems
-    g, c, y, k = place.g, place.c, place.y, place.k
-    n = len(pieces)
-    lines = place.groups - 1
-    f32, bf16 = jnp.float32, jnp.bfloat16
-    c1, c2, c3, c4 = [None] * n, [None] * n, [None] * n, [None] * n
-
-    def to_core(q):
-        cols = pl.ds(*pieces[q])
-        make(q, theirs, 1 - k)
-        c1[q] = remote(theirs.at[..., cols], b1.at[..., cols], sa.at[q], ra.at[q], place.core)
-        c1[q].start()
-        make(q, mine, k)
-
-    def to_side(q):
-        cols = pl.ds(*pieces[q])
-        c1[q].wait_recv()
-        b1[..., cols] = (b1[..., cols].astype(f32) + mine[..., cols].astype(f32)).astype(bf16)
-        if q % 2 == 0:
-            part, device = b1.at[:, :, 1 - y, :, cols], place.side_y
-        else:
-            part, device = b1.at[:, 1 - c, :, :, cols], place.side_x
-        c2[q] = remote(part, b2.at[:, :, :, cols], sb.at[q], rb.at[q], device)
-        c2[q].start()
-
-    def to_other_side(q):
-        cols = pl.ds(*pieces[q])
-        c2[q].wait_recv()
-        own = b1[:, :, y, :, cols] if q % 2 == 0 else b1[:, c, :, :, cols]
-        b2[:, :, :, cols] = (b2[:, :, :, cols].astype(f32) + own.astype(f32)).astype(bf16)
-        if q % 2 == 0:
-            part, device = b2.at[:, 1 - c, :, cols], place.side_x
-        else:
-            part, device = b2.at[:, 1 - y, :, cols], place.side_y
-        c3[q] = remote(part, b3.at[:, :, cols], sc.at[q], rc.at[q], device)
-        c3[q].start()
-
-    def along_line(q):
-        cols = pl.ds(*pieces[q])
-        c3[q].wait_recv()
-        own = b2[:, c, :, cols] if q % 2 == 0 else b2[:, y, :, cols]
-        b3[:, :, cols] = (b3[:, :, cols].astype(f32) + own.astype(f32)).astype(bf16)
-        c4[q] = []
-        for d in range(lines):
-            to = lax.rem(g + d + 1, place.groups)
-            copy = remote(
-                b3.at[to, :, cols], b4.at[d, :, cols], sd.at[q, d], rd.at[q, d], place.line[d]
-            )
+            self.c4[q].append(copy)
+
+    def land(self, q):
+        b3, b4 = self.bufs[4:]
+        cols = pl.ds(*self.pieces[q])
+        total = b3[self.place.g, :, cols].astype(jnp.float32)
+        for d in range(self.place.groups - 1):
+            self.c4[q][d].wait_recv()
+            total = total + b4[d, :, cols].astype(jnp.float32)
+        self.acc[:, cols] = total
+
+    def steps(self):
+        stages = (self.to_core, self.to_side, self.to_other_side, self.along_line, self.land)
+        return pipelined(self.n, stages)
+
+    def end(self):
+        for q in range(self.n):
+            for copy in [self.c1[q], self.c2[q], self.c3[q]] + self.c4[q]:
+                copy.wait_send()
+
+
+class SmallSum:
+    def __init__(self, place, x, o, zbuf, buf, zs, zr, ss, rs):
+        self.place, self.x, self.o, self.zbuf, self.buf = place, x, o, zbuf, buf
+        self.zs, self.zr, self.ss, self.rs = zs, zr, ss, rs
+
+    def begin(self):
+        self.copies = []
+        for d, device in enumerate(self.place.line):
+            copy = remote(self.x, self.zbuf.at[d], self.zs.at[d], self.zr.at[d], device)
             copy.start()
-            c4[q].append(copy)
-
-    def land(q):
-        cols = pl.ds(*pieces[q])
-        total = b3[g, :, cols].astype(f32)
-        for d in range(lines):
-            c4[q][d].wait_recv()
-            total = total + b4[d, :, cols].astype(f32)
-        acc[:, cols] = total
-
-    for step in range(n + 4):
-        for lag, stage in enumerate((to_core, to_side, to_other_side, along_line, land)):
-            if 0 <= step - lag < n:
-                stage(step - lag)
-        between()
-    for q in range(n):
-        for copy in [c1[q], c2[q], c3[q]] + c4[q]:
+            self.copies.append(copy)
+
+    def line(self):
+        place, groups = self.place, self.place.groups
+        for copy in self.copies:
+            copy.wait_recv()
+        total = None
+        for owner in range(groups):
+            part = self.x[...]
+            for d in range(groups - 1):
+                source = lax.rem(place.g + groups - d - 1, groups)
+                part = jnp.where(source == owner, self.zbuf[d], part)
+            total = part if total is None else total + part
+        self.o[...] = total
+        self.send(0)
+
+    def send(self, i):
+        device = (self.place.side_x, self.place.side_y, self.place.core)[i]
+        self.copy = remote(self.o, self.buf.at[i], self.ss.at[i], self.rs.at[i], device)
+        self.copy.start()
+
+    def add(self, i):
+        self.copy.wait_recv()
+        self.copy.wait_send()
+        self.o[...] = self.o[...] + self.buf[i]
+        if i < 2:
+            self.send(i + 1)
+
+    def steps(self):
+        return [self.line] + [functools.partial(self.add, i) for i in range(3)]
+
+    def end(self):
+        for copy in self.copies:
             copy.wait_send()
+
+
+def small_scratch(shape, groups):
+    f32 = jnp.float32
+    return [
+        pltpu.VMEM((groups - 1, *shape), f32),
+        pltpu.VMEM((3, *shape), f32),
+        DMA((groups - 1,)),
+        DMA((groups - 1,)),
+        DMA((3,)),
+        DMA((3,)),
+    ]
+
+
+def weave(*streams):
+    found = []
+    rounds = max((start + len(steps) for start, steps in streams), default=0)
+    for at in range(rounds):
+        for start, steps in streams:
+            if 0 <= at - start < len(steps):
+                found.append(steps[at - start])
+    return found
 
 
 def scatter_scratch(n, groups, rows, width):
@@ -906,59 +1000,147 @@
 NN = (((1,), (0,)), ((), ()))
 
 
+class Summed:
+    def __init__(self, sizes, products, extra=None, pieces=SUM_SHARES):
+        self.sizes, self.products, self.extra = sizes, products, extra
+        self.rows = products[0][0].shape[0] // (sizes[0] * sizes[1] * sizes[2])
+        self.width = products[0][1].shape[-2 if products[0][3] else -1]
+        self.more = 0 if extra is None else extra.shape[1]
+        self.rights, self.places = [], []
+        for _, right, _, _ in products:
+            found = [i for i, other in enumerate(self.rights) if other is right]
+            self.places.append(found[0] if found else len(self.rights))
+            if not found:
+                self.rights.append(right)
+        at, self.pieces = 0, []
+        for share in pieces:
+            self.pieces.append((at, self.width * share // 16))
+            at += self.width * share // 16
+        if self.more:
+            self.pieces.append((self.width, self.more))
+        self.bufs, self.sems = scatter_scratch(
+            len(self.pieces), sizes[0], self.rows, self.width + self.more
+        )
+
+    def operands(self):
+        groups, ctx, tp = self.sizes
+        split = (groups, ctx, tp // 2, 2, self.rows)
+        found = [product[0].reshape(*split, product[0].shape[1]) for product in self.products]
+        found += self.rights
+        if self.more:
+            found.append(self.extra.reshape(*split, self.more))
+        return found
+
+    def stage(self, place, inputs, scratch):
+        count = len(self.products)
+        lefts, rights = inputs[:count], inputs[count : count + len(self.rights)]
+        bufs, sems = scratch[: len(self.bufs)], scratch[len(self.bufs) :]
+        groups, ctx, tp = self.sizes
+
+        def make(q, into, core):
+            at, size = self.pieces[q]
+            if at >= self.width:
+                into[..., pl.ds(at, size)] = inputs[-1][:, :, :, core]
+                return
+
+            def block(i, _):
+                total = None
+                for left, where, (_, _, lead, transposed) in zip(
+                    lefts, self.places, self.products
+                ):
+                    right = rights[where] if lead is None else rights[where].at[lead]
+                    a = left[i, :, :, core]
+                    a = a.reshape(-1, a.shape[-1])
+                    some = right[pl.ds(at, size), :] if transposed else right[:, pl.ds(at, size)]
+                    part = lax.dot_general(
+                        a, some, NT if transposed else NN, preferred_element_type=jnp.float32
+                    )
+                    total = part if total is None else total + part
+                into[i, :, :, :, pl.ds(at, size)] = total.astype(into.dtype).reshape(
+                    ctx, tp // 2, self.rows, size
+                )
+                return 0
+
+            lax.fori_loop(0, groups, block, 0)
+
+        return Scatter(place, make, self.pieces, bufs[:-1], bufs[-1], sems)
+
+
 def exchange(
     sizes,
     number,
-    products,
-    extra,
+    summed,
     finish,
     finish_args,
     finish_outs,
     gathered,
     moves,
     early_share=60,
+    also_gather=None,
+    also_sum=None,
     tail=0,
+    small=0,
 ):
     groups, ctx, tp = sizes
     f32, bf16 = jnp.float32, jnp.bfloat16
-    total_rows = products[0][0].shape[0]
-    rows = total_rows // (groups * ctx * tp)
-    width = products[0][1].shape[-2 if products[0][3] else -1]
-    rights_all, places = [], []
-    for _, right, _, _ in products:
-        found = [i for i, other in enumerate(rights_all) if other is right]
-        places.append(found[0] if found else len(rights_all))
-        if not found:
-            rights_all.append(right)
-    more = 0 if extra is None else extra.shape[1]
-    pieces = spans(width, more, 4)
-    out_pieces = spans(gathered, 0, 1) if gathered < 1024 else spans(2048, gathered - 2048, 4)
+    rows = summed.rows
+    out_pieces = gather_pieces(gathered)
     move_outs, move_scratch = moves_setup(moves, groups * ctx)
-    bufs, sems = scatter_scratch(len(pieces), groups, rows, width + more)
-    n_prod, n_args, n_outs, n_moves = len(products), len(finish_args), len(finish_outs), len(moves)
+    n_moves = len(moves)
     move_specs = [(split, join) for _, split, join in moves]
+    S = jax.ShapeDtypeStruct
+
+    operands, in_specs, out_shape, out_specs, scratch = [], [], [], [], []
+
+    def add_in(arrays, spec=IN_VMEM):
+        at = len(operands)
+        operands.extend(arrays)
+        in_specs.extend([spec] * len(arrays))
+        return slice(at, len(operands))
+
+    def add_out(shapes, spec=IN_VMEM):
+        at = len(out_shape)
+        out_shape.extend(shapes)
+        out_specs.extend([spec] * len(shapes))
+        return slice(at, len(out_shape))
+
+    def add_scratch(shapes):
+        at = len(scratch)
+        scratch.extend(shapes)
+        return slice(at, len(scratch))
+
+    in_sum = add_in(summed.operands())
+    in_args = add_in(list(finish_args))
+    o_main = add_out([S((groups, ctx, tp // 2, 2, rows, gathered), bf16)])
+    o_finish = add_out([S(shape, f32) for shape in finish_outs])
+    s_sum = add_scratch(summed.bufs + summed.sems)
+    s_main = add_scratch(
+        [pltpu.VMEM((rows, gathered), bf16)] + gather_sems(len(out_pieces), groups)
+    )
+    if also_gather is not None:
+        also_pieces = gather_pieces(also_gather.shape[1])
+        in_also = add_in([also_gather])
+        o_also = add_out([S((groups, ctx, tp // 2, 2, rows, also_gather.shape[1]), bf16)])
+        s_also = add_scratch(gather_sems(len(also_pieces), groups))
+    if also_sum is not None:
+        second, second_finish, second_args, second_out = also_sum
+        in_second, in_second_args = add_in(second.operands()), add_in(second_args)
+        o_second = add_out([second_out])
+        s_second = add_scratch(second.bufs + second.sems)
+    if tail:
+        o_tail = add_out([S((tp // 2, 2, rows, tail), bf16)])
+        s_tail = add_scratch([pltpu.VMEM((rows, tail), bf16)] + [DMA] * 5)
+    if small:
+        o_small = add_out([S((1, small), f32)])
+        s_small = add_scratch([pltpu.VMEM((1, small), f32)] + small_scratch((1, small), groups))
+    in_moves = add_in([array for array, _, _ in moves], IN_HBM)
+    o_moves = add_out(move_outs, IN_HBM)
+    s_moves = add_scratch(move_scratch)
 
     def kernel(*refs):
-        refs = list(refs)
-
-        def take(count):
-            head = refs[:count]
-            del refs[:count]
-            return head
-
-        lefts, rights = take(n_prod), take(len(rights_all))
-        extra_ref = take(1)[0] if more else None
-        args, sources = take(n_args), take(n_moves)
-        o = take(1)[0]
-        o_tail = take(1)[0] if tail else None
-        outs, targets = take(n_outs), take(n_moves)
-        b = take(len(bufs))
-        acc = b.pop()
-        s = take(len(sems))
-        low = take(1)[0]
-        gs = take(9)
-        if tail:
-            low_tail, ts = take(1)[0], take(5)
+        ins = refs[: len(operands)]
+        outs = refs[len(operands) : len(operands) + len(out_shape)]
+        scr = refs[len(operands) + len(out_shape) :]
         place = Place(sizes)
         devices = [place.core, place.side_y]
         if n_moves:
@@ -968,92 +1150,77 @@
         greet(devices)
         carried = None
         if n_moves:
-            stages = take(n_moves)
-            send, recv, local = take(3)
-            carried = Moves(place, move_specs, sources, targets, stages, send, recv, local)
-
-        def make(q, into, core):
-            at, size = pieces[q]
-            if at >= width:
-                into[..., pl.ds(at, size)] = extra_ref[:, :, :, core]
-                return
-
-            def block(i, _):
-                total = None
-                for left, where, (_, _, lead, transposed) in zip(lefts, places, products):
-                    right = rights[where] if lead is None else rights[where].at[lead]
-                    a = left[i, :, :, core]
-                    a = a.reshape(-1, a.shape[-1])
-                    if transposed:
-                        part = lax.dot_general(
-                            a, right[pl.ds(at, size), :], NT, preferred_element_type=f32
-                        )
-                    else:
-                        part = lax.dot_general(
-                            a, right[:, pl.ds(at, size)], NN, preferred_element_type=f32
-                        )
-                    total = part if total is None else total + part
-                into[i, :, :, :, pl.ds(at, size)] = total.astype(bf16).reshape(
-                    ctx, tp // 2, rows, size
-                )
-                return 0
-
-            lax.fori_loop(0, groups, block, 0)
-
-        def between(count):
-            return lambda: carried.issue(count) if carried is not None else None
-
-        if carried is not None:
+            parts = scr[s_moves]
+            carried = Moves(
+                place, move_specs, ins[in_moves], outs[o_moves], parts[:n_moves], *parts[n_moves:]
+            )
             carried.start()
-        steps = len(pieces) + 4
-        early = -(-(n_moves * (groups * ctx - 1) * early_share) // (100 * steps))
-        scatter_stage(place, make, pieces, b, acc, s, between(early))
+        main_sum = summed.stage(place, ins[in_sum], scr[s_sum])
+        low, *main_sems = scr[s_main]
+        main_gather = Gather(place, low, outs[o_main][0], out_pieces, main_sems)
+        streams = [(0, main_sum.steps())]
+        ends = [main_sum, main_gather]
+        if also_gather is not None:
+            side_gather = Gather(place, ins[in_also][0], outs[o_also][0], also_pieces, scr[s_also])
+            side_gather.begin()
+            streams.append((2, side_gather.steps()))
+            ends.append(side_gather)
+        later = []
+        if also_sum is not None:
+            side_sum = second.stage(place, ins[in_second], scr[s_second])
+            side_steps = side_sum.steps()
+            streams.append((6, side_steps[:3]))
+            later.append((0, side_steps[3:]))
+            ends.append(side_sum)
+        total = n_moves * (groups * ctx - 1)
+        steps = weave(*streams)
+        per_step = -(-total * early_share // (100 * len(steps)))
+        for step in steps:
+            step()
+            if carried is not None:
+                carried.issue(per_step)
         if carried is not None:
             carried.settle()
-        finish(place, acc, args, outs, low, low_tail if tail else None)
+        low_tail = scr[s_tail][0] if tail else None
+        low_small = scr[s_small][0] if small else None
+        finish(place, main_sum.acc, ins[in_args], outs[o_finish], low, low_tail, low_small)
+        main_gather.begin()
+        if small:
+            small_sum = SmallSum(place, low_small, outs[o_small][0], *scr[s_small][1:])
+            small_sum.begin()
+            later.append((1, small_sum.steps()))
+            ends.append(small_sum)
         if tail:
-            ys, yr, ks, kr, own_sem = ts
-            y, k = place.y, place.k
-            own = pltpu.make_async_copy(low_tail, o_tail.at[y, k], own_sem)
+            ys, yr, ks, kr, own_sem = scr[s_tail][1:]
+            y, k, spot = place.y, place.k, outs[o_tail][0]
+            own = pltpu.make_async_copy(low_tail, spot.at[y, k], own_sem)
             own.start()
-            to_y = remote(low_tail, o_tail.at[y, k], ys, yr, place.side_y)
+            to_y = remote(low_tail, spot.at[y, k], ys, yr, place.side_y)
             to_y.start()
             own.wait()
-        late = -(-n_moves * (groups * ctx - 1) // max(1, len(out_pieces)))
-        gather_stage(place, low, o, out_pieces, gs, between(late))
+        steps = weave((0, main_gather.steps()), *later)
+        left = 0 if carried is None else len(carried.queue)
+        per_step = -(-left // max(1, len(steps) - 2))
+        for step in steps:
+            if carried is not None:
+                carried.issue(per_step)
+            step()
         if tail:
             to_y.wait_recv()
-            part = o_tail.at[:, k]
+            part = spot.at[:, k]
             to_k = remote(part, part, ks, kr, place.core)
             to_k.start()
             to_k.wait_recv()
             to_y.wait_send()
             to_k.wait_send()
+        if also_sum is not None:
+            second_finish(side_sum.acc, ins[in_second_args], outs[o_second][0])
+        for stage in ends:
+            stage.end()
         if carried is not None:
-            carried.issue(10**6)
+            carried.issue(total)
             carried.finish()
 
-    S = jax.ShapeDtypeStruct
-    out_shape = [S((groups, ctx, tp // 2, 2, rows, gathered), bf16)]
-    out_specs = [IN_VMEM]
-    if tail:
-        out_shape.append(S((tp // 2, 2, rows, tail), bf16))
-        out_specs.append(IN_VMEM)
-    out_shape += [S(shape, f32) for shape in finish_outs] + move_outs
-    out_specs += [IN_VMEM] * n_outs + [IN_HBM] * n_moves
-    scratch = bufs + sems + [pltpu.VMEM((rows, gathered), bf16)]
-    scratch += gather_sems(len(out_pieces), groups)
-    if tail:
-        scratch += [pltpu.VMEM((rows, tail), bf16)] + [DMA] * 5
-    scratch += move_scratch
-    split = (groups, ctx, tp // 2, 2, rows)
-    operands = [product[0].reshape(*split, product[0].shape[1]) for product in products]
-    operands += rights_all
-    if more:
-        operands.append(extra.reshape(*split, more))
-    operands += list(finish_args)
-    in_specs = [IN_VMEM] * len(operands) + [IN_HBM] * n_moves
-    operands += [array for array, _, _ in moves]
     results = pl.pallas_call(
         kernel,
         out_shape=out_shape,
@@ -1065,10 +1232,30 @@
             collective_id=number, has_side_effects=True, vmem_limit_bytes=62 * 2**20
         ),
     )(*operands)
-    results = list(results)
-    spread_out = results.pop(0).reshape(total_rows, gathered)
-    tail_out = [results.pop(0).reshape(tp * rows, tail)] if tail else []
-    return [spread_out] + tail_out + results
+    found = {"gathered": results[0].reshape(-1, gathered), "finish": results[o_finish]}
+    if also_gather is not None:
+        found["also"] = results[o_also][0].reshape(-1, also_gather.shape[1])
+    if also_sum is not None:
+        found["second"] = results[o_second][0]
+    if tail:
+        found["tail"] = results[o_tail][0].reshape(-1, tail)
+    if small:
+        found["small"] = results[o_small][0]
+    found["moves"] = results[o_moves]
+    return found
+
+
+def gather_pieces(width):
+    if width < 1024:
+        return [(0, width)]
+    whole = width // 2048 * 2048
+    at, found = 0, []
+    for share in GATHER_SHARES:
+        found.append((at, whole * share // 16))
+        at += whole * share // 16
+    if width > whole:
+        found.append((whole, width - whole))
+    return found
 
 
 def opening(sizes, number, hidden, embeds, lengths, gain, down_all, moves):
@@ -1078,7 +1265,7 @@
     half = hidden.shape[1]
     mids = down_all.shape[1]
     width = 2 * half + mids + 128
-    out_pieces = spans(4096, width - 4096, 4)
+    out_pieces = gather_pieces(width)
     move_outs, move_scratch = moves_setup(moves, groups * ctx)
     move_specs = [(split, join) for _, split, join in moves]
     n_moves = len(moves)
@@ -1122,9 +1309,14 @@
             position = position - passed * length
         marks = jnp.where(lane == 0, segment, position)
         low[:, 2 * half + mids :] = marks.astype(f32).astype(bf16)
-        gather_stage(place, low, o, out_pieces, gs, lambda: carried.issue(4))
-        carried.issue(10**6)
+        gather = Gather(place, low, o, out_pieces, gs)
+        gather.begin()
+        for step in gather.steps():
+            carried.issue(4)
+            step()
+        carried.issue(len(carried.queue))
         carried.settle()
+        gather.end()
         carried.finish()
 
     S = jax.ShapeDtypeStruct
@@ -1145,68 +1337,33 @@
 
 
 def sum_small(sizes, number, values):
-    groups, ctx, tp = sizes
-    f32 = jnp.float32
-
-    def kernel(x, o, zbuf, buf, zs, zr, ss, rs):
+    def kernel(x, o, *scratch):
         place = Place(sizes)
         greet([place.core, place.side_y, place.side_x] + place.line)
-        copies = []
-        for d, device in enumerate(place.line):
-            copy = remote(x, zbuf.at[d], zs.at[d], zr.at[d], device)
-            copy.start()
-            copies.append(copy)
-        total = x[...]
-        for d in range(groups - 1):
-            copies[d].wait_recv()
-        order = [zbuf[d] for d in range(groups - 1)]
-        parts = []
-        for g in range(groups):
-            part = total
-            for d in range(groups - 1):
-                src = lax.rem(place.g + groups - d - 1, groups)
-                part = jnp.where(src == g, order[d], part)
-            parts.append(part)
-        total = parts[0]
-        for part in parts[1:]:
-            total = total + part
-        for i, device in enumerate((place.side_x, place.side_y, place.core)):
-            o[...] = total
-            copy = remote(o, buf.at[i], ss.at[i], rs.at[i], device)
-            copy.start()
-            copy.wait_recv()
-            copy.wait_send()
-            total = total + buf[i]
-        o[...] = total
-        for copy in copies:
-            copy.wait_send()
-
-    shape = values.shape
+        summing = SmallSum(place, x, o, *scratch)
+        summing.begin()
+        for step in summing.steps():
+            step()
+        summing.end()
+
     return pl.pallas_call(
         kernel,
-        out_shape=jax.ShapeDtypeStruct(shape, f32),
+        out_shape=jax.ShapeDtypeStruct(values.shape, jnp.float32),
         in_specs=[IN_VMEM],
         out_specs=IN_VMEM,
-        scratch_shapes=[
-            pltpu.VMEM((groups - 1, *shape), f32),
-            pltpu.VMEM((3, *shape), f32),
-            DMA((groups - 1,)),
-            DMA((groups - 1,)),
-            DMA((3,)),
-            DMA((3,)),
-        ],
+        scratch_shapes=small_scratch(values.shape, sizes[0]),
         name=f"sum_small_{number}",
         compiler_params=pltpu.CompilerParams(collective_id=number, has_side_effects=True),
     )(values)
 
 
-def finish_forward(place, acc, args, outs, low, low_tail):
+def finish_forward(place, acc, args, outs, low, low_tail, low_small):
     rest, gain = args
     outs[0][...] = rest[...] + acc[...]
     low[...] = rms_rows(outs[0][...], gain[...]).astype(jnp.bfloat16)
 
 
-def finish_mixer_back(place, acc, args, outs, low, low_tail):
+def finish_mixer_back(place, acc, args, outs, low, low_tail, low_small):
     after_mlp, gain, cot, state_map = args
     width = after_mlp.shape[1]
     low[:, width:] = acc[:, width:].astype(jnp.bfloat16)
@@ -1220,7 +1377,7 @@
     low[:, :width] = d_rows.astype(jnp.bfloat16)
 
 
-def finish_mlp_back(place, acc, args, outs, low, low_tail):
+def finish_mlp_back(place, acc, args, outs, low, low_tail, low_small):
     after_attn, gain, d_after_mlp = args
     d_rows, d_gain = rms_back(after_attn[...], gain[...], acc[...])
     outs[1][...] = d_gain
@@ -1229,8 +1386,8 @@
     low[...] = d_rows.astype(jnp.bfloat16)
 
 
-def finish_attention_back(place, acc, args, outs, low, low_tail):
-    hidden, embeds, gain, d_after_attn, down_all, out_mine = args
+def finish_attention_back(place, acc, args, outs, low, low_tail, low_small):
+    hidden, embeds, gain, d_after_attn, down_all, out_mine, row = args
     half = hidden.shape[1]
     bf16, f32 = jnp.bfloat16, jnp.float32
     low[...] = acc[:, 2 * half :].astype(bf16)
@@ -1247,20 +1404,42 @@
         along = along + jnp.sum(grad * gain[:, cols] * part[...], axis=1, keepdims=True)
     along = along / (2 * half)
     low_tail[:, :half] = out_mine[...]
+    low_small[:, 2 * half :] = row[...]
     for i, part in enumerate(inputs):
         cols = slice(i * half, (i + 1) * half)
         grad = acc[:, cols]
-        outs[0][:, cols] = jnp.sum(grad * part[...] * inverse, axis=0, keepdims=True)
+        low_small[:, cols] = jnp.sum(grad * part[...] * inverse, axis=0, keepdims=True)
         d_rows = grad * gain[:, cols] * inverse - part[...] * inverse**3 * along
         if i == 0:
             d_rows = d_rows + d_after_attn[...]
         low_tail[:, (i + 1) * half : (i + 2) * half] = d_rows.astype(bf16)
 
 
-def pack(parts, dtype):
-    flat = jnp.concatenate([part.reshape(-1).astype(dtype) for part in parts])
-    count = -(-flat.shape[0] // 2048) * 2048
-    return jnp.pad(flat, (0, count - flat.shape[0])).reshape(-1, 128)
+def finish_out(acc, args, out):
+    out[...] = (args[0][...] + acc[...]).astype(out.dtype)
+
+
+def adapter_products(xa, dmid, width):
+    block, rank = 512, dmid.shape[1] // 3
+
+    def kernel(a, b, o):
+        both = lax.dot_general(
+            a[...], b[...], (((0,), (0,)), ((), ())), preferred_element_type=jnp.float32
+        )
+        for j in range(3):
+            o[j] = both[:, j * rank : (j + 1) * rank]
+
+    return pl.pallas_call(
+        kernel,
+        out_shape=jax.ShapeDtypeStruct((3, width, rank), jnp.float32),
+        grid=(width // block,),
+        in_specs=[
+            pl.BlockSpec((xa.shape[0], block), lambda i: (0, i)),
+            pl.BlockSpec(dmid.shape, lambda i: (0, 0)),
+        ],
+        out_specs=pl.BlockSpec((3, block, rank), lambda i: (0, i, 0)),
+        name="adapter_products",
+    )(xa, dmid)
 
 
 def unpack(packed, parts):
@@ -1392,7 +1571,7 @@
     rank = adapter_down_maps.shape[2]
     width_a = adapter_down_maps.shape[1]
     down_all = jnp.concatenate([adapter_down_maps[j] for j in range(3)], axis=1)
-    gathered, w_qkv, w_o = opening(
+    xa_wide, w_qkv, w_o = opening(
         sizes,
         1,
         hidden,
@@ -1402,13 +1581,11 @@
         down_all,
         [(query_key_value_weight, 2, 1), (attention_output_weight, 0, 1)],
     )
-    xa = gathered[:, :width_a]
-    mid = gathered[:, width_a : width_a + 3 * rank]
-    segment = gathered[:, width_a + 3 * rank].astype(jnp.int32).reshape(groups, group_rows)
-    position = gathered[:, width_a + 3 * rank + 1].astype(jnp.int32).reshape(groups, group_rows)
+    xa = xa_wide[:, :width_a]
+    mid = xa_wide[:, width_a : width_a + 3 * rank]
+    segment = xa_wide[:, width_a + 3 * rank].astype(jnp.int32).reshape(groups, group_rows)
+    position = xa_wide[:, width_a + 3 * rank + 1].astype(jnp.int32).reshape(groups, group_rows)
     position_flat = position.reshape(-1)
-    late_cot, _ = lax.optimization_barrier((cot_low, w_o))
-    cot = lax.all_gather(late_cot, EVERY, axis=0, tiled=True)
     proj = [
         (
             matrix_product(xa, w_qkv[j])
@@ -1423,33 +1600,35 @@
     ao_low = ao.astype(bf16).reshape(groups * group_rows, AHD)
 
     gain_m = feedforward_norm_gain.reshape(1, -1)
-    xm, after_attn, w_gu, w_down = exchange(
+    found = exchange(
         sizes,
         2,
-        [(ao_low, w_o, None, False)],
-        None,
+        Summed(sizes, [(ao_low, w_o, None, False)]),
         finish_forward,
         [hidden_f, gain_m],
         [hidden_f.shape],
         width,
         [(gate_up_weight, 2, 1), (down_weight, 0, 1)],
     )
+    xm, (after_attn,), (w_gu, w_down) = found["gathered"], found["finish"], found["moves"]
     gate_pre, up_pre = matrix_product(xm, w_gu[0]), matrix_product(xm, w_gu[1])
     activated, act_back = jax.vjp(gated_gelu, gate_pre, up_pre)
     hid_low = activated.astype(bf16)
 
     gain_n = mixer_norm_gain.reshape(1, -1)
-    xn, after_mlp, w_zx, w_out = exchange(
+    found = exchange(
         sizes,
         3,
-        [(hid_low, w_down, None, False)],
-        None,
+        Summed(sizes, [(hid_low, w_down, None, False)]),
         finish_forward,
         [after_attn, gain_n],
         [hidden_f.shape],
         width,
         [(mixer_gate_input_weight, 2, 1), (mixer_output_weight, 0, 1)],
-    )
+        also_gather=cot_low,
+    )
+    xn, cot, (after_mlp,) = found["gathered"], found["also"], found["finish"]
+    w_zx, w_out = found["moves"]
     gate_z = matrix_product(xn, w_zx[0])
     inner_x = matrix_product(xn, w_zx[1]).astype(bf16)
     step_raw = matrix_product(xn, w_step).astype(bf16)
@@ -1481,9 +1660,6 @@
     inverse = lax.rsqrt(sums[0] / INNER + epsilon)[:, None]
     cross = (sums[1] / INNER)[:, None]
     yn_low = (gated * inverse * gate_gain).astype(bf16)
-    out_part = matrix_product(yn_low, w_out).astype(bf16)
-    out_mine = lax.psum_scatter(out_part, EVERY, scatter_dimension=0, tiled=True)
-    out_mine = (after_mlp + out_mine.astype(f32)).astype(bf16)
 
     grad_w_out = outer_product_sum(yn_low, cot)
     grad_g_gate = jnp.sum(d_yn * gated * inverse, axis=0)
@@ -1508,21 +1684,32 @@
     )
     grad_w_dt = outer_product_sum(xn, d_step)
     lanes = ((0, 0), (0, 128 - d_step.shape[1]))
-    gathered, d_after_mlp, grad_g_mamba, grad_w_zx, grad_w_out = exchange(
+    found = exchange(
         sizes,
         5,
-        [
-            (d_z, w_zx, 0, True),
-            (d_xs, w_zx, 1, True),
-            (jnp.pad(d_step, lanes), jnp.pad(w_step, lanes), None, True),
-        ],
-        d_bc_part.astype(bf16),
+        Summed(
+            sizes,
+            [
+                (d_z, w_zx, 0, True),
+                (d_xs, w_zx, 1, True),
+                (jnp.pad(d_step, lanes), jnp.pad(w_step, lanes), None, True),
+            ],
+            d_bc_part.astype(bf16),
+        ),
         finish_mixer_back,
         [after_mlp, gain_n, cot_low, state_map_weight],
         [hidden_f.shape, gain_n.shape],
         width + d_bc_part.shape[1],
         [(grad_w_zx, 1, 2), (grad_w_out.astype(bf16), 1, 0)],
-    )
+        also_sum=(
+            Summed(sizes, [(yn_low, w_out, None, False)]),
+            finish_out,
+            [after_mlp],
+            jax.ShapeDtypeStruct(hidden_f.shape, bf16),
+        ),
+    )
+    gathered, (d_after_mlp, grad_g_mamba) = found["gathered"], found["finish"]
+    out_mine, (grad_w_zx, grad_w_out) = found["second"], found["moves"]
 
     d_mlp, d_bc = gathered[:, :width], gathered[:, width:]
     grad_w_bc = outer_product_sum(xn, d_bc)
@@ -1533,17 +1720,18 @@
         [outer_product_sum(xm, d_gate).astype(bf16), outer_product_sum(xm, d_up).astype(bf16)]
     )
 
-    d_attn, d_after_attn, grad_g_mlp, grad_w_gu, grad_w_down = exchange(
+    found = exchange(
         sizes,
         6,
-        [(d_gate, w_gu, 0, True), (d_up, w_gu, 1, True)],
-        None,
+        Summed(sizes, [(d_gate, w_gu, 0, True), (d_up, w_gu, 1, True)]),
         finish_mlp_back,
         [after_attn, gain_m, d_after_mlp],
         [hidden_f.shape, gain_m.shape],
         width,
         [(grad_w_gu, 1, 2), (grad_w_down.astype(bf16), 1, 0)],
     )
+    d_attn, (d_after_attn, grad_g_mlp) = found["gathered"], found["finish"]
+    grad_w_gu, grad_w_down = found["moves"]
     grad_w_o = outer_product_sum(ao_low, d_attn)
     d_ao = matrix_product_transposed(d_attn, w_o).astype(bf16)
     d_proj = [
@@ -1558,21 +1746,19 @@
         [outer_product_sum(mid[:, j * rank : (j + 1) * rank], d_proj[j]) for j in range(3)]
     )
     shares = [
-        adapter_up_gradient,
-        grad_w_dt,
-        grad_conv_x,
-        grad_conv_x_bias,
-        grad_g_gate,
-        grad_dt_bias,
-        grad_a_log,
-        grad_d_skip,
+        jnp.pad(part, (0, 128 - part.shape[0]))[None]
+        for part in (grad_dt_bias, grad_a_log, grad_d_skip)
     ]
-    joins = (2, 1, 1, 0, 0, 0, 0, 0)
-    dmid, back, grad_g_attn, grad_w_qkv, grad_w_o, shared = exchange(
+    shares = jnp.concatenate(
+        [grad_conv_x, grad_conv_x_bias[None], grad_g_gate[None]] + shares
+        + [jnp.zeros((7, 128), f32), jnp.pad(grad_w_dt.T.reshape(-1, 128), ((0, 0), (0, 0)))]
+    ).astype(bf16)
+    sums = [grad_g_mlp[0], grad_g_mamba[0], grad_conv_bc, grad_conv_bc_bias]
+    row = jnp.concatenate([part.reshape(-1) for part in sums])[None]
+    found = exchange(
         sizes,
         7,
-        [(d_proj[j], w_qkv, j, True) for j in range(3)],
-        dmid_part,
+        Summed(sizes, [(d_proj[j], w_qkv, j, True) for j in range(3)], dmid_part),
         finish_attention_back,
         [
             hidden_f,
@@ -1581,52 +1767,51 @@
             d_after_attn,
             down_all,
             out_mine,
+            row,
         ],
-        [(1, width_a)],
+        [],
         3 * rank,
-        [(grad_w_qkv, 1, 2), (grad_w_o.astype(bf16), 1, 0), (pack(shares, bf16), None, 0)],
+        [
+            (grad_w_qkv, 1, 2),
+            (grad_w_o.astype(bf16), 1, 0),
+            (adapter_up_gradient.astype(bf16), None, 2),
+            (shares, None, 1),
+        ],
         early_share=100,
         tail=3 * width,
-    )
-    adapter_down_gradient = jnp.stack(
-        [outer_product_sum(xa, dmid[:, j * rank : (j + 1) * rank]) for j in range(3)]
-    )
+        small=width_a + row.shape[1],
+    )
+    dmid, back, row = found["gathered"], found["tail"], found["small"][0]
+    grad_w_qkv, grad_w_o, adapter_up_gradient, shared = found["moves"]
+    adapter_down_gradient = adapter_products(xa_wide, dmid, width_a)
     result = back[:, :width]
     d_hidden = back[:, width : 2 * width].astype(f32)
     d_embeds = back[:, 2 * width :].astype(f32)
-    (
-        adapter_up_gradient,
-        grad_w_dt,
-        grad_conv_x,
-        grad_conv_x_bias,
-        grad_g_gate,
-        grad_dt_bias,
-        grad_a_log,
-        grad_d_skip,
-    ) = [
-        jnp.concatenate(parts, axis=join).astype(f32)
-        for parts, join in zip(
-            zip(*[unpack(shared[i], shares) for i in range(plane_size)]), joins
-        )
+    adapter_up_gradient = adapter_up_gradient.astype(f32)
+    shared = shared.astype(f32)
+    grad_conv_x, grad_conv_x_bias, grad_g_gate = shared[:4], shared[4], shared[5]
+    few = step_bias.shape[0]
+    grad_dt_bias, grad_a_log, grad_d_skip = [
+        shared[i].reshape(plane_size, 128)[:, :few].reshape(-1) for i in (6, 7, 8)
     ]
-    sums = [grad_g_attn, grad_g_mlp, grad_g_mamba, grad_conv_bc, grad_conv_bc_bias]
-    grad_g_attn, grad_g_mlp, grad_g_mamba, grad_conv_bc, grad_conv_bc_bias = unpack(
-        sum_small(sizes, 8, pack(sums, f32)), sums
-    )
+    grad_w_dt = shared[16:].reshape(few, -1, plane_size, 128).transpose(1, 3, 2, 0)
+    grad_w_dt = grad_w_dt.reshape(-1, plane_size * few)
+    grad_g_attn = row[:width_a]
+    grad_g_mlp, grad_g_mamba, grad_conv_bc, grad_conv_bc_bias = unpack(row[width_a:], sums)
 
     return (
         result,
         d_hidden,
         d_embeds,
-        grad_g_attn[0],
+        grad_g_attn,
         adapter_down_gradient,
         grad_w_qkv.astype(f32),
         adapter_up_gradient,
         grad_w_o.astype(f32),
-        grad_g_mlp[0],
+        grad_g_mlp,
         grad_w_gu.astype(f32),
         grad_w_down.astype(f32),
-        grad_g_mamba[0],
+        grad_g_mamba,
         grad_w_zx.astype(f32),
         grad_w_bc,
         grad_w_dt,

time: 1340 us -> 1180 us (0.88)
  waiting for transfers between devices: 66.5 us -> 0 us
  local copies, waits for them, and re-layouts: 79.7 us -> 43 us
  matrix products: 178 us -> 142 us
  other arithmetic: 74.7 us -> 57.7 us
  between operations: 16.7 us -> 2.63 us
    reduce_scatter x1 -> x0, waiting for transfers between devices: 66.5 us -> none  [per_device_split(): lax.psum_scatter(out_part, EVERY, scatter_dimension=0, tiled=True)]
    dot_general x18 -> x15, matrix products: 76.8 us -> 45.4 us  [outer_product_sum(): lax.dot_general(left, right, (((0,), (0,)), ((), ())), preferred_element_...]
    dot_general x13 -> x12, matrix products: 52.7 us -> 46.7 us  [matrix_product(): return jnp.dot(left, right, preferred_element_type=jnp.float32)]
  transfers between devices with their start and end apart: 2 -> 0, of which waited for: 1 -> 0; matrix products, arithmetic and copies ran while one was open for 11% -> 0% of each run, Pallas kernels for 21% -> 0%
where the time goes in v3:
time: 1180 us; the launch traced here: 1170 us
  Pallas kernels  922 us (78%)
  matrix products  142 us (12%)
  other arithmetic  57.7 us (5%)
  local copies, waits for them, and re-layouts  43 us (4%)
    pallas_call x5, Pallas kernels, exchange(): pl.pallas_call(kernel, out_shape=out_shape, in_specs=in_specs, out_specs=...  749 us
    pallas_call x1, Pallas kernels, opening(): pl.pallas_call(kernel, out_shape=[S((groups, ctx, tp // 2, 2, rows, width...  146 us
    dot_general x12, matrix products, matrix_product(): return jnp.dot(left, right, preferred_element_type=jnp.float32)  46.7 us
    dot_general x15, matrix products, outer_product_sum(): lax.dot_general(left, right, (((0,), (0,)), ((), ())), preferred_element_...  45.4 us

profile of v3, /device:TPU:0, one launch (start us, length us, event | category | flops | bytes accessed | tf_op | source)
XLA Modules:
  0.0 1167.3 jit_solution(6933678680475165947)
XLA Ops:
  0.7 2.1 slice_bitcast_fusion.2
  2.8 2.1 pad_maximum_fusion.refs_4_.refs_9_
  4.9 145.8 %opening_1.1 = (bf16[4,2,2,2,48,4608]{5,4,3,2,1,0:T(8,128)(2,1)}, bf16[3,4096,128]{2,1,0:T(8,128)(2,1)}, bf16[128,2048]{1,0:T(8,128)(2,1)}) custom-call(bf16[192,2048]{1,0:T(8,128)(2,1)} %refs_0_.1, bf16[192,2048]{1,0:T(8,128)(2,1)} %refs_1_.1, s32[1,3]{1,0:T(1,128)} %refs_2_.1, f32[1,4096]{1,0:T(1,128)} %bitcast.311, ...), custom_call_target="tpu_custom_call" | custom-call | tf_op jit(solution)/shard_map/opening_1/pallas_call | solution.py:1323
  150.7 6.8 fusion.12
  158.8 6.7 fusion.14
  166.8 1.9 convert_reduce_fusion.2
  168.8 4.5 fusion.145
  173.3 1.6 convert_reduce_fusion.3
  175.0 2.4 fusion.214
  179.1 7.1 fusion.10
  188.8 2.0 dynamic-slice_convert_fusion
  190.8 148.7 %exchange_2.1 = (bf16[4,2,2,2,48,2048]{5,4,3,2,1,0:T(8,128)(2,1)}, f32[48,2048]{1,0:T(8,128)}, bf16[2,2048,256]{2,1,0:T(8,128)(2,1)}, bf16[256,2048]{1,0:T(8,128)(2,1)}) custom-call(bf16[4,2,2,2,48,128]{5,4,3,2,1,0:T(8,128)(2,1)} %bitcast.275, bf16[128,2048]{1,0:T(8,128)(2,1)} %get-tuple-element.56.refs_1_, f32[48,2048]{1,0:T(8,128)} %get-tuple-element.176.refs_2_.refs_5_, ...), custom_call_target="tpu_custom_call" | custom-call | tf_op jit(solution)/shard_map/exchange_2/pallas_call | solution.py:1224
  339.5 5.1 fusion.127
  345.0 3.6 multiply_convert_fusion.1
  348.6 1.6 constant_dynamic-slice_fusion.2.refs_4_.refs_8_
  350.3 131.9 %exchange_3.1 = (bf16[4,2,2,2,48,2048]{5,4,3,2,1,0:T(8,128)(2,1)}, f32[48,2048]{1,0:T(8,128)}, bf16[4,2,2,2,48,2048]{5,4,3,2,1,0:T(8,128)(2,1)}, bf16[2,2048,128]{2,1,0:T(8,128)(2,1)}, bf16[128,2048]{1,0:T(8,128)(2,1)}) custom-call(bf16[4,2,2,2,48,256]{5,4,3,2,1,0:T(8,128)(2,1)} %bitcast.305, bf16[256,2048]{1,0:T(8,128)(2,1)} %get-tuple-element.59.refs_1_, ...), custom_call_target="tpu_custom_call" | custom-call | tf_op jit(solution)/shard_map/exchange_3/pallas_call | solution.py:1224
  483.0 5.3 compare_select_fusion.2
  489.4 1.9 fusion.45
  491.3 2.8 fusion.88
  495.2 2.5 fusion.215
  497.7 1.8 fusion.51
  501.1 1.8 fusion.162
  503.9 2.0 copy.111
  508.2 6.5 fusion.101
  514.7 2.9 copy.154
  517.6 1.8 reshape.445
  519.3 4.8 fusion.166
  524.9 5.6 multiply_reduce_fusion.13
  531.2 14.5 %sum_small_4.1 = f32[24,128]{1,0:T(8,128)} custom-call(f32[24,128]{1,0:T(8,128)} %reshape.396.x), custom_call_target="tpu_custom_call" | custom-call | tf_op jit(solution)/shard_map/sum_small_4/pallas_call | solution.py:1349
  547.1 2.8 multiply_reduce_fusion.5
  549.9 4.9 convolution_convert_fusion.7.refs_14_
  554.8 5.4 fusion.68
  561.1 1.9 copy.120
  563.3 5.9 multiply_reduce_fusion.11
  569.2 3.4 copy.155
  572.6 3.0 reshape.446
  575.6 3.4 multiply_reduce_fusion.10
  580.5 1.8 fusion.69
  583.5 4.7 fusion.41
  589.4 2.1 fusion.217
  591.6 1.9 multiply_reduce_fusion.4
  600.0 143.7 %exchange_5.1 = (bf16[4,2,2,2,48,2304]{5,4,3,2,1,0:T(8,128)(2,1)}, f32[48,2048]{1,0:T(8,128)}, f32[1,2048]{1,0:T(1,128)}, bf16[48,2048]{1,0:T(8,128)(2,1)}, bf16...) custom-call(bf16[4,2,2,2,48,128]{5,4,3,2,1,0:T(8,128)(2,1)} %bitcast.295, bf16[4,2,2,2,48,128]{5,4,3,2,1,0:T(8,128)(2,1)} %bitcast.297, ...), custom_call_target="tpu_custom_call" | custom-call | tf_op jit(solution)/shard_map/exchange_5/pallas_call | solution.py:1224
  743.7 6.2 fusion.159
  749.9 3.8 convolution_convert_fusion.12
  754.1 1.8 concatenate.26.refs_15_
  755.9 5.7 fusion.42.refs_7_
  761.6 5.9 multiply_convert_fusion
  767.6 2.0 fusion.46
  769.6 2.2 fusion.47
  771.8 1.5 pad_maximum_fusion.2.refs_6_
  773.3 144.1 %exchange_6.1 = (bf16[4,2,2,2,48,2048]{5,4,3,2,1,0:T(8,128)(2,1)}, f32[48,2048]{1,0:T(8,128)}, f32[1,2048]{1,0:T(1,128)}, bf16[2,256,2048]{2,1,0:T(8,128)(2,1)}, bf16[2048,256]{1,0:T(8,128)(2,1)}) custom-call(bf16[4,2,2,2,48,256]{5,4,3,2,1,0:T(8,128)(2,1)} %bitcast.304, bf16[4,2,2,2,48,256]{5,4,3,2,1,0:T(8,128)(2,1)} %bitcast.303, ...), custom_call_target="tpu_custom_call" | custom-call | tf_op jit(solution)/shard_map/exchange_6/pallas_call | solution.py:1224
  917.4 4.7 convolution_convert_fusion.10
  926.2 3.9 fusion.154
  933.0 1.8 convolution_convert_fusion.3.refs_13_
  934.8 3.5 fusion.37
  938.3 3.5 fusion.34
  941.8 3.7 fusion.31
  945.5 2.0 pad_maximum_fusion.1.refs_12_
  950.5 180.5 %exchange_7.1 = (bf16[4,2,2,2,48,384]{5,4,3,2,1,0:T(8,128)(2,1)}, bf16[2,2,48,6144]{3,2,1,0:T(8,128)(2,1)}, f32[1,9472]{1,0:T(1,128)}, bf16[3,512,1024]{2,1,0:T(...) custom-call(bf16[4,2,2,2,48,128]{5,4,3,2,1,0:T(8,128)(2,1)} %bitcast.280, ...), custom_call_target="tpu_custom_call" | custom-call | tf_op jit(solution)/shard_map/exchange_7/pallas_call | solution.py:1224
  1131.0 13.2 %adapter_products.1 = f32[3,4096,128]{2,1,0:T(8,128)} custom-call(bf16[1536,4608]{1,0:T(8,128)(2,1)} %bitcast.254, bf16[1536,384]{1,0:T(8,128)(2,1)} %bitcast.302), custom_call_target="tpu_custom_call" | custom-call | tf_op jit(solution)/shard_map/adapter_products/pallas_call | solution.py:1432
  1144.2 5.5 convert_element_type.346
  1149.7 2.1 slice_convert_fusion
  1160.4 2.5 convert_element_type.349
  1164.5 1.6 convert_element_type.351
  (340 shorter events, 50.3 us)
Async XLA Ops:
  0.7 156.8 %copy-start = (bf16[3,128,1024]{2,1,0:T(8,128)(2,1)S(1)}, bf16[3,128,1024]{2,1,0:T(8,128)(2,1)}, u32[]{:S(2)}) copy-start(bf16[3,128,1024]{2,1,0:T(8,128)(2,1)} %param.32) | copy-start | bytes 2359300
  168.8 332.3 %copy-start.49 = (f32[1536]{0:T(1024)}, f32[1536]{0:T(1024)S(1)}, u32[]{:S(2)}) copy-start(f32[1536]{0:T(1024)S(1)} %get-tuple-element.86) | copy-start | bytes 18436
  168.8 4.5 copy-start.65
  168.8 4.5 copy-start.92
  173.3 4.1 copy-start.53
  173.3 4.1 copy-start.55
  174.9 330.9 %copy-start.63 = (s32[4,384]{1,0:T(4,128)}, s32[4,384]{1,0:T(4,128)S(1)}, u32[]{:S(2)}) copy-start(s32[4,384]{1,0:T(4,128)S(1)} %reshape.434) | copy-start | bytes 18436
  175.0 330.9 %copy-start.42 = (pred[384,384]{0,1:T(8,128)(4,1)}, pred[384,384]{0,1:T(8,128)(4,1)S(1)}, u32[]{:S(2)}) copy-start(pred[384,384]{0,1:T(8,128)(4,1)S(1)} %iota_compare_fusion) | copy-start | bytes 442372
  177.5 8.8 copy-start.68
  179.1 8.4 copy-start.2
  339.5 5.1 copy-start.24
  339.5 5.5 copy-start.98
  345.0 3.6 copy-start.104
  348.6 134.3 %copy-start.99 = (f32[16]{0:T(128)S(1)}, f32[16]{0:T(128)}, u32[]{:S(2)}) copy-start(f32[16]{0:T(128)} %param.45) | copy-start | bytes 196
  482.9 5.4 copy-start.60
  483.0 5.3 copy-start.96
  483.0 6.3 copy-start.1
  483.0 6.3 copy-start.28
  488.3 19.2 %copy-start.70 = (f32[1536,2]{0,1:T(2,128)}, f32[1536,2]{0,1:T(2,128)S(1)}, u32[]{:S(2)}) copy-start(f32[1536,2]{0,1:T(2,128)S(1)} %get-tuple-element.170) | copy-start | bytes 36868
  489.3 18.1 %copy-start.107 = (f32[4,2,384]{2,1,0:T(2,128)}, f32[4,2,384]{2,1,0:T(2,128)S(1)}, u32[]{:S(2)}) copy-start(f32[4,2,384]{2,1,0:T(2,128)S(1)} %fusion.188) | copy-start | bytes 36868
  500.3 3.5 copy-start.82
  500.3 3.5 copy-start.84
  500.3 3.5 copy-start.86
  500.3 3.5 copy-start.88
  503.9 3.5 copy-start.100
  508.2 6.5 copy-start.103
  519.3 5.6 copy-start.21
  519.3 5.6 copy-start.46
  524.1 6.4 copy-start.39
  549.9 4.9 copy-start.13
  549.9 4.9 copy-start.26
  563.3 5.9 copy-start.51
  569.2 6.5 copy-start.50
  569.2 11.2 slice-start
  572.6 6.5 copy-start.83
  572.6 6.5 copy-start.85
  572.6 6.5 copy-start.87
  575.6 4.8 slice-start.1
  583.5 4.8 copy-start.9
  749.9 3.8 copy-start.97
  749.9 3.9 copy-start.95
  749.9 4.2 copy-start.91
  749.9 6.0 copy-start.38
  755.9 5.7 copy-start.32
  755.9 5.7 copy-start.105
  755.9 5.7 copy-start.106
  755.9 11.7 %slice-start.8 = ((s8[6291456]{0:T(1024)(128)(4,1)}), s8[4194304]{0:T(1024)(128)(4,1)S(1)}, s32[]{:S(2)}) async-start(s8[6291456]{0:T(1024)(128)(4,1)} %bitcast.358), calls=%async_computation.8 | async-start | bytes 8388608
  761.6 6.0 slice-start.9
  773.3 144.1 %copy-start.44 = (bf16[128,2048]{1,0:T(8,128)(2,1)S(1)}, bf16[128,2048]{1,0:T(8,128)(2,1)}, u32[]{:S(2)}) copy-start(bf16[128,2048]{1,0:T(8,128)(2,1)} %get-tuple-element.56.refs_1_) | copy-start | bytes 1572868
  917.4 4.8 copy-start.69
  917.4 4.8 copy-start.5
  917.4 4.8 copy-start.19
  923.3 7.1 slice-start.2
  923.3 7.1 slice-start.3
  924.9 5.6 slice-start.4
  924.9 5.6 slice-start.5
  924.9 8.1 slice-start.6
  926.2 6.8 slice-start.7
  930.4 18.3 %copy-start.15 = (bf16[4,384,128]{2,1,0:T(8,128)(2,1)}, bf16[4,384,128]{2,1,0:T(8,128)(2,1)S(1)}, u32[]{:S(2)}) copy-start(bf16[4,384,128]{2,1,0:T(8,128)(2,1)S(1)} %add_convert_fusion.1) | copy-start | bytes 1179652
  931.1 17.4 %copy-start.16 = (bf16[4,384,128]{2,1,0:T(8,128)(2,1)}, bf16[4,384,128]{2,1,0:T(8,128)(2,1)S(1)}, u32[]{:S(2)}) copy-start(bf16[4,384,128]{2,1,0:T(8,128)(2,1)S(1)} %add_convert_fusion) | copy-start | bytes 1179652
  932.0 16.2 %copy-start.17 = (bf16[4,384,128]{2,1,0:T(8,128)(2,1)}, bf16[4,384,128]{2,1,0:T(8,128)(2,1)S(1)}, u32[]{:S(2)}) copy-start(bf16[4,384,128]{2,1,0:T(8,128)(2,1)S(1)} %convolution_convert_fusion.15) | copy-start | bytes 1179652
  1144.2 5.5 copy-start.22
  1151.8 5.6 copy-start.67
  1151.8 8.6 copy-start.25
  (56 other events, 115.8 us)

commit v4 on v3

--- a/solution.py
+++ b/solution.py
@@ -674,7 +674,7 @@
             cut(dst, join, origin, dst.shape[join] // n),
         )
 
-    def start(self):
+    def start(self, first=0):
         place = self.place
         self.loads, self.queue = [], []
         for i in range(len(self.specs)):
@@ -683,6 +683,7 @@
             load = pltpu.make_async_copy(src, self.stages[i], self.local.at[i, 0])
             load.start()
             self.loads.append(load)
+        self.queue.sort(key=lambda one: one[1] % place.ctx != first)
 
     def issue(self, count):
         for i, d in self.queue[:count]:
@@ -1075,7 +1076,7 @@
     finish_outs,
     gathered,
     moves,
-    early_share=60,
+    early_share=22,
     also_gather=None,
     also_sum=None,
     tail=0,
@@ -1174,11 +1175,10 @@
             ends.append(side_sum)
         total = n_moves * (groups * ctx - 1)
         steps = weave(*streams)
-        per_step = -(-total * early_share // (100 * len(steps)))
+        if carried is not None:
+            carried.issue(total * early_share // 100)
         for step in steps:
             step()
-            if carried is not None:
-                carried.issue(per_step)
         if carried is not None:
             carried.settle()
         low_tail = scr[s_tail][0] if tail else None
@@ -1199,11 +1199,9 @@
             to_y.start()
             own.wait()
         steps = weave((0, main_gather.steps()), *later)
-        left = 0 if carried is None else len(carried.queue)
-        per_step = -(-left // max(1, len(steps) - 2))
+        if carried is not None:
+            carried.issue(total)
         for step in steps:
-            if carried is not None:
-                carried.issue(per_step)
             step()
         if tail:
             to_y.wait_recv()
@@ -1218,7 +1216,6 @@
         for stage in ends:
             stage.end()
         if carried is not None:
-            carried.issue(total)
             carried.finish()
 
     results = pl.pallas_call(
@@ -1286,8 +1283,7 @@
             + [place.plane_peer(d)[1] for d in range(1, place.plane)]
         )
         carried = Moves(place, move_specs, sources, targets, stages, send, recv, local)
-        carried.start()
-        carried.issue(2)
+        carried.start(1)
         mine = pl.ds(pl.multiple_of(place.t * rows, 16), rows)
         a, b = hid[mine, :].astype(f32), emb[mine, :].astype(f32)
         squares = jnp.sum(a * a, axis=1, keepdims=True) + jnp.sum(b * b, axis=1, keepdims=True)
@@ -1311,10 +1307,9 @@
         low[:, 2 * half + mids :] = marks.astype(f32).astype(bf16)
         gather = Gather(place, low, o, out_pieces, gs)
         gather.begin()
+        carried.issue(len(carried.queue))
         for step in gather.steps():
-            carried.issue(4)
             step()
-        carried.issue(len(carried.queue))
         carried.settle()
         gather.end()
         carried.finish()
@@ -1450,15 +1445,6 @@
     return found
 
 
-def shift_conv(values, kernel, bias, position):
-    total = values * kernel[0][None, :] + bias[None, :]
-    for lag in range(1, kernel.shape[0]):
-        shifted = jnp.pad(values, ((lag, 0), (0, 0)))[: values.shape[0]]
-        keep = (position >= lag).astype(values.dtype)[:, None]
-        total = total + shifted * keep * kernel[lag][None, :]
-    return jax.nn.silu(total)
-
-
 def attend_groups(queries, keys_all, vals_all, segment, position):
     def rot(values):
         half_dim = values.shape[-1] // 2
@@ -1483,32 +1469,293 @@
     )
 
 
-def mixer_groups(
-    inner_in, step_in, bc_post, bias_in, decay_in, skip_in, kernel_in, conv_bias_in, position, segment
-):
-    groups, rows = segment.shape
-    heads = step_in.shape[1]
-    xc = shift_conv(inner_in, kernel_in, conv_bias_in, position.reshape(-1))
-    xc = xc.reshape(groups, rows, heads, MIXER_HEAD_SIZE)
-    step = jax.nn.softplus(step_in + bias_in[None, :]).reshape(groups, rows, heads)
-    log_decay = step * -jnp.exp(decay_in)
-    order = jnp.arange(rows)
-    same = (segment[:, :, None] == segment[:, None, :]) & (order[:, None] >= order[None, :])
-    running = jnp.einsum("gts,gsh->gth", same.astype(jnp.float32), log_decay, precision=highest)
-    gap = running.transpose(0, 2, 1)
-    gap = gap[:, :, :, None] - gap[:, :, None, :]
-    decay = jnp.where(same[:, None], jnp.exp(jnp.where(same[:, None], gap, 0.0)), 0.0)
-    b_mat = bc_post[:, :STATE].reshape(groups, rows, STATE)
-    c_mat = bc_post[:, STATE:].reshape(groups, rows, STATE)
-    meet = jnp.einsum("gtn,gsn->gts", c_mat, b_mat, precision=lax.Precision.HIGH)
-    out = jnp.einsum(
-        "ghts,gshp->gthp",
-        decay * meet[:, None],
-        xc * step[..., None],
-        precision=lax.Precision.HIGH,
-    )
-    out = out + skip_in[:, None] * xc
-    return out.reshape(groups * rows, heads * MIXER_HEAD_SIZE)
+TN = (((0,), (0,)), ((), ()))
+
+
+def exact(left, right, dims):
+    return lax.dot_general(left, right, dims, precision=highest, preferred_element_type=jnp.float32)
+
+
+def quick(left, right, dims):
+    return lax.dot_general(left, right, dims, preferred_element_type=jnp.float32)
+
+
+def down_rows(values, by):
+    return pltpu.roll(values, by, 0)
+
+
+def up_rows(values, by):
+    return pltpu.roll(values, values.shape[0] - by, 0)
+
+
+def taps_forward(values, taps, bias, position):
+    total = values * taps[0:1, :] + bias
+    for lag in range(1, taps.shape[0]):
+        kept = jnp.where(position >= lag, down_rows(values, lag), 0.0)
+        total = total + kept * taps[lag : lag + 1, :]
+    return total
+
+
+def taps_backward(d_total, values, taps, position):
+    d_values = d_total * taps[0:1, :]
+    rows = [jnp.sum(d_total * values, axis=0, keepdims=True)]
+    for lag in range(1, taps.shape[0]):
+        kept = jnp.where(position >= lag, d_total, 0.0)
+        rows.append(jnp.sum(kept * down_rows(values, lag), axis=0, keepdims=True))
+        d_values = d_values + up_rows(kept, lag) * taps[lag : lag + 1, :]
+    return d_values, rows + [jnp.sum(d_total, axis=0, keepdims=True)]
+
+
+def silu_slope(values):
+    sigmoid = jax.nn.sigmoid(values)
+    return sigmoid * (1.0 + values * (1.0 - sigmoid))
+
+
+class Scan:
+    def __init__(self, xs, raw, bc, marks, taps, bias, bc_taps, bc_bias, heads):
+        f32 = jnp.float32
+        rows, lanes = xs.shape
+        self.rows, self.half = rows, lanes // 2
+        self.position = marks[:, 1:2].astype(f32)
+        self.lane = lax.broadcasted_iota(jnp.int32, (rows, lanes), 1)
+        self.xs, self.bc = xs.astype(f32), bc.astype(f32)
+        self.pre_x = taps_forward(self.xs, taps, bias, self.position)
+        self.pre_bc = taps_forward(self.bc, bc_taps, bc_bias, self.position)
+        self.xc, bcc = jax.nn.silu(self.pre_x), jax.nn.silu(self.pre_bc)
+        self.b_mat, self.c_mat = bcc[:, :STATE], bcc[:, STATE:]
+        self.step_in = raw.astype(f32) + heads[0:1, :]
+        self.dt = jax.nn.softplus(self.step_in)
+        self.rate = -jnp.exp(heads[1:2, :])
+        self.log_decay = self.dt * self.rate
+        running, by = self.log_decay, 1
+        while by < rows:
+            running = running + jnp.where(self.position >= by, down_rows(running, by), 0.0)
+            by *= 2
+        self.running = running
+        self.across = running.T
+        row = lax.broadcasted_iota(jnp.int32, (rows, rows), 0)
+        col = lax.broadcasted_iota(jnp.int32, (rows, rows), 1)
+        first = row.astype(f32) - self.position
+        self.same = (col <= row) & (col.astype(f32) >= first)
+        self.meet = exact(self.c_mat, self.b_mat, NT)
+        self.dt_wide = self.by_head([self.dt[:, h : h + 1] for h in range(2)])
+        self.weighted = self.xc * self.dt_wide
+
+    def by_head(self, values):
+        return jnp.where(self.lane < self.half, values[0], values[1])
+
+    def in_lane(self, values):
+        return jnp.where(self.lane == 0, values[0], jnp.where(self.lane == 1, values[1], 0.0))
+
+    def decay(self, h):
+        gap = self.running[:, h : h + 1] - self.across[h : h + 1, :]
+        return jnp.where(self.same, jnp.exp(jnp.where(self.same, gap, 0.0)), 0.0)
+
+    def forward(self, skip):
+        outs = [exact(self.decay(h) * self.meet, self.weighted, NN) for h in range(2)]
+        return self.by_head(outs) + skip * self.xc
+
+    def to_ends(self, values):
+        rows = values.shape[0]
+        row = lax.broadcasted_iota(jnp.int32, values.shape, 0)
+        wide = jnp.broadcast_to(self.position, values.shape)
+        by = 1
+        while by < rows:
+            inside = (up_rows(wide, by) >= by) & (row < rows - by)
+            values = values + jnp.where(inside, up_rows(values, by), 0.0)
+            by *= 2
+        return values
+
+
+def mixer_forward(xn, cot, marked, mark_block, w_zx, w_step, state_map, w_out, small, bc_small, groups):
+    f32, bf16 = jnp.float32, jnp.bfloat16
+    total, width = xn.shape
+    rows, lanes = total // groups, w_zx.shape[2]
+    state2 = state_map.shape[1]
+
+    def kernel(xn_r, cot_r, marks_r, zx_r, st_r, sm_r, wo_r, sml, bsml, z_o, xs_o, raw_o, bc_o, y_o, dyn_o, sums_o):
+        x = xn_r[...]
+        z = quick(x, zx_r[0], NN)
+        xs = quick(x, zx_r[1], NN).astype(bf16)
+        raw = quick(x, st_r[...], NN).astype(bf16)
+        bc = quick(x, sm_r[...], NN).astype(bf16)
+        z_o[...], xs_o[...], raw_o[...], bc_o[...] = z, xs, raw, bc
+        scan = Scan(
+            xs, raw, bc, marks_r[...].astype(f32), sml[0:4, :], sml[4:5, :], bsml[0:4, :], bsml[4:5, :], sml[8:10, :]
+        )
+        y = scan.forward(sml[5:6, :]).astype(bf16)
+        y_o[...] = y
+        gated = y.astype(f32) * jax.nn.silu(z)
+        d_yn = quick(cot_r[...], wo_r[...], NT)
+        dyn_o[...] = d_yn
+        ones = jnp.ones((8, lanes), f32)
+        sums_o[0, 0:1] = exact(ones, gated * gated, NT)[0:1]
+        sums_o[0, 1:2] = exact(ones, d_yn * sml[6:7, :] * gated, NT)[0:1]
+
+    def by_group(columns):
+        return pl.BlockSpec((rows, columns), lambda g: (g, 0))
+
+    def whole(array):
+        return pl.BlockSpec(array.shape, lambda g: (0,) * array.ndim)
+
+    S = jax.ShapeDtypeStruct
+    return pl.pallas_call(
+        kernel,
+        grid=(groups,),
+        in_specs=[by_group(width), by_group(width), pl.BlockSpec((rows, 128), lambda g: (g, mark_block))]
+        + [whole(array) for array in (w_zx, w_step, state_map, w_out, small, bc_small)],
+        out_specs=[by_group(lanes)] * 3
+        + [by_group(state2), by_group(lanes), by_group(lanes), pl.BlockSpec((1, 2, rows), lambda g: (g, 0, 0))],
+        out_shape=[
+            S((total, lanes), f32),
+            S((total, lanes), bf16),
+            S((total, lanes), bf16),
+            S((total, state2), bf16),
+            S((total, lanes), bf16),
+            S((total, lanes), f32),
+            S((groups, 2, rows), f32),
+        ],
+        compiler_params=pltpu.CompilerParams(vmem_limit_bytes=60 * 2**20),
+        name="mixer_forward",
+    )(xn, cot, marked, w_zx, w_step, state_map, w_out, small, bc_small)
+
+
+def mixer_backward(xn, cot, marked, mark_block, kept, sums, small, bc_small, groups):
+    f32, bf16 = jnp.float32, jnp.bfloat16
+    z, xs, raw, bc, y, d_yn = kept
+    total, width = xn.shape
+    rows, lanes, state2 = total // groups, z.shape[1], bc.shape[1]
+
+    def kernel(
+        xn_r, cot_r, marks_r, z_r, xs_r, raw_r, bc_r, y_r, dyn_r, sums_r, sml, bsml,
+        dz_o, dxs_o, draw_o, dbc_o, yn_o, gzx_o, gst_o, gout_o, gsm_o, gbc_o, acc_in, acc_out,
+    ):
+        group = pl.program_id(0)
+        scan = Scan(
+            xs_r[...], raw_r[...], bc_r[...], marks_r[...].astype(f32),
+            sml[0:4, :], sml[4:5, :], bsml[0:4, :], bsml[4:5, :], sml[8:10, :],
+        )
+        skip, gain = sml[5:6, :], sml[6:7, :]
+        sums_wide = [jnp.broadcast_to(sums_r[0, i : i + 1], (128, rows)).T for i in range(2)]
+        inverse = lax.rsqrt(sums_wide[0] / INNER + epsilon)
+        cross = sums_wide[1] / INNER
+        gate, out, d_normed = z_r[...], y_r[...].astype(f32), dyn_r[...]
+        silu_z = jax.nn.silu(gate)
+        gated = out * silu_z
+        yn = (gated * inverse * gain).astype(bf16)
+        yn_o[...] = yn
+        g_gate = jnp.sum(d_normed * gated * inverse, axis=0, keepdims=True)
+        d_gated = d_normed * gain * inverse - gated * inverse**3 * cross
+        d_y = (d_gated * silu_z).astype(bf16).astype(f32)
+        d_z = (d_gated * out * silu_slope(gate)).astype(bf16)
+        dz_o[...] = d_z
+        g_skip = jnp.sum(d_y * scan.xc, axis=0, keepdims=True)
+        d_weighted, d_meet = jnp.zeros_like(d_y), jnp.zeros_like(scan.meet)
+        by_row, by_col = [], []
+        for h in range(2):
+            mine = (scan.lane < scan.half) if h == 0 else (scan.lane >= scan.half)
+            d_head = jnp.where(mine, d_y, 0.0)
+            decay = scan.decay(h)
+            mixing = decay * scan.meet
+            d_mixing = exact(d_head, scan.weighted, NT)
+            d_weighted = d_weighted + exact(mixing, d_head, TN)
+            d_meet = d_meet + d_mixing * decay
+            moved = d_mixing * mixing
+            by_row.append(jnp.sum(moved, axis=1, keepdims=True))
+            by_col.append(jnp.sum(moved, axis=0, keepdims=True))
+        columns = [jnp.broadcast_to(by_col[h], (128, rows)).T for h in range(2)]
+        d_running = scan.in_lane([by_row[h] - columns[h] for h in range(2)])
+        d_log = scan.to_ends(d_running)
+        shared = d_weighted * scan.xc
+        d_dt = scan.in_lane(
+            [
+                jnp.sum(jnp.where(scan.lane < scan.half, shared, 0.0), axis=1, keepdims=True),
+                jnp.sum(jnp.where(scan.lane >= scan.half, shared, 0.0), axis=1, keepdims=True),
+            ]
+        )
+        d_step = (d_dt + d_log * scan.rate) * jax.nn.sigmoid(scan.step_in)
+        g_bias = jnp.sum(d_step, axis=0, keepdims=True)
+        g_decay = jnp.sum(d_log * scan.log_decay, axis=0, keepdims=True)
+        d_raw = d_step.astype(bf16)
+        draw_o[...] = d_raw
+        d_xc = skip * d_y + d_weighted * scan.dt_wide
+        d_xs, g_taps = taps_backward(
+            d_xc * silu_slope(scan.pre_x), scan.xs, sml[0:4, :], scan.position
+        )
+        d_xs = d_xs.astype(bf16)
+        dxs_o[...] = d_xs
+        d_bcc = jnp.concatenate(
+            [exact(d_meet, scan.c_mat, TN), exact(d_meet, scan.b_mat, NN)], axis=1
+        )
+        d_bc, g_bc_taps = taps_backward(
+            d_bcc * silu_slope(scan.pre_bc), scan.bc, bsml[0:4, :], scan.position
+        )
+        dbc_o[...] = d_bc.astype(bf16)
+        in_part = quick(jnp.concatenate([d_z, d_xs, d_raw], axis=1), xn_r[...], TN)
+        out_part = quick(yn, cot_r[...], TN)
+        blank = jnp.zeros((1, lanes), f32)
+        few = jnp.concatenate(
+            g_taps + [g_gate, g_bias, g_decay, g_skip] + [blank] * 7, axis=0
+        )
+        few_bc = jnp.concatenate(g_bc_taps + [jnp.zeros((3, state2), f32)], axis=0)
+
+        @pl.when(group == 0)
+        def _():
+            acc_in[...], acc_out[...] = in_part, out_part
+            gsm_o[...], gbc_o[...] = few, few_bc
+
+        @pl.when(group > 0)
+        def _():
+            acc_in[...] += in_part
+            acc_out[...] += out_part
+            gsm_o[...] += few
+            gbc_o[...] += few_bc
+
+        @pl.when(group == groups - 1)
+        def _():
+            for i in range(2):
+                gzx_o[i] = acc_in[i * lanes : (i + 1) * lanes, :].T.astype(bf16)
+            gst_o[...] = acc_in[2 * lanes : 2 * lanes + 8, :]
+            gout_o[...] = acc_out[...].astype(bf16)
+
+    def by_group(columns):
+        return pl.BlockSpec((rows, columns), lambda g: (g, 0))
+
+    def whole(shape):
+        return pl.BlockSpec(shape, lambda g: (0,) * len(shape))
+
+    S = jax.ShapeDtypeStruct
+    return pl.pallas_call(
+        kernel,
+        grid=(groups,),
+        in_specs=[by_group(width), by_group(width), pl.BlockSpec((rows, 128), lambda g: (g, mark_block))]
+        + [by_group(array.shape[1]) for array in kept]
+        + [pl.BlockSpec((1, 2, rows), lambda g: (g, 0, 0)), whole(small.shape), whole(bc_small.shape)],
+        out_specs=[by_group(lanes)] * 3
+        + [by_group(state2), by_group(lanes)]
+        + [
+            whole((2, width, lanes)),
+            whole((8, width)),
+            whole((lanes, width)),
+            whole((16, lanes)),
+            whole((8, state2)),
+        ],
+        out_shape=[
+            S((total, lanes), bf16),
+            S((total, lanes), bf16),
+            S((total, lanes), bf16),
+            S((total, state2), bf16),
+            S((total, lanes), bf16),
+            S((2, width, lanes), bf16),
+            S((8, width), f32),
+            S((lanes, width), bf16),
+            S((16, lanes), f32),
+            S((8, state2), f32),
+        ],
+        scratch_shapes=[pltpu.VMEM((3 * lanes, width), f32), pltpu.VMEM((lanes, width), f32)],
+        compiler_params=pltpu.CompilerParams(vmem_limit_bytes=60 * 2**20),
+        name="mixer_backward",
+    )(xn, cot, marked, z, xs, raw, bc, y, d_yn, sums, small, bc_small)
 
 
 def per_device_split(
@@ -1571,7 +1818,7 @@
     rank = adapter_down_maps.shape[2]
     width_a = adapter_down_maps.shape[1]
     down_all = jnp.concatenate([adapter_down_maps[j] for j in range(3)], axis=1)
-    xa_wide, w_qkv, w_o = opening(
+    xa_wide, w_o, w_qkv = opening(
         sizes,
         1,
         hidden,
@@ -1579,13 +1826,12 @@
         lengths,
         attention_norm_gain,
         down_all,
-        [(query_key_value_weight, 2, 1), (attention_output_weight, 0, 1)],
+        [(attention_output_weight, 0, 1), (query_key_value_weight, 2, 1)],
     )
     xa = xa_wide[:, :width_a]
     mid = xa_wide[:, width_a : width_a + 3 * rank]
     segment = xa_wide[:, width_a + 3 * rank].astype(jnp.int32).reshape(groups, group_rows)
     position = xa_wide[:, width_a + 3 * rank + 1].astype(jnp.int32).reshape(groups, group_rows)
-    position_flat = position.reshape(-1)
     proj = [
         (
             matrix_product(xa, w_qkv[j])
@@ -1625,65 +1871,36 @@
         [hidden_f.shape],
         width,
         [(mixer_gate_input_weight, 2, 1), (mixer_output_weight, 0, 1)],
+        early_share=0,
         also_gather=cot_low,
     )
     xn, cot, (after_mlp,) = found["gathered"], found["also"], found["finish"]
     w_zx, w_out = found["moves"]
-    gate_z = matrix_product(xn, w_zx[0])
-    inner_x = matrix_product(xn, w_zx[1]).astype(bf16)
-    step_raw = matrix_product(xn, w_step).astype(bf16)
-    bc_low = matrix_product(xn, state_map_weight).astype(bf16)
-    bc_post, bc_conv_back = jax.vjp(
-        lambda v, k, b: shift_conv(v, k, b, position_flat),
-        bc_low.astype(f32),
-        state_map_taps,
-        state_map_tap_bias,
-    )
-    scan_out, scan_back = jax.vjp(
-        lambda *parts: mixer_groups(*parts, position, segment),
-        inner_x.astype(f32),
-        step_raw.astype(f32),
-        bc_post,
-        step_bias,
-        decay_rate,
-        skip,
-        taps,
-        tap_bias,
-    )
-    y = scan_out.astype(bf16).astype(f32)
-    silu_z = jax.nn.silu(gate_z)
-    gated = y * silu_z
-    d_yn = matrix_product_transposed(cot, w_out)
-    gain_part = d_yn * gate_gain
-    sums = jnp.stack([jnp.sum(gated * gated, axis=1), jnp.sum(gain_part * gated, axis=1)])
-    sums = sum_small(sizes, 4, sums.reshape(-1, 128)).reshape(2, -1)
-    inverse = lax.rsqrt(sums[0] / INNER + epsilon)[:, None]
-    cross = (sums[1] / INNER)[:, None]
-    yn_low = (gated * inverse * gate_gain).astype(bf16)
-
-    grad_w_out = outer_product_sum(yn_low, cot)
-    grad_g_gate = jnp.sum(d_yn * gated * inverse, axis=0)
-    d_gated = gain_part * inverse - gated * inverse**3 * cross
-    d_y = (d_gated * silu_z).astype(bf16)
-    sigmoid_z = jax.nn.sigmoid(gate_z)
-    d_z = (d_gated * y * sigmoid_z * (1.0 + gate_z * (1.0 - sigmoid_z))).astype(bf16)
-    (
-        d_xs,
-        d_step,
-        d_bc_post,
-        grad_dt_bias,
-        grad_a_log,
-        grad_d_skip,
-        grad_conv_x,
-        grad_conv_x_bias,
-    ) = scan_back(d_y.astype(f32))
-    d_xs, d_step = d_xs.astype(bf16), d_step.astype(bf16)
-    d_bc_part, grad_conv_bc, grad_conv_bc_bias = bc_conv_back(d_bc_post)
-    grad_w_zx = jnp.stack(
-        [outer_product_sum(xn, d_z).astype(bf16), outer_product_sum(xn, d_xs).astype(bf16)]
-    )
-    grad_w_dt = outer_product_sum(xn, d_step)
-    lanes = ((0, 0), (0, 128 - d_step.shape[1]))
+    few = step_bias.shape[0]
+    lanes = ((0, 0), (0, 128 - few))
+    row_of = lambda part: jnp.pad(part[None], lanes)
+    small = jnp.concatenate(
+        [
+            taps,
+            tap_bias[None],
+            jnp.repeat(skip, MIXER_HEAD_SIZE)[None],
+            gate_gain[None],
+            jnp.zeros((1, 128), f32),
+            row_of(step_bias),
+            row_of(decay_rate),
+        ]
+    )
+    bc_small = jnp.concatenate([state_map_taps, state_map_tap_bias[None]])
+    mark_block = (width_a + 3 * rank) // 128
+    w_step = jnp.pad(w_step, lanes)
+    *kept, sums = mixer_forward(
+        xn, cot, xa_wide, mark_block, w_zx, w_step, state_map_weight, w_out, small, bc_small, groups
+    )
+    sums = sum_small(sizes, 4, sums)
+    d_z, d_xs, d_step, d_bc_part, yn_low, grad_w_zx, grad_w_dt, grad_w_out, few_x, few_bc = (
+        mixer_backward(xn, cot, xa_wide, mark_block, kept, sums, small, bc_small, groups)
+    )
+    grad_conv_bc, grad_conv_bc_bias = few_bc[:4], few_bc[4]
     found = exchange(
         sizes,
         5,
@@ -1692,15 +1909,16 @@
             [
                 (d_z, w_zx, 0, True),
                 (d_xs, w_zx, 1, True),
-                (jnp.pad(d_step, lanes), jnp.pad(w_step, lanes), None, True),
+                (d_step, w_step, None, True),
             ],
-            d_bc_part.astype(bf16),
+            d_bc_part,
         ),
         finish_mixer_back,
         [after_mlp, gain_n, cot_low, state_map_weight],
         [hidden_f.shape, gain_n.shape],
         width + d_bc_part.shape[1],
-        [(grad_w_zx, 1, 2), (grad_w_out.astype(bf16), 1, 0)],
+        [(grad_w_zx, 1, 2), (grad_w_out, 1, 0)],
+        early_share=43,
         also_sum=(
             Summed(sizes, [(yn_low, w_out, None, False)]),
             finish_out,
@@ -1745,14 +1963,7 @@
     adapter_up_gradient = jnp.stack(
         [outer_product_sum(mid[:, j * rank : (j + 1) * rank], d_proj[j]) for j in range(3)]
     )
-    shares = [
-        jnp.pad(part, (0, 128 - part.shape[0]))[None]
-        for part in (grad_dt_bias, grad_a_log, grad_d_skip)
-    ]
-    shares = jnp.concatenate(
-        [grad_conv_x, grad_conv_x_bias[None], grad_g_gate[None]] + shares
-        + [jnp.zeros((7, 128), f32), jnp.pad(grad_w_dt.T.reshape(-1, 128), ((0, 0), (0, 0)))]
-    ).astype(bf16)
+    shares = jnp.concatenate([few_x, grad_w_dt[:few].reshape(-1, 128)]).astype(bf16)
     sums = [grad_g_mlp[0], grad_g_mamba[0], grad_conv_bc, grad_conv_bc_bias]
     row = jnp.concatenate([part.reshape(-1) for part in sums])[None]
     found = exchange(
@@ -1777,7 +1988,7 @@
             (adapter_up_gradient.astype(bf16), None, 2),
             (shares, None, 1),
         ],
-        early_share=100,
+        early_share=30,
         tail=3 * width,
         small=width_a + row.shape[1],
     )
@@ -1790,10 +2001,10 @@
     adapter_up_gradient = adapter_up_gradient.astype(f32)
     shared = shared.astype(f32)
     grad_conv_x, grad_conv_x_bias, grad_g_gate = shared[:4], shared[4], shared[5]
-    few = step_bias.shape[0]
-    grad_dt_bias, grad_a_log, grad_d_skip = [
-        shared[i].reshape(plane_size, 128)[:, :few].reshape(-1) for i in (6, 7, 8)
-    ]
+    heads = shared.reshape(-1, plane_size, 128)
+    grad_dt_bias = heads[6, :, :few].reshape(-1)
+    grad_a_log = heads[7, :, :few].reshape(-1)
+    grad_d_skip = heads[8].reshape(plane_size, few, MIXER_HEAD_SIZE).sum(axis=2).reshape(-1)
     grad_w_dt = shared[16:].reshape(few, -1, plane_size, 128).transpose(1, 3, 2, 0)
     grad_w_dt = grad_w_dt.reshape(-1, plane_size * few)
     grad_g_attn = row[:width_a]

time: 1180 us -> 1030 us (0.87)
  matrix products: 142 us -> 79.5 us
  Pallas kernels: 922 us -> 879 us
  local copies, waits for them, and re-layouts: 43 us -> 21.5 us
  other arithmetic: 57.7 us -> 39.9 us
    pallas_call x5, Pallas kernels: 749 us -> 664 us  [exchange(): pl.pallas_call(kernel, out_shape=out_shape, in_specs=in_specs, out_specs=...]
    pallas_call x0 -> x2, Pallas kernels: none -> 55.7 us  [the longest x1 30.7 us: mixer_backward(): pl.pallas_call(kernel, grid=(groups,), in_specs=[by_group(width), by_grou...]
    dot_general x8 -> x0, matrix products: 25.3 us -> none  [the longest x3 17.1 us: mixer_groups(): jnp.einsum('ghts,gshp->gthp', decay * meet[:, None], xc * step[..., None]...]
    dot_general x15 -> x11, matrix products: 45.4 us -> 29.4 us  [outer_product_sum(): lax.dot_general(left, right, (((0,), (0,)), ((), ())), preferred_element_...]
    pallas_call x1, Pallas kernels: 146 us -> 130 us  [opening(): pl.pallas_call(kernel, out_shape=[S((groups, ctx, tp // 2, 2, rows, width...]
    dot_general x12 -> x8, matrix products: 46.7 us -> 32.5 us  [matrix_product(): return jnp.dot(left, right, preferred_element_type=jnp.float32)]
    reshape x12 -> x2, local copies, waits for them, and re-layouts: 14.5 us -> 0.61 us  [the longest x1 0.6 us: per_device_split(): heads[8].reshape(plane_size, few, MIXER_HEAD_SIZE).sum(axis=2).reshape(-1)]
where the time goes in v4:
time: 1030 us; the launch traced here: 1020 us
  Pallas kernels  879 us (85%)
  matrix products  79.5 us (8%)
  other arithmetic  39.9 us (4%)
  local copies, waits for them, and re-layouts  21.5 us (2%)
    pallas_call x5, Pallas kernels, exchange(): pl.pallas_call(kernel, out_shape=out_shape, in_specs=in_specs, out_specs=...  664 us
    pallas_call x1, Pallas kernels, opening(): pl.pallas_call(kernel, out_shape=[S((groups, ctx, tp // 2, 2, rows, width...  130 us
    dot_general x8, matrix products, matrix_product(): return jnp.dot(left, right, preferred_element_type=jnp.float32)  32.5 us
    pallas_call x1, Pallas kernels, mixer_backward(): pl.pallas_call(kernel, grid=(groups,), in_specs=[by_group(width), by_grou...  30.7 us
    dot_general x11, matrix products, outer_product_sum(): lax.dot_general(left, right, (((0,), (0,)), ((), ())), preferred_element_...  29.4 us
    pallas_call x1, Pallas kernels, mixer_forward(): pl.pallas_call(kernel, grid=(groups,), in_specs=[by_group(width), by_grou...  25 us

profile of v4, /device:TPU:0, one launch (start us, length us, event | category | flops | bytes accessed | tf_op | source)
XLA Modules:
  0.0 1021.7 jit_solution(802925728799025706)
XLA Ops:
  0.7 2.1 slice_bitcast_fusion.2
  2.8 2.1 pad_maximum_fusion.refs_4_.refs_9_
  4.9 129.8 %opening_1.1 = (bf16[4,2,2,2,48,4608]{5,4,3,2,1,0:T(8,128)(2,1)}, bf16[128,2048]{1,0:T(8,128)(2,1)}, bf16[3,4096,128]{2,1,0:T(8,128)(2,1)}) custom-call(bf16[192,2048]{1,0:T(8,128)(2,1)} %refs_0_.1, bf16[192,2048]{1,0:T(8,128)(2,1)} %refs_1_.1, s32[1,3]{1,0:T(1,128)} %refs_2_.1, f32[1,4096]{1,0:T(1,128)} %bitcast.215, ...), custom_call_target="tpu_custom_call" | custom-call | tf_op jit(solution)/shard_map/opening_1/pallas_call | solution.py:1318
  134.7 6.7 fusion.12
  141.4 1.3 fusion.40
  142.8 6.7 fusion.14
  149.5 1.2 fusion.39
  150.8 1.4 convert_reduce_fusion.1
  152.2 4.4 fusion.89
  156.7 1.6 convert_reduce_fusion
  158.3 2.2 fusion.122
  160.7 1.4 copy-done.1
  162.3 6.7 fusion.10
  169.0 1.2 fusion.41
  170.3 0.8 copy-done.7
  171.0 1.3 convolution_convert_fusion.9
  172.3 2.0 dynamic-slice_convert_fusion
  174.3 119.2 %exchange_2.1 = (bf16[4,2,2,2,48,2048]{5,4,3,2,1,0:T(8,128)(2,1)}, f32[48,2048]{1,0:T(8,128)}, bf16[2,2048,256]{2,1,0:T(8,128)(2,1)}, bf16[256,2048]{1,0:T(8,128)(2,1)}) custom-call(bf16[4,2,2,2,48,128]{5,4,3,2,1,0:T(8,128)(2,1)} %bitcast.181, bf16[128,2048]{1,0:T(8,128)(2,1)} %get-tuple-element.73.refs_1_, f32[48,2048]{1,0:T(8,128)} %get-tuple-element.155.refs_2_.refs_5_, ...), custom_call_target="tpu_custom_call" | custom-call | tf_op jit(solution)/shard_map/exchange_2/pallas_call | solution.py:1221
  293.5 5.1 fusion.78
  299.0 3.6 multiply_convert_fusion.1
  302.7 1.6 constant_dynamic-slice_fusion.2.refs_4_.refs_8_
  304.3 126.4 %exchange_3.1 = (bf16[4,2,2,2,48,2048]{5,4,3,2,1,0:T(8,128)(2,1)}, f32[48,2048]{1,0:T(8,128)}, bf16[4,2,2,2,48,2048]{5,4,3,2,1,0:T(8,128)(2,1)}, bf16[2,2048,128]{2,1,0:T(8,128)(2,1)}, bf16[128,2048]{1,0:T(8,128)(2,1)}) custom-call(bf16[4,2,2,2,48,256]{5,4,3,2,1,0:T(8,128)(2,1)} %bitcast.206, bf16[256,2048]{1,0:T(8,128)(2,1)} %get-tuple-element.76.refs_1_, ...), custom_call_target="tpu_custom_call" | custom-call | tf_op jit(solution)/shard_map/exchange_3/pallas_call | solution.py:1221
  430.7 0.8 dynamic-slice_bitcast_fusion.11
  431.5 0.7 constant_dynamic-slice_fusion
  432.5 1.2 concatenate.30.sml
  433.7 0.8 constant_dynamic-slice_fusion.1
  434.8 0.9 pad.23.st_r.refs_4_
  436.3 25.0 %mixer_forward.1 = (f32[1536,128]{1,0:T(8,128)}, bf16[1536,128]{1,0:T(8,128)(2,1)}, bf16[1536,128]{1,0:T(8,128)(2,1)}, bf16[1536,256]{1,0:T(8,128)(2,1)}, bf16[1...) custom-call(bf16[1536,2048]{1,0:T(8,128)(2,1)} %bitcast.171, bf16[1536,2048]{1,0:T(8,128)(2,1)} %bitcast.174, ...), custom_call_target="tpu_custom_call" | custom-call | tf_op jit(solution)/shard_map/mixer_forward/pallas_call | solution.py:1602
  461.3 16.5 %sum_small_4.1.sums_r = f32[4,2,384]{2,1,0:T(2,128)} custom-call(f32[4,2,384]{2,1,0:T(2,128)} %get-tuple-element.88.x), custom_call_target="tpu_custom_call" | custom-call | tf_op jit(solution)/shard_map/sum_small_4/pallas_call | solution.py:1344
  477.8 30.7 %mixer_backward.1 = (bf16[1536,128]{1,0:T(8,128)(2,1)}, bf16[1536,128]{1,0:T(8,128)(2,1)}, bf16[1536,128]{1,0:T(8,128)(2,1)}, bf16[1536,256]{1,0:T(8,128)(2,1)},...) custom-call(bf16[1536,2048]{1,0:T(8,128)(2,1)} %bitcast.172, ...), custom_call_target="tpu_custom_call" | custom-call | tf_op jit(solution)/shard_map/mixer_backward/pallas_call | solution.py:1728
  508.5 137.7 %exchange_5.1 = (bf16[4,2,2,2,48,2304]{5,4,3,2,1,0:T(8,128)(2,1)}, f32[48,2048]{1,0:T(8,128)}, f32[1,2048]{1,0:T(1,128)}, bf16[48,2048]{1,0:T(8,128)(2,1)}, bf16...) custom-call(bf16[4,2,2,2,48,128]{5,4,3,2,1,0:T(8,128)(2,1)} %bitcast.209, bf16[4,2,2,2,48,128]{5,4,3,2,1,0:T(8,128)(2,1)} %bitcast.210, ...), custom_call_target="tpu_custom_call" | custom-call | tf_op jit(solution)/shard_map/exchange_5/pallas_call | solution.py:1221
  646.3 6.2 fusion.100
  652.5 0.8 slice.306
  654.0 5.7 fusion.34.refs_7_
  659.7 4.8 multiply_convert_fusion
  664.6 2.0 fusion.37
  666.6 2.0 fusion.38
  668.6 1.5 pad_maximum_fusion.2.refs_6_
  670.1 119.6 %exchange_6.1 = (bf16[4,2,2,2,48,2048]{5,4,3,2,1,0:T(8,128)(2,1)}, f32[48,2048]{1,0:T(8,128)}, f32[1,2048]{1,0:T(1,128)}, bf16[2,256,2048]{2,1,0:T(8,128)(2,1)}, bf16[2048,256]{1,0:T(8,128)(2,1)}) custom-call(bf16[4,2,2,2,48,256]{5,4,3,2,1,0:T(8,128)(2,1)} %bitcast.205, bf16[4,2,2,2,48,256]{5,4,3,2,1,0:T(8,128)(2,1)} %bitcast.204, ...), custom_call_target="tpu_custom_call" | custom-call | tf_op jit(solution)/shard_map/exchange_6/pallas_call | solution.py:1221
  789.8 4.8 convolution_convert_fusion.6
  795.8 1.5 fusion.56
  797.3 1.2 fusion.55
  798.6 3.7 fusion.98
  804.4 0.7 pad_maximum_fusion.6.refs_14_
  805.0 1.8 convolution_convert_fusion.2.refs_13_
  806.8 3.5 fusion.31
  810.3 3.5 fusion.28
  813.8 3.7 fusion.25
  817.6 2.0 pad_maximum_fusion.1.refs_12_
  819.6 0.6 broadcast_in_dim.57.refs_11_
  821.2 1.4 copy.67
  822.6 160.7 %exchange_7.1 = (bf16[4,2,2,2,48,384]{5,4,3,2,1,0:T(8,128)(2,1)}, bf16[2,2,48,6144]{3,2,1,0:T(8,128)(2,1)}, f32[1,9472]{1,0:T(1,128)}, bf16[3,512,1024]{2,1,0:T(...) custom-call(bf16[4,2,2,2,48,128]{5,4,3,2,1,0:T(8,128)(2,1)} %bitcast.186, ...), custom_call_target="tpu_custom_call" | custom-call | tf_op jit(solution)/shard_map/exchange_7/pallas_call | solution.py:1221
  983.3 13.2 %adapter_products.1 = f32[3,4096,128]{2,1,0:T(8,128)} custom-call(bf16[1536,4608]{1,0:T(8,128)(2,1)} %bitcast.162, bf16[1536,384]{1,0:T(8,128)(2,1)} %bitcast.202), custom_call_target="tpu_custom_call" | custom-call | tf_op jit(solution)/shard_map/adapter_products/pallas_call | solution.py:1427
  996.5 5.5 convert_element_type.241
  1002.0 2.1 slice_convert_fusion
  1004.1 1.3 convert_element_type.242
  1005.6 0.7 copy.82
  1006.3 1.0 convert_element_type.243
  1009.9 0.6 slice.182
  1010.5 0.6 slice.216
  1012.9 4.2 convert_element_type.244
  1017.1 1.5 convert_element_type.245
  1018.7 1.6 convert_element_type.246
  1020.3 1.0 convert_element_type.248
  (165 shorter events, 11.5 us)
Async XLA Ops:
  0.7 140.8 %copy-start = (bf16[3,128,1024]{2,1,0:T(8,128)(2,1)S(1)}, bf16[3,128,1024]{2,1,0:T(8,128)(2,1)}, u32[]{:S(2)}) copy-start(bf16[3,128,1024]{2,1,0:T(8,128)(2,1)} %param.32) | copy-start | bytes 2359300
  152.2 4.4 copy-start.38
  156.7 3.9 copy-start.20
  156.7 3.9 copy-start.22
  156.7 4.0 copy-start.24
  158.3 2.4 copy-start.34
  158.3 2.3 copy-start.28
  160.6 1.4 copy-start.1
  170.3 0.8 copy-start.7
  293.5 5.1 copy-start.10
  293.5 5.5 copy-start.44
  299.0 3.6 copy-start.46
  302.6 129.5 %copy-start.41 = (f32[16]{0:T(128)S(1)}, f32[16]{0:T(128)}, u32[]{:S(2)}) copy-start(f32[16]{0:T(128)} %param.46) | copy-start | bytes 196
  302.6 129.5 %copy-start.42 = (f32[16]{0:T(128)S(1)}, f32[16]{0:T(128)}, u32[]{:S(2)}) copy-start(f32[16]{0:T(128)} %param.45) | copy-start | bytes 196
  302.6 129.6 %copy-start.45 = (f32[16]{0:T(128)S(1)}, f32[16]{0:T(128)}, u32[]{:S(2)}) copy-start(f32[16]{0:T(128)} %param.47) | copy-start | bytes 196
  304.3 131.4 %copy-start.36 = (f32[4,256]{1,0:T(4,128)S(1)}, f32[4,256]{1,0:T(4,128)}, u32[]{:S(2)}) copy-start(f32[4,256]{1,0:T(4,128)} %param.43) | copy-start | bytes 12292
  304.3 131.4 %copy-start.40 = (f32[256]{0:T(256)S(1)}, f32[256]{0:T(256)}, u32[]{:S(2)}) copy-start(f32[256]{0:T(256)} %param.44) | copy-start | bytes 3076
  646.3 7.1 copy-start.31
  646.3 7.7 copy-start.17
  654.0 5.7 copy-start.13
  654.0 5.7 copy-start.43
  654.0 10.5 %slice-start.6 = ((s8[6291456]{0:T(1024)(128)(4,1)}), s8[4194304]{0:T(1024)(128)(4,1)S(1)}, s32[]{:S(2)}) async-start(s8[6291456]{0:T(1024)(128)(4,1)} %bitcast.237), calls=%async_computation.6 | async-start | bytes 8388608
  659.7 4.8 slice-start.7
  664.5 2.1 copy-start.15
  664.5 2.1 copy-start.14
  789.7 4.9 copy-start.2
  789.8 4.9 copy-start.8
  794.6 1.0 copy-start.25
  794.6 1.1 copy-start.26
  794.6 1.1 copy-start.29
  794.6 1.1 copy-start.35
  795.7 1.5 copy-start.21
  795.7 1.5 copy-start.23
  795.7 6.9 slice-start
  795.8 6.9 slice-start.1
  797.3 1.4 copy-start.39
  797.3 5.3 slice-start.2
  797.3 5.3 slice-start.3
  798.6 6.4 slice-start.4
  802.3 2.7 slice-start.5
  802.6 18.2 %copy-start.4 = (bf16[4,384,128]{2,1,0:T(8,128)(2,1)}, bf16[4,384,128]{2,1,0:T(8,128)(2,1)S(1)}, u32[]{:S(2)}) copy-start(bf16[4,384,128]{2,1,0:T(8,128)(2,1)S(1)} %add_convert_fusion.1) | copy-start | bytes 1179652
  803.2 17.3 %copy-start.5 = (bf16[4,384,128]{2,1,0:T(8,128)(2,1)}, bf16[4,384,128]{2,1,0:T(8,128)(2,1)S(1)}, u32[]{:S(2)}) copy-start(bf16[4,384,128]{2,1,0:T(8,128)(2,1)S(1)} %add_convert_fusion) | copy-start | bytes 1179652
  803.2 1.8 copy-start.3
  804.0 16.2 %copy-start.6 = (bf16[4,384,128]{2,1,0:T(8,128)(2,1)}, bf16[4,384,128]{2,1,0:T(8,128)(2,1)S(1)}, u32[]{:S(2)}) copy-start(bf16[4,384,128]{2,1,0:T(8,128)(2,1)S(1)} %convolution_convert_fusion.8) | copy-start | bytes 1179652
  817.5 2.0 copy-start.37
  817.5 2.0 copy-start.32
  817.5 2.0 copy-start.33
  996.5 5.5 copy-start.9
  1002.0 2.1 copy-start.16
  1004.1 1.3 copy-start.27
  1004.1 2.2 copy-start.19
  1005.4 3.9 copy-start.30
  1012.9 4.2 copy-start.12
  1017.1 1.6 copy-start.11
  1018.6 1.6 copy-start.18

commit v5 on v4

--- a/solution.py
+++ b/solution.py
@@ -602,8 +602,10 @@
 IN_HBM = pl.BlockSpec(memory_space=pltpu.HBM)
 IN_SMEM = pl.BlockSpec(memory_space=pltpu.SMEM)
 DMA = pltpu.SemaphoreType.DMA
-GATHER_SHARES = (4, 4, 4, 4)
-SUM_SHARES = (4, 4, 4, 4)
+GATHER_SHARES = (2,) * 8
+SUM_SHARES = (2,) * 8
+GATHER_LAGS = (0, 2, 4)
+SUM_LAGS = (0, 1, 3, 5, 7)
 
 
 class Place:
@@ -790,7 +792,7 @@
         self.fourth[q].start()
 
     def steps(self):
-        return pipelined(self.n, (self.to_side, self.to_other_side, self.to_core))
+        return pipelined(self.n, (self.to_side, self.to_other_side, self.to_core), GATHER_LAGS)
 
     def end(self):
         for copy in self.fourth:
@@ -799,13 +801,13 @@
             copy.wait_send()
 
 
-def pipelined(count, stages):
+def pipelined(count, stages, lags):
     def step(at):
-        for lag, stage in enumerate(stages):
+        for stage, lag in zip(stages, lags):
             if 0 <= at - lag < count:
                 stage(at - lag)
 
-    return [functools.partial(step, at) for at in range(count + len(stages) - 1)]
+    return [functools.partial(step, at) for at in range(count + max(lags))]
 
 
 def gather_sems(n, groups):
@@ -894,7 +896,7 @@
 
     def steps(self):
         stages = (self.to_core, self.to_side, self.to_other_side, self.along_line, self.land)
-        return pipelined(self.n, stages)
+        return pipelined(self.n, stages, SUM_LAGS)
 
     def end(self):
         for q in range(self.n):
@@ -1076,7 +1078,9 @@
     finish_outs,
     gathered,
     moves,
-    early_share=22,
+    plan=(3,),
+    start_also=5,
+    start_second=10,
     also_gather=None,
     also_sum=None,
     tail=0,
@@ -1164,20 +1168,21 @@
         if also_gather is not None:
             side_gather = Gather(place, ins[in_also][0], outs[o_also][0], also_pieces, scr[s_also])
             side_gather.begin()
-            streams.append((2, side_gather.steps()))
+            streams.append((start_also, side_gather.steps()))
             ends.append(side_gather)
         later = []
         if also_sum is not None:
             side_sum = second.stage(place, ins[in_second], scr[s_second])
             side_steps = side_sum.steps()
-            streams.append((6, side_steps[:3]))
-            later.append((0, side_steps[3:]))
+            ready = max(0, min(len(side_steps), len(summed.pieces) + SUM_LAGS[-1] - start_second))
+            streams.append((start_second, side_steps[:ready]))
+            later.append((0, side_steps[ready:]))
             ends.append(side_sum)
         total = n_moves * (groups * ctx - 1)
         steps = weave(*streams)
-        if carried is not None:
-            carried.issue(total * early_share // 100)
-        for step in steps:
+        for i, step in enumerate(steps):
+            if carried is not None and i < len(plan):
+                carried.issue(plan[i])
             step()
         if carried is not None:
             carried.settle()
@@ -1255,12 +1260,13 @@
     return found
 
 
-def opening(sizes, number, hidden, embeds, lengths, gain, down_all, moves):
+def opening(sizes, number, hidden, embeds, lengths, gain, down_maps, moves):
     groups, ctx, tp = sizes
     f32, bf16 = jnp.float32, jnp.bfloat16
     rows = hidden.shape[0] // tp
     half = hidden.shape[1]
-    mids = down_all.shape[1]
+    rank = down_maps.shape[2]
+    mids = down_maps.shape[0] * rank
     width = 2 * half + mids + 128
     out_pieces = gather_pieces(width)
     move_outs, move_scratch = moves_setup(moves, groups * ctx)
@@ -1290,9 +1296,11 @@
         inverse = lax.rsqrt(squares / (2 * half) + epsilon)
         low[:, :half] = (a * inverse * gain_ref[:, :half]).astype(bf16)
         low[:, half : 2 * half] = (b * inverse * gain_ref[:, half:]).astype(bf16)
-        low[:, 2 * half : 2 * half + mids] = lax.dot_general(
-            low[:, : 2 * half], down_ref[...], NN, preferred_element_type=f32
-        ).astype(bf16)
+        for j in range(down_maps.shape[0]):
+            at = 2 * half + j * rank
+            low[:, at : at + rank] = lax.dot_general(
+                low[:, : 2 * half], down_ref[j], NN, preferred_element_type=f32
+            ).astype(bf16)
         slot = lax.broadcasted_iota(jnp.int32, (rows, 128), 0)
         slot = slot + (place.c * tp + place.t) * rows
         lane = lax.broadcasted_iota(jnp.int32, (rows, 128), 1)
@@ -1327,7 +1335,7 @@
         compiler_params=pltpu.CompilerParams(
             collective_id=number, has_side_effects=True, vmem_limit_bytes=62 * 2**20
         ),
-    )(hidden, embeds, lengths, gain.reshape(1, -1), down_all, *[array for array, _, _ in moves])
+    )(hidden, embeds, lengths, gain.reshape(1, -1), down_maps, *[array for array, _, _ in moves])
     return [results[0].reshape(-1, width)] + list(results[1:])
 
 
@@ -1352,9 +1360,15 @@
     )(values)
 
 
+def own_of(place, ref, rows):
+    if ref.shape[0] == rows:
+        return ref[...].astype(jnp.float32)
+    return ref[pl.ds(pl.multiple_of(place.t * rows, 16), rows), :].astype(jnp.float32)
+
+
 def finish_forward(place, acc, args, outs, low, low_tail, low_small):
     rest, gain = args
-    outs[0][...] = rest[...] + acc[...]
+    outs[0][...] = own_of(place, rest, acc.shape[0]) + acc[...]
     low[...] = rms_rows(outs[0][...], gain[...]).astype(jnp.bfloat16)
 
 
@@ -1382,29 +1396,35 @@
 
 
 def finish_attention_back(place, acc, args, outs, low, low_tail, low_small):
-    hidden, embeds, gain, d_after_attn, down_all, out_mine, row = args
+    hidden, embeds, gain, d_after_attn, down_maps, out_mine, row = args
     half = hidden.shape[1]
     bf16, f32 = jnp.bfloat16, jnp.float32
     low[...] = acc[:, 2 * half :].astype(bf16)
-    inputs = (hidden, embeds)
-    squares = sum(jnp.sum(part[...] * part[...], axis=1, keepdims=True) for part in inputs)
+    inputs = [own_of(place, part, acc.shape[0]) for part in (hidden, embeds)]
+    squares = sum(jnp.sum(part * part, axis=1, keepdims=True) for part in inputs)
     inverse = lax.rsqrt(squares / (2 * half) + epsilon)
     along = jnp.zeros_like(squares)
     for i, part in enumerate(inputs):
         cols = slice(i * half, (i + 1) * half)
-        grad = acc[:, cols] + lax.dot_general(
-            low[...], down_all[cols, :], NT, preferred_element_type=f32
-        )
+        grad = acc[:, cols]
+        for j in range(down_maps.shape[0]):
+            rank = down_maps.shape[2]
+            grad = grad + lax.dot_general(
+                low[:, j * rank : (j + 1) * rank],
+                down_maps[j, cols, :],
+                NT,
+                preferred_element_type=f32,
+            )
         acc[:, cols] = grad
-        along = along + jnp.sum(grad * gain[:, cols] * part[...], axis=1, keepdims=True)
+        along = along + jnp.sum(grad * gain[:, cols] * part, axis=1, keepdims=True)
     along = along / (2 * half)
     low_tail[:, :half] = out_mine[...]
     low_small[:, 2 * half :] = row[...]
     for i, part in enumerate(inputs):
         cols = slice(i * half, (i + 1) * half)
         grad = acc[:, cols]
-        low_small[:, cols] = jnp.sum(grad * part[...] * inverse, axis=0, keepdims=True)
-        d_rows = grad * gain[:, cols] * inverse - part[...] * inverse**3 * along
+        low_small[:, cols] = jnp.sum(grad * part * inverse, axis=0, keepdims=True)
+        d_rows = grad * gain[:, cols] * inverse - part * inverse**3 * along
         if i == 0:
             d_rows = d_rows + d_after_attn[...]
         low_tail[:, (i + 1) * half : (i + 2) * half] = d_rows.astype(bf16)
@@ -1418,11 +1438,9 @@
     block, rank = 512, dmid.shape[1] // 3
 
     def kernel(a, b, o):
-        both = lax.dot_general(
-            a[...], b[...], (((0,), (0,)), ((), ())), preferred_element_type=jnp.float32
-        )
+        both = quick(b[...], a[...], TN)
         for j in range(3):
-            o[j] = both[:, j * rank : (j + 1) * rank]
+            o[j] = both[j * rank : (j + 1) * rank].T
 
     return pl.pallas_call(
         kernel,
@@ -1443,30 +1461,6 @@
         found.append(flat[at : at + part.size].reshape(part.shape))
         at += part.size
     return found
-
-
-def attend_groups(queries, keys_all, vals_all, segment, position):
-    def rot(values):
-        half_dim = values.shape[-1] // 2
-        inverse = 10000.0 ** (-jnp.arange(half_dim, dtype=jnp.float32) / half_dim)
-        angle = position.astype(jnp.float32)[..., None] * inverse
-        cosine, sine = jnp.cos(angle), jnp.sin(angle)
-        a, b = values[..., :half_dim], values[..., half_dim:]
-        return jnp.concatenate([a * cosine - b * sine, b * cosine + a * sine], axis=-1).astype(
-            jnp.bfloat16
-        )
-
-    rows = queries.shape[1]
-    order = jnp.arange(rows)
-    scores = jnp.einsum(
-        "gqd,gkd->gqk", rot(queries), rot(keys_all), preferred_element_type=jnp.float32
-    ) * AHD ** (-0.5)
-    allowed = (segment[:, :, None] == segment[:, None, :]) & (order[:, None] >= order[None, :])
-    weights = jnp.exp(jnp.where(allowed, scores, -1e30))
-    low = (weights / jnp.sum(weights, axis=-1, keepdims=True)).astype(jnp.bfloat16)
-    return jnp.einsum(
-        "gqk,gkd->gqd", low, vals_all.astype(jnp.bfloat16), preferred_element_type=jnp.float32
-    )
 
 
 TN = (((0,), (0,)), ((), ()))
@@ -1758,6 +1752,152 @@
     )(xn, cot, marked, z, xs, raw, bc, y, d_yn, sums, small, bc_small)
 
 
+def swap_halves(values):
+    return pltpu.roll(values, values.shape[1] // 2, 1)
+
+
+def attend_weights(qr, kr, marks, rows):
+    f32 = jnp.float32
+    row = lax.broadcasted_iota(jnp.int32, (rows, rows), 0)
+    col = lax.broadcasted_iota(jnp.int32, (rows, rows), 1)
+    first = row.astype(f32) - marks[:, 1:2]
+    allowed = (col <= row) & (col.astype(f32) >= first)
+    weights = jnp.exp(jnp.where(allowed, quick(qr, kr, NT) * AHD ** (-0.5), -1e30))
+    return weights / jnp.sum(weights, axis=-1, keepdims=True)
+
+
+def attention_forward(xa, width, w_qkv, up_maps, frequencies, groups):
+    f32, bf16 = jnp.float32, jnp.bfloat16
+    total, columns = xa.shape
+    rows, rank = total // groups, up_maps.shape[1]
+
+    def kernel(xa_r, w_r, up_r, freq_r, ao_o, q_o, k_o, v_o, cos_o, sin_o, w_all):
+        @pl.when(pl.program_id(0) == 0)
+        def _():
+            for j in range(3):
+                w_all[:, j * AHD : (j + 1) * AHD] = w_r[j]
+
+        marks = xa_r[:, width + 3 * rank :].astype(f32)
+        wide = quick(xa_r[:, :width], w_all[...], NN)
+        proj = []
+        for j in range(3):
+            mid = xa_r[:, width + j * rank : width + (j + 1) * rank]
+            proj.append((wide[:, j * AHD : (j + 1) * AHD] + quick(mid, up_r[j], NN)).astype(bf16))
+        angle = marks[:, 1:2] * freq_r[...]
+        lane = lax.broadcasted_iota(jnp.int32, angle.shape, 1)
+        cosine, sine = jnp.cos(angle), jnp.sin(angle)
+        sine = jnp.where(lane < AHD // 2, -sine, sine)
+        cos_o[...], sin_o[...] = cosine, sine
+        qr, kr = [
+            (piece * cosine + swap_halves(piece) * sine).astype(bf16)
+            for piece in (proj[0].astype(f32), proj[1].astype(f32))
+        ]
+        q_o[...], k_o[...], v_o[...] = qr, kr, proj[2]
+        low = attend_weights(qr, kr, marks, rows).astype(bf16)
+        ao_o[...] = quick(low, proj[2], NN).astype(bf16)
+
+    def by_group(size):
+        return pl.BlockSpec((rows, size), lambda g: (g, 0))
+
+    def whole(array):
+        return pl.BlockSpec(array.shape, lambda g: (0,) * array.ndim)
+
+    S = jax.ShapeDtypeStruct
+    return pl.pallas_call(
+        kernel,
+        grid=(groups,),
+        in_specs=[by_group(columns), whole(w_qkv), whole(up_maps), whole(frequencies)],
+        out_specs=[by_group(AHD)] * 6,
+        out_shape=[S((total, AHD), bf16)] * 4 + [S((total, AHD), f32)] * 2,
+        scratch_shapes=[pltpu.VMEM((width, 3 * AHD), bf16)],
+        compiler_params=pltpu.CompilerParams(vmem_limit_bytes=60 * 2**20),
+        name="attention_forward",
+    )(xa, w_qkv, up_maps, frequencies)
+
+
+def attention_backward(d_attn, xa, width, w_o, up_maps, kept, groups):
+    f32, bf16 = jnp.float32, jnp.bfloat16
+    total, columns = xa.shape
+    rows, rank = total // groups, up_maps.shape[1]
+    model = d_attn.shape[1]
+
+    def kernel(
+        da_r, xa_r, wo_r, up_r, ao_r, q_r, k_r, v_r, cos_r, sin_r,
+        dq_o, dk_o, dv_o, dmid_o, gw_o, go_o, gup_o, acc_w, acc_o,
+    ):
+        group = pl.program_id(0)
+        d_rows = da_r[...]
+        marks = xa_r[:, width + 3 * rank :].astype(f32)
+        d_ao = quick(d_rows, wo_r[...], NT).astype(bf16)
+        qr, kr, vals = q_r[...], k_r[...], v_r[...]
+        weights = attend_weights(qr, kr, marks, rows)
+        d_vals = quick(weights.astype(bf16), d_ao, TN)
+        d_weights = quick(d_ao, vals, NT).astype(bf16).astype(f32)
+        along = jnp.sum(d_weights * weights, axis=-1, keepdims=True)
+        d_scores = (weights * (d_weights - along) * AHD ** (-0.5)).astype(bf16)
+        cosine, sine = cos_r[...], sin_r[...]
+        pieces = []
+        for d_turned in (quick(d_scores, kr, NN), quick(d_scores, qr, TN)):
+            d_turned = d_turned.astype(bf16).astype(f32)
+            pieces.append((d_turned * cosine + swap_halves(d_turned * sine)).astype(bf16))
+        pieces.append(d_vals.astype(bf16))
+        for j, out in enumerate((dq_o, dk_o, dv_o)):
+            out[...] = pieces[j]
+            dmid_o[:, j * rank : (j + 1) * rank] = quick(pieces[j], up_r[j], NT).astype(bf16)
+        part = quick(jnp.concatenate(pieces, axis=1), xa_r[:, :width], TN)
+        part_o = quick(ao_r[...], d_rows, TN)
+        parts_up = [
+            quick(xa_r[:, width + j * rank : width + (j + 1) * rank], pieces[j], TN)
+            for j in range(3)
+        ]
+
+        @pl.when(group == 0)
+        def _():
+            acc_w[...], acc_o[...] = part, part_o
+            for j in range(3):
+                gup_o[j] = parts_up[j]
+
+        @pl.when(group > 0)
+        def _():
+            acc_w[...] += part
+            acc_o[...] += part_o
+            for j in range(3):
+                gup_o[j] += parts_up[j]
+
+        @pl.when(group == groups - 1)
+        def _():
+            for j in range(3):
+                gw_o[j] = acc_w[j * AHD : (j + 1) * AHD, :].T.astype(bf16)
+            go_o[...] = acc_o[...].astype(bf16)
+
+    def by_group(size):
+        return pl.BlockSpec((rows, size), lambda g: (g, 0))
+
+    def whole(shape):
+        return pl.BlockSpec(shape, lambda g: (0,) * len(shape))
+
+    S = jax.ShapeDtypeStruct
+    return pl.pallas_call(
+        kernel,
+        grid=(groups,),
+        in_specs=[by_group(model), by_group(columns), whole(w_o.shape), whole(up_maps.shape)]
+        + [by_group(AHD)] * 6,
+        out_specs=[by_group(AHD)] * 3
+        + [by_group(3 * rank)]
+        + [whole((3, width, AHD)), whole((AHD, model)), whole((3, rank, AHD))],
+        out_shape=[S((total, AHD), bf16)] * 3
+        + [
+            S((total, 3 * rank), bf16),
+            S((3, width, AHD), bf16),
+            S((AHD, model), bf16),
+            S((3, rank, AHD), f32),
+        ],
+        scratch_shapes=[pltpu.VMEM((3 * AHD, width), f32), pltpu.VMEM((AHD, model), f32)],
+        compiler_params=pltpu.CompilerParams(vmem_limit_bytes=60 * 2**20),
+        name="attention_backward",
+    )(d_attn, xa, w_o, up_maps, *kept)
+
+
 def per_device_split(
     hidden,
     embeds,
@@ -1805,8 +1945,7 @@
         return lax.dynamic_slice_in_dim(values, plane_index * width, width, axis)
 
     width = hidden.shape[1]
-    hidden_f = own_rows(hidden).astype(f32)
-    embeds_f = own_rows(embeds).astype(f32)
+    own_shape = (mine, width)
     cot_low = own_rows(cotangent)
 
     up_maps = own_part(adapter_up_maps, 2)
@@ -1817,7 +1956,6 @@
 
     rank = adapter_down_maps.shape[2]
     width_a = adapter_down_maps.shape[1]
-    down_all = jnp.concatenate([adapter_down_maps[j] for j in range(3)], axis=1)
     xa_wide, w_o, w_qkv = opening(
         sizes,
         1,
@@ -1825,25 +1963,14 @@
         embeds,
         lengths,
         attention_norm_gain,
-        down_all,
+        adapter_down_maps,
         [(attention_output_weight, 0, 1), (query_key_value_weight, 2, 1)],
     )
-    xa = xa_wide[:, :width_a]
-    mid = xa_wide[:, width_a : width_a + 3 * rank]
-    segment = xa_wide[:, width_a + 3 * rank].astype(jnp.int32).reshape(groups, group_rows)
-    position = xa_wide[:, width_a + 3 * rank + 1].astype(jnp.int32).reshape(groups, group_rows)
-    proj = [
-        (
-            matrix_product(xa, w_qkv[j])
-            + matrix_product(mid[:, j * rank : (j + 1) * rank], up_maps[j])
-        ).astype(bf16)
-        for j in range(3)
-    ]
-    ao, attend_back = jax.vjp(
-        lambda q, k, v: attend_groups(q, k, v, segment, position),
-        *[piece.astype(f32).reshape(groups, group_rows, AHD) for piece in proj],
-    )
-    ao_low = ao.astype(bf16).reshape(groups * group_rows, AHD)
+    half = AHD // 2
+    frequencies = 10000.0 ** (-jnp.arange(half, dtype=f32) / half)
+    frequencies = jnp.concatenate([frequencies, frequencies])[None]
+    kept_a = attention_forward(xa_wide, width_a, w_qkv, up_maps, frequencies, groups)
+    ao_low = kept_a[0]
 
     gain_m = feedforward_norm_gain.reshape(1, -1)
     found = exchange(
@@ -1851,8 +1978,8 @@
         2,
         Summed(sizes, [(ao_low, w_o, None, False)]),
         finish_forward,
-        [hidden_f, gain_m],
-        [hidden_f.shape],
+        [hidden, gain_m],
+        [own_shape],
         width,
         [(gate_up_weight, 2, 1), (down_weight, 0, 1)],
     )
@@ -1868,10 +1995,10 @@
         Summed(sizes, [(hid_low, w_down, None, False)]),
         finish_forward,
         [after_attn, gain_n],
-        [hidden_f.shape],
+        [own_shape],
         width,
         [(mixer_gate_input_weight, 2, 1), (mixer_output_weight, 0, 1)],
-        early_share=0,
+        plan=(),
         also_gather=cot_low,
     )
     xn, cot, (after_mlp,) = found["gathered"], found["also"], found["finish"]
@@ -1915,15 +2042,15 @@
         ),
         finish_mixer_back,
         [after_mlp, gain_n, cot_low, state_map_weight],
-        [hidden_f.shape, gain_n.shape],
+        [own_shape, gain_n.shape],
         width + d_bc_part.shape[1],
         [(grad_w_zx, 1, 2), (grad_w_out, 1, 0)],
-        early_share=43,
+        plan=(6,),
         also_sum=(
             Summed(sizes, [(yn_low, w_out, None, False)]),
             finish_out,
             [after_mlp],
-            jax.ShapeDtypeStruct(hidden_f.shape, bf16),
+            jax.ShapeDtypeStruct(own_shape, bf16),
         ),
     )
     gathered, (d_after_mlp, grad_g_mamba) = found["gathered"], found["finish"]
@@ -1944,24 +2071,14 @@
         Summed(sizes, [(d_gate, w_gu, 0, True), (d_up, w_gu, 1, True)]),
         finish_mlp_back,
         [after_attn, gain_m, d_after_mlp],
-        [hidden_f.shape, gain_m.shape],
+        [own_shape, gain_m.shape],
         width,
         [(grad_w_gu, 1, 2), (grad_w_down.astype(bf16), 1, 0)],
     )
     d_attn, (d_after_attn, grad_g_mlp) = found["gathered"], found["finish"]
     grad_w_gu, grad_w_down = found["moves"]
-    grad_w_o = outer_product_sum(ao_low, d_attn)
-    d_ao = matrix_product_transposed(d_attn, w_o).astype(bf16)
-    d_proj = [
-        piece.reshape(groups * group_rows, AHD).astype(bf16)
-        for piece in attend_back(d_ao.astype(f32).reshape(groups, group_rows, AHD))
-    ]
-    dmid_part = jnp.concatenate(
-        [matrix_product_transposed(d_proj[j], up_maps[j]).astype(bf16) for j in range(3)], axis=1
-    )
-    grad_w_qkv = jnp.stack([outer_product_sum(xa, d_proj[j]).astype(bf16) for j in range(3)])
-    adapter_up_gradient = jnp.stack(
-        [outer_product_sum(mid[:, j * rank : (j + 1) * rank], d_proj[j]) for j in range(3)]
+    *d_proj, dmid_part, grad_w_qkv, grad_w_o, adapter_up_gradient = attention_backward(
+        d_attn, xa_wide, width_a, w_o, up_maps, kept_a, groups
     )
     shares = jnp.concatenate([few_x, grad_w_dt[:few].reshape(-1, 128)]).astype(bf16)
     sums = [grad_g_mlp[0], grad_g_mamba[0], grad_conv_bc, grad_conv_bc_bias]
@@ -1972,11 +2089,11 @@
         Summed(sizes, [(d_proj[j], w_qkv, j, True) for j in range(3)], dmid_part),
         finish_attention_back,
         [
-            hidden_f,
-            embeds_f,
+            hidden,
+            embeds,
             attention_norm_gain.reshape(1, -1),
             d_after_attn,
-            down_all,
+            adapter_down_maps,
             out_mine,
             row,
         ],
@@ -1984,11 +2101,11 @@
         3 * rank,
         [
             (grad_w_qkv, 1, 2),
-            (grad_w_o.astype(bf16), 1, 0),
+            (grad_w_o, 1, 0),
             (adapter_up_gradient.astype(bf16), None, 2),
             (shares, None, 1),
         ],
-        early_share=30,
+        plan=(5,),
         tail=3 * width,
         small=width_a + row.shape[1],
     )

time: 1030 us -> 972 us (0.944)
  matrix products: 79.5 us -> 26.6 us
  other arithmetic: 39.9 us -> 23.1 us
  Pallas kernels: 879 us -> 891 us
    pallas_call x0 -> x2, Pallas kernels: none -> 42.4 us  [the longest x1 26.2 us: attention_backward(): pl.pallas_call(kernel, grid=(groups,), in_specs=[by_group(model), by_grou...]
    dot_general x8 -> x2, matrix products: 32.5 us -> 8.66 us  [matrix_product(): return jnp.dot(left, right, preferred_element_type=jnp.float32)]
    pallas_call x5, Pallas kernels: 664 us -> 641 us  [exchange(): pl.pallas_call(kernel, out_shape=out_shape, in_specs=in_specs, out_specs=...]
    dot_general x11 -> x4, matrix products: 29.4 us -> 13.1 us  [outer_product_sum(): lax.dot_general(left, right, (((0,), (0,)), ((), ())), preferred_element_...]
where the time goes in v5:
time: 972 us; the launch traced here: 962 us
  Pallas kernels  891 us (92%)
  matrix products  26.6 us (3%)
  other arithmetic  23.1 us (2%)
  local copies, waits for them, and re-layouts  19.5 us (2%)
    pallas_call x5, Pallas kernels, exchange(): pl.pallas_call(kernel, out_shape=out_shape, in_specs=in_specs, out_specs=...  641 us
    pallas_call x1, Pallas kernels, opening(): pl.pallas_call(kernel, out_shape=[S((groups, ctx, tp // 2, 2, rows, width...  125 us
    pallas_call x1, Pallas kernels, mixer_backward(): pl.pallas_call(kernel, grid=(groups,), in_specs=[by_group(width), by_grou...  30.9 us
    pallas_call x1, Pallas kernels, attention_backward(): pl.pallas_call(kernel, grid=(groups,), in_specs=[by_group(model), by_grou...  26.2 us
    pallas_call x1, Pallas kernels, mixer_forward(): pl.pallas_call(kernel, grid=(groups,), in_specs=[by_group(width), by_grou...  24.6 us

profile of v5, /device:TPU:0, one launch (start us, length us, event | category | flops | bytes accessed | tf_op | source)
XLA Modules:
  0.0 961.6 jit_solution(12191968923734195905)
XLA Ops:
  0.7 0.8 dynamic_slice.32
  1.5 0.1 broadcast_in_dim.29
  1.6 0.1 broadcast_in_dim_reshape.3
  1.7 0.6 maximum_bitcast_fusion.freq_r
  2.2 0.8 dynamic-slice_bitcast_fusion.2
  3.0 0.7 dynamic-slice_bitcast_fusion
  3.8 0.7 constant_dynamic-slice_fusion
  4.5 1.2 concatenate.17.sml
  5.7 0.8 constant_dynamic-slice_fusion.1
  6.5 1.3 pad_maximum_fusion.3.bsml
  7.8 1.5 constant_dynamic-slice_fusion.3.up_r
  9.3 0.7 constant_dynamic-slice_fusion.2.refs_4_.refs_8_
  10.0 0.3 copy.53
  10.3 0.9 pad.11.st_r.refs_4_
  11.2 125.4 %opening_1.1 = (bf16[4,2,2,2,48,4608]{5,4,3,2,1,0:T(8,128)(2,1)}, bf16[128,2048]{1,0:T(8,128)(2,1)}, bf16[3,4096,128]{2,1,0:T(8,128)(2,1)}) custom-call(bf16[192,2048]{1,0:T(8,128)(2,1)} %refs_5_.7, bf16[192,2048]{1,0:T(8,128)(2,1)} %refs_6_.5, s32[1,3]{1,0:T(1,128)} %refs_2_.2, f32[1,4096]{1,0:T(1,128)} %bitcast.116, bf16[3,4096,128]{2,1,0:T(8,128)(2,1)} %refs_9_.3, ...), custom_call_target="tpu_custom_call" | custom-call | tf_op jit(solution)/shard_map/opening_1/pallas_call | solution.py:1326
  136.6 16.2 %attention_forward.1 = (bf16[1536,128]{1,0:T(8,128)(2,1)}, bf16[1536,128]{1,0:T(8,128)(2,1)}, bf16[1536,128]{1,0:T(8,128)(2,1)}, bf16[1536,128]{1,0:T(8,128)(2,1...) custom-call(bf16[1536,4608]{1,0:T(8,128)(2,1)} %bitcast.86, bf16[3,4096,128]{2,1,0:T(8,128)(2,1)} %get-tuple-element.85.w_r.refs_3_, ...), custom_call_target="tpu_custom_call" | custom-call | tf_op jit(solution)/shard_map/attention_forward/pallas_call | solution.py:1806
  152.9 118.8 %exchange_2.1 = (bf16[4,2,2,2,48,2048]{5,4,3,2,1,0:T(8,128)(2,1)}, f32[48,2048]{1,0:T(8,128)}, bf16[2,2048,256]{2,1,0:T(8,128)(2,1)}, bf16[256,2048]{1,0:T(8,128)(2,1)}) custom-call(bf16[4,2,2,2,48,128]{5,4,3,2,1,0:T(8,128)(2,1)} %bitcast.98, bf16[128,2048]{1,0:T(8,128)(2,1)} %get-tuple-element.87.refs_1_.wo_r, bf16[192,2048]{1,0:T(8,128)(2,1)} %refs_5_.7, ...), custom_call_target="tpu_custom_call" | custom-call | tf_op jit(solution)/shard_map/exchange_2/pallas_call | solution.py:1226
  271.7 5.1 fusion.18
  276.8 0.4 copy-done.18
  277.2 3.6 multiply_convert_fusion.1
  280.8 122.2 %exchange_3.1 = (bf16[4,2,2,2,48,2048]{5,4,3,2,1,0:T(8,128)(2,1)}, f32[48,2048]{1,0:T(8,128)}, bf16[4,2,2,2,48,2048]{5,4,3,2,1,0:T(8,128)(2,1)}, bf16[2,2048,128]{2,1,0:T(8,128)(2,1)}, bf16[128,2048]{1,0:T(8,128)(2,1)}) custom-call(bf16[4,2,2,2,48,256]{5,4,3,2,1,0:T(8,128)(2,1)} %bitcast.104, bf16[256,2048]{1,0:T(8,128)(2,1)} %get-tuple-element.90.refs_1_, ...), custom_call_target="tpu_custom_call" | custom-call | tf_op jit(solution)/shard_map/exchange_3/pallas_call | solution.py:1226
  403.0 24.6 %mixer_forward.1 = (f32[1536,128]{1,0:T(8,128)}, bf16[1536,128]{1,0:T(8,128)(2,1)}, bf16[1536,128]{1,0:T(8,128)(2,1)}, bf16[1536,256]{1,0:T(8,128)(2,1)}, bf16[1...) custom-call(bf16[1536,2048]{1,0:T(8,128)(2,1)} %bitcast.91, bf16[1536,2048]{1,0:T(8,128)(2,1)} %bitcast.94, ...), custom_call_target="tpu_custom_call" | custom-call | tf_op jit(solution)/shard_map/mixer_forward/pallas_call | solution.py:1596
  427.6 13.7 %sum_small_4.1.sums_r = f32[4,2,384]{2,1,0:T(2,128)} custom-call(f32[4,2,384]{2,1,0:T(2,128)} %get-tuple-element.102.x), custom_call_target="tpu_custom_call" | custom-call | tf_op jit(solution)/shard_map/sum_small_4/pallas_call | solution.py:1352
  441.3 30.9 %mixer_backward.1 = (bf16[1536,128]{1,0:T(8,128)(2,1)}, bf16[1536,128]{1,0:T(8,128)(2,1)}, bf16[1536,128]{1,0:T(8,128)(2,1)}, bf16[1536,256]{1,0:T(8,128)(2,1)},...) custom-call(bf16[1536,2048]{1,0:T(8,128)(2,1)} %bitcast.92, ...), custom_call_target="tpu_custom_call" | custom-call | tf_op jit(solution)/shard_map/mixer_backward/pallas_call | solution.py:1722
  472.2 0.7 slice.91
  472.9 0.7 slice_bitcast_fusion.1
  473.6 0.7 convert.8
  474.3 0.8 slice.149
  475.2 0.6 pad_maximum_fusion.2.refs_15_
  475.8 128.3 %exchange_5.1 = (bf16[4,2,2,2,48,2304]{5,4,3,2,1,0:T(8,128)(2,1)}, f32[48,2048]{1,0:T(8,128)}, f32[1,2048]{1,0:T(1,128)}, bf16[48,2048]{1,0:T(8,128)(2,1)}, bf16...) custom-call(bf16[4,2,2,2,48,128]{5,4,3,2,1,0:T(8,128)(2,1)} %bitcast.107, bf16[4,2,2,2,48,128]{5,4,3,2,1,0:T(8,128)(2,1)} %bitcast.108, ...), custom_call_target="tpu_custom_call" | custom-call | tf_op jit(solution)/shard_map/exchange_5/pallas_call | solution.py:1226
  604.1 6.3 fusion.22
  610.5 4.9 multiply_convert_fusion
  615.4 2.8 fusion.4.refs_7_
  618.2 2.0 fusion.8
  620.2 2.0 fusion.7
  622.2 1.5 pad_maximum_fusion.refs_6_
  623.7 1.0 convert_element_type.73
  624.8 1.6 convert_element_type.71
  626.4 116.5 %exchange_6.1 = (bf16[4,2,2,2,48,2048]{5,4,3,2,1,0:T(8,128)(2,1)}, f32[48,2048]{1,0:T(8,128)}, f32[1,2048]{1,0:T(1,128)}, bf16[2,256,2048]{2,1,0:T(8,128)(2,1)}, bf16[2048,256]{1,0:T(8,128)(2,1)}) custom-call(bf16[4,2,2,2,48,256]{5,4,3,2,1,0:T(8,128)(2,1)} %bitcast.103, bf16[4,2,2,2,48,256]{5,4,3,2,1,0:T(8,128)(2,1)} %bitcast.102, ...), custom_call_target="tpu_custom_call" | custom-call | tf_op jit(solution)/shard_map/exchange_6/pallas_call | solution.py:1226
  742.9 26.2 %attention_backward.1 = (bf16[1536,128]{1,0:T(8,128)(2,1)}, bf16[1536,128]{1,0:T(8,128)(2,1)}, bf16[1536,128]{1,0:T(8,128)(2,1)}, bf16[1536,384]{1,0:T(8,128)(2,...) custom-call(bf16[1536,2048]{1,0:T(8,128)(2,1)} %bitcast.96, ...), custom_call_target="tpu_custom_call" | custom-call | tf_op jit(solution)/shard_map/attention_backward/pallas_call | solution.py:1880
  769.1 0.6 broadcast_in_dim.35.refs_11_
  769.7 1.6 convert_element_type.63.refs_14_
  771.3 155.0 %exchange_7.1 = (bf16[4,2,2,2,48,384]{5,4,3,2,1,0:T(8,128)(2,1)}, bf16[2,2,48,6144]{3,2,1,0:T(8,128)(2,1)}, f32[1,9472]{1,0:T(1,128)}, bf16[3,512,1024]{2,1,0:T(...) custom-call(bf16[4,2,2,2,48,128]{5,4,3,2,1,0:T(8,128)(2,1)} %bitcast.111, ...), custom_call_target="tpu_custom_call" | custom-call | tf_op jit(solution)/shard_map/exchange_7/pallas_call | solution.py:1226
  926.3 13.0 %adapter_products.1 = f32[3,4096,128]{2,1,0:T(8,128)} custom-call(bf16[1536,4608]{1,0:T(8,128)(2,1)} %bitcast.90, bf16[1536,384]{1,0:T(8,128)(2,1)} %bitcast.100), custom_call_target="tpu_custom_call" | custom-call | tf_op jit(solution)/shard_map/adapter_products/pallas_call | solution.py:1445
  939.3 0.6 slice.107
  939.9 0.6 reshape.180
  940.5 0.6 fusion.25
  941.1 0.6 slice.120
  941.7 0.6 slice.96
  942.3 0.6 fusion.26
  943.0 0.6 reshape_squeeze.10
  943.6 0.6 reshape_squeeze.9
  944.3 0.7 copy.59
  945.0 0.1 reshape_squeeze.11
  945.1 0.1 reduce_sum.9
  945.2 0.6 reshape.182
  945.8 2.1 convert_element_type.68
  947.9 2.5 convert_element_type.67
  950.3 2.1 slice_convert_fusion
  952.4 1.5 convert_element_type.70
  953.9 0.9 copy-done.4
  954.8 2.5 convert_element_type.69
  957.3 0.3 copy-done.2
  957.7 3.5 convert_element_type.66
  (60 shorter events, 0.3 us)
Async XLA Ops:
  0.7 8.7 copy-start
  271.7 5.1 copy-start.5
  271.7 5.5 copy-start.18
  277.2 3.6 copy-start.19
  604.1 6.4 copy-start.8
  604.1 6.4 copy-start.17
  604.1 6.4 copy-start.20
  604.1 14.0 %slice-start = ((s8[6291456]{0:T(1024)(128)(4,1)}), s8[4194304]{0:T(1024)(128)(4,1)S(1)}, s32[]{:S(2)}) async-start(s8[6291456]{0:T(1024)(128)(4,1)} %bitcast.138), calls=%async_computation | async-start | bytes 8388608
  610.5 4.9 copy-start.11
  610.5 7.7 slice-start.1
  615.4 2.8 copy-start.9
  615.4 4.8 copy-start.10
  622.2 1.5 copy-start.12
  622.2 2.6 copy-start.7
  742.9 26.2 %copy-start.15 = (f32[1,2048]{1,0:T(1,128)S(1)}, f32[1,2048]{1,0:T(1,128)}, u32[]{:S(2)}) copy-start(f32[1,2048]{1,0:T(1,128)} %get-tuple-element.126) | copy-start | bytes 24580
  742.9 26.2 %copy-start.16 = (f32[1,2048]{1,0:T(1,128)S(1)}, f32[1,2048]{1,0:T(1,128)}, u32[]{:S(2)}) copy-start(f32[1,2048]{1,0:T(1,128)} %get-tuple-element.125) | copy-start | bytes 24580
  926.3 13.1 %copy-start.14 = (f32[1,9472]{1,0:T(1,128)S(1)}, f32[1,9472]{1,0:T(1,128)}, u32[]{:S(2)}) copy-start(f32[1,9472]{1,0:T(1,128)} %get-tuple-element.134) | copy-start | bytes 113668
  926.3 14.2 %copy-start.13 = (bf16[48,1024]{1,0:T(8,128)(2,1)S(1)}, bf16[48,1024]{1,0:T(8,128)(2,1)}, u32[]{:S(2)}) copy-start(bf16[48,1024]{1,0:T(8,128)(2,1)} %get-tuple-element.142) | copy-start | bytes 294916
  944.3 6.0 copy-start.3
  950.3 2.1 copy-start.6
  952.4 2.3 copy-start.4
  954.8 2.9 copy-start.2
  957.7 3.5 copy-start.1

commit v6 on v5

--- a/solution.py
+++ b/solution.py
@@ -1260,29 +1260,31 @@
     return found
 
 
-def opening(sizes, number, hidden, embeds, lengths, gain, down_maps, moves):
+def opening(sizes, number, hidden, embeds, cotangent, lengths, gain, down_maps, shard, moves):
     groups, ctx, tp = sizes
     f32, bf16 = jnp.float32, jnp.bfloat16
     rows = hidden.shape[0] // tp
     half = hidden.shape[1]
     rank = down_maps.shape[2]
     mids = down_maps.shape[0] * rank
-    width = 2 * half + mids + 128
+    rest = 3 * half
+    width = rest + mids + 128
     out_pieces = gather_pieces(width)
     move_outs, move_scratch = moves_setup(moves, groups * ctx)
     move_specs = [(split, join) for _, split, join in moves]
     n_moves = len(moves)
 
     def kernel(*refs):
-        hid, emb, lens, gain_ref, down_ref = refs[:5]
-        refs = list(refs[5:])
+        hid, emb, cot, lens, gain_ref, down_ref = refs[:6]
+        up_ref, step_ref, taps_ref, bias_ref, norm_ref, *head_refs = refs[6:14]
+        refs = list(refs[14:])
         sources = refs[:n_moves]
-        o = refs[n_moves]
-        targets = refs[n_moves + 1 : 2 * n_moves + 1]
-        rest = refs[2 * n_moves + 1 :]
-        low, gs = rest[0], rest[1:10]
-        stages = rest[10 : 10 + n_moves]
-        send, recv, local = rest[10 + n_moves :]
+        o, up_o, step_o, small_o = refs[n_moves : n_moves + 4]
+        targets = refs[n_moves + 4 : 2 * n_moves + 4]
+        own = refs[2 * n_moves + 4 :]
+        low, gs = own[0], own[1:10]
+        stages = own[10 : 10 + n_moves]
+        send, recv, local = own[10 + n_moves :]
         place = Place(sizes)
         greet(
             [place.core, place.side_y]
@@ -1297,7 +1299,7 @@
         low[:, :half] = (a * inverse * gain_ref[:, :half]).astype(bf16)
         low[:, half : 2 * half] = (b * inverse * gain_ref[:, half:]).astype(bf16)
         for j in range(down_maps.shape[0]):
-            at = 2 * half + j * rank
+            at = rest + j * rank
             low[:, at : at + rank] = lax.dot_general(
                 low[:, : 2 * half], down_ref[j], NN, preferred_element_type=f32
             ).astype(bf16)
@@ -1312,10 +1314,35 @@
             segment = segment + passed
             position = position - passed * length
         marks = jnp.where(lane == 0, segment, position)
-        low[:, 2 * half + mids :] = marks.astype(f32).astype(bf16)
+        low[:, 2 * half : rest] = cot[mine, :]
+        low[:, rest + mids :] = marks.astype(f32).astype(bf16)
         gather = Gather(place, low, o, out_pieces, gs)
         gather.begin()
         carried.issue(len(carried.queue))
+        lanes = pl.ds(pl.multiple_of(place.index * 128, 128), 128)
+        for j in range(up_o.shape[0]):
+            up_o[j] = up_ref[j, :, lanes]
+        heads = step_ref.shape[1]
+        few = heads // place.plane
+        row = lax.broadcasted_iota(jnp.int32, (heads, 128), 0) - place.index * few
+        col = lax.broadcasted_iota(jnp.int32, (heads, 128), 1)
+        pick = (row == col) & (col < few)
+        wide = row == col // (128 // few)
+        step_o[...] = lax.dot_general(
+            step_ref[...], pick.astype(bf16), NN, preferred_element_type=f32
+        ).astype(bf16)
+        small_o[...] = jnp.zeros_like(small_o)
+        small_o[0:4, :] = taps_ref[:, lanes]
+        small_o[4:5, :] = bias_ref[:, lanes]
+        small_o[6:7, :] = norm_ref[:, lanes]
+        for at, head_ref, chosen in zip((5, 8, 9), head_refs, (wide, pick, pick)):
+            small_o[at : at + 1, :] = lax.dot_general(
+                jnp.broadcast_to(head_ref[...], (8, heads)),
+                chosen.astype(f32),
+                NN,
+                precision=highest,
+                preferred_element_type=f32,
+            )[0:1]
         for step in gather.steps():
             step()
         carried.settle()
@@ -1325,9 +1352,15 @@
     S = jax.ShapeDtypeStruct
     results = pl.pallas_call(
         kernel,
-        out_shape=[S((groups, ctx, tp // 2, 2, rows, width), bf16)] + move_outs,
-        in_specs=[IN_VMEM, IN_VMEM, IN_SMEM, IN_VMEM, IN_VMEM] + [IN_HBM] * n_moves,
-        out_specs=[IN_VMEM] + [IN_HBM] * n_moves,
+        out_shape=[
+            S((groups, ctx, tp // 2, 2, rows, width), bf16),
+            S((*shard[0].shape[:2], 128), bf16),
+            S((shard[1].shape[0], 128), bf16),
+            S((16, 128), f32),
+        ]
+        + move_outs,
+        in_specs=[IN_VMEM] * 3 + [IN_SMEM] + [IN_VMEM] * 10 + [IN_HBM] * n_moves,
+        out_specs=[IN_VMEM] * 4 + [IN_HBM] * n_moves,
         scratch_shapes=[pltpu.VMEM((rows, width), bf16)]
         + gather_sems(len(out_pieces), groups)
         + move_scratch,
@@ -1335,7 +1368,11 @@
         compiler_params=pltpu.CompilerParams(
             collective_id=number, has_side_effects=True, vmem_limit_bytes=62 * 2**20
         ),
-    )(hidden, embeds, lengths, gain.reshape(1, -1), down_maps, *[array for array, _, _ in moves])
+    )(
+        *(hidden, embeds, cotangent, lengths, gain.reshape(1, -1), down_maps),
+        *shard,
+        *[array for array, _, _ in moves],
+    )
     return [results[0].reshape(-1, width)] + list(results[1:])
 
 
@@ -1435,10 +1472,14 @@
 
 
 def adapter_products(xa, dmid, width):
-    block, rank = 512, dmid.shape[1] // 3
-
-    def kernel(a, b, o):
-        both = quick(b[...], a[...], TN)
+    block, rank = 1024, dmid.shape[1] // 3
+
+    def kernel(a, b, o, b_t):
+        @pl.when(pl.program_id(0) == 0)
+        def _():
+            b_t[...] = b[...].T
+
+        both = quick(b_t[...], a[...], NN)
         for j in range(3):
             o[j] = both[j * rank : (j + 1) * rank].T
 
@@ -1451,6 +1492,8 @@
             pl.BlockSpec(dmid.shape, lambda i: (0, 0)),
         ],
         out_specs=pl.BlockSpec((3, block, rank), lambda i: (0, i, 0)),
+        scratch_shapes=[pltpu.VMEM(dmid.shape[::-1], dmid.dtype)],
+        compiler_params=pltpu.CompilerParams(vmem_limit_bytes=60 * 2**20),
         name="adapter_products",
     )(xa, dmid)
 
@@ -1561,13 +1604,13 @@
         return values
 
 
-def mixer_forward(xn, cot, marked, mark_block, w_zx, w_step, state_map, w_out, small, bc_small, groups):
+def mixer_forward(xn, marked, mark_block, w_zx, w_step, state_map, w_out, small, bc_taps, bc_bias, groups):
     f32, bf16 = jnp.float32, jnp.bfloat16
     total, width = xn.shape
     rows, lanes = total // groups, w_zx.shape[2]
     state2 = state_map.shape[1]
 
-    def kernel(xn_r, cot_r, marks_r, zx_r, st_r, sm_r, wo_r, sml, bsml, z_o, xs_o, raw_o, bc_o, y_o, dyn_o, sums_o):
+    def kernel(xn_r, cot_r, marks_r, zx_r, st_r, sm_r, wo_r, sml, bt_r, bb_r, z_o, xs_o, raw_o, bc_o, y_o, dyn_o, sums_o):
         x = xn_r[...]
         z = quick(x, zx_r[0], NN)
         xs = quick(x, zx_r[1], NN).astype(bf16)
@@ -1575,7 +1618,7 @@
         bc = quick(x, sm_r[...], NN).astype(bf16)
         z_o[...], xs_o[...], raw_o[...], bc_o[...] = z, xs, raw, bc
         scan = Scan(
-            xs, raw, bc, marks_r[...].astype(f32), sml[0:4, :], sml[4:5, :], bsml[0:4, :], bsml[4:5, :], sml[8:10, :]
+            xs, raw, bc, marks_r[...].astype(f32), sml[0:4, :], sml[4:5, :], bt_r[...], bb_r[...], sml[8:10, :]
         )
         y = scan.forward(sml[5:6, :]).astype(bf16)
         y_o[...] = y
@@ -1596,8 +1639,9 @@
     return pl.pallas_call(
         kernel,
         grid=(groups,),
-        in_specs=[by_group(width), by_group(width), pl.BlockSpec((rows, 128), lambda g: (g, mark_block))]
-        + [whole(array) for array in (w_zx, w_step, state_map, w_out, small, bc_small)],
+        in_specs=[by_group(width), pl.BlockSpec((rows, width), lambda g: (g, 2))]
+        + [pl.BlockSpec((rows, 128), lambda g: (g, mark_block))]
+        + [whole(array) for array in (w_zx, w_step, state_map, w_out, small, bc_taps, bc_bias)],
         out_specs=[by_group(lanes)] * 3
         + [by_group(state2), by_group(lanes), by_group(lanes), pl.BlockSpec((1, 2, rows), lambda g: (g, 0, 0))],
         out_shape=[
@@ -1611,23 +1655,23 @@
         ],
         compiler_params=pltpu.CompilerParams(vmem_limit_bytes=60 * 2**20),
         name="mixer_forward",
-    )(xn, cot, marked, w_zx, w_step, state_map, w_out, small, bc_small)
-
-
-def mixer_backward(xn, cot, marked, mark_block, kept, sums, small, bc_small, groups):
+    )(xn, marked, marked, w_zx, w_step, state_map, w_out, small, bc_taps, bc_bias)
+
+
+def mixer_backward(xn, marked, mark_block, kept, sums, small, bc_taps, bc_bias, groups):
     f32, bf16 = jnp.float32, jnp.bfloat16
     z, xs, raw, bc, y, d_yn = kept
     total, width = xn.shape
     rows, lanes, state2 = total // groups, z.shape[1], bc.shape[1]
 
     def kernel(
-        xn_r, cot_r, marks_r, z_r, xs_r, raw_r, bc_r, y_r, dyn_r, sums_r, sml, bsml,
+        xn_r, cot_r, marks_r, z_r, xs_r, raw_r, bc_r, y_r, dyn_r, sums_r, sml, bt_r, bb_r,
         dz_o, dxs_o, draw_o, dbc_o, yn_o, gzx_o, gst_o, gout_o, gsm_o, gbc_o, acc_in, acc_out,
     ):
         group = pl.program_id(0)
         scan = Scan(
             xs_r[...], raw_r[...], bc_r[...], marks_r[...].astype(f32),
-            sml[0:4, :], sml[4:5, :], bsml[0:4, :], bsml[4:5, :], sml[8:10, :],
+            sml[0:4, :], sml[4:5, :], bt_r[...], bb_r[...], sml[8:10, :],
         )
         skip, gain = sml[5:6, :], sml[6:7, :]
         sums_wide = [jnp.broadcast_to(sums_r[0, i : i + 1], (128, rows)).T for i in range(2)]
@@ -1682,7 +1726,7 @@
             [exact(d_meet, scan.c_mat, TN), exact(d_meet, scan.b_mat, NN)], axis=1
         )
         d_bc, g_bc_taps = taps_backward(
-            d_bcc * silu_slope(scan.pre_bc), scan.bc, bsml[0:4, :], scan.position
+            d_bcc * silu_slope(scan.pre_bc), scan.bc, bt_r[...], scan.position
         )
         dbc_o[...] = d_bc.astype(bf16)
         in_part = quick(jnp.concatenate([d_z, d_xs, d_raw], axis=1), xn_r[...], TN)
@@ -1722,9 +1766,10 @@
     return pl.pallas_call(
         kernel,
         grid=(groups,),
-        in_specs=[by_group(width), by_group(width), pl.BlockSpec((rows, 128), lambda g: (g, mark_block))]
+        in_specs=[by_group(width), pl.BlockSpec((rows, width), lambda g: (g, 2))]
+        + [pl.BlockSpec((rows, 128), lambda g: (g, mark_block))]
         + [by_group(array.shape[1]) for array in kept]
-        + [pl.BlockSpec((1, 2, rows), lambda g: (g, 0, 0)), whole(small.shape), whole(bc_small.shape)],
+        + [pl.BlockSpec((1, 2, rows), lambda g: (g, 0, 0)), whole(small.shape), whole(bc_taps.shape), whole(bc_bias.shape)],
         out_specs=[by_group(lanes)] * 3
         + [by_group(state2), by_group(lanes)]
         + [
@@ -1749,7 +1794,7 @@
         scratch_shapes=[pltpu.VMEM((3 * lanes, width), f32), pltpu.VMEM((lanes, width), f32)],
         compiler_params=pltpu.CompilerParams(vmem_limit_bytes=60 * 2**20),
         name="mixer_backward",
-    )(xn, cot, marked, z, xs, raw, bc, y, d_yn, sums, small, bc_small)
+    )(xn, marked, marked, z, xs, raw, bc, y, d_yn, sums, small, bc_taps, bc_bias)
 
 
 def swap_halves(values):
@@ -1770,18 +1815,20 @@
     f32, bf16 = jnp.float32, jnp.bfloat16
     total, columns = xa.shape
     rows, rank = total // groups, up_maps.shape[1]
-
-    def kernel(xa_r, w_r, up_r, freq_r, ao_o, q_o, k_o, v_o, cos_o, sin_o, w_all):
+    side = columns - (3 * width) // 2
+    side_block = pl.BlockSpec((rows, side), lambda g: (g, columns // side - 1))
+
+    def kernel(xa_r, side_r, w_r, up_r, freq_r, ao_o, q_o, k_o, v_o, cos_o, sin_o, w_all):
         @pl.when(pl.program_id(0) == 0)
         def _():
             for j in range(3):
                 w_all[:, j * AHD : (j + 1) * AHD] = w_r[j]
 
-        marks = xa_r[:, width + 3 * rank :].astype(f32)
-        wide = quick(xa_r[:, :width], w_all[...], NN)
+        marks = side_r[:, 3 * rank :].astype(f32)
+        wide = quick(xa_r[...], w_all[...], NN)
         proj = []
         for j in range(3):
-            mid = xa_r[:, width + j * rank : width + (j + 1) * rank]
+            mid = side_r[:, j * rank : (j + 1) * rank]
             proj.append((wide[:, j * AHD : (j + 1) * AHD] + quick(mid, up_r[j], NN)).astype(bf16))
         angle = marks[:, 1:2] * freq_r[...]
         lane = lax.broadcasted_iota(jnp.int32, angle.shape, 1)
@@ -1806,28 +1853,30 @@
     return pl.pallas_call(
         kernel,
         grid=(groups,),
-        in_specs=[by_group(columns), whole(w_qkv), whole(up_maps), whole(frequencies)],
+        in_specs=[by_group(width), side_block, whole(w_qkv), whole(up_maps), whole(frequencies)],
         out_specs=[by_group(AHD)] * 6,
         out_shape=[S((total, AHD), bf16)] * 4 + [S((total, AHD), f32)] * 2,
         scratch_shapes=[pltpu.VMEM((width, 3 * AHD), bf16)],
         compiler_params=pltpu.CompilerParams(vmem_limit_bytes=60 * 2**20),
         name="attention_forward",
-    )(xa, w_qkv, up_maps, frequencies)
+    )(xa, xa, w_qkv, up_maps, frequencies)
 
 
 def attention_backward(d_attn, xa, width, w_o, up_maps, kept, groups):
     f32, bf16 = jnp.float32, jnp.bfloat16
     total, columns = xa.shape
     rows, rank = total // groups, up_maps.shape[1]
+    side = columns - (3 * width) // 2
+    side_block = pl.BlockSpec((rows, side), lambda g: (g, columns // side - 1))
     model = d_attn.shape[1]
 
     def kernel(
-        da_r, xa_r, wo_r, up_r, ao_r, q_r, k_r, v_r, cos_r, sin_r,
+        da_r, xa_r, side_r, wo_r, up_r, ao_r, q_r, k_r, v_r, cos_r, sin_r,
         dq_o, dk_o, dv_o, dmid_o, gw_o, go_o, gup_o, acc_w, acc_o,
     ):
         group = pl.program_id(0)
         d_rows = da_r[...]
-        marks = xa_r[:, width + 3 * rank :].astype(f32)
+        marks = side_r[:, 3 * rank :].astype(f32)
         d_ao = quick(d_rows, wo_r[...], NT).astype(bf16)
         qr, kr, vals = q_r[...], k_r[...], v_r[...]
         weights = attend_weights(qr, kr, marks, rows)
@@ -1844,10 +1893,10 @@
         for j, out in enumerate((dq_o, dk_o, dv_o)):
             out[...] = pieces[j]
             dmid_o[:, j * rank : (j + 1) * rank] = quick(pieces[j], up_r[j], NT).astype(bf16)
-        part = quick(jnp.concatenate(pieces, axis=1), xa_r[:, :width], TN)
+        part = quick(jnp.concatenate(pieces, axis=1), xa_r[...], TN)
         part_o = quick(ao_r[...], d_rows, TN)
         parts_up = [
-            quick(xa_r[:, width + j * rank : width + (j + 1) * rank], pieces[j], TN)
+            quick(side_r[:, j * rank : (j + 1) * rank], pieces[j], TN)
             for j in range(3)
         ]
 
@@ -1880,7 +1929,7 @@
     return pl.pallas_call(
         kernel,
         grid=(groups,),
-        in_specs=[by_group(model), by_group(columns), whole(w_o.shape), whole(up_maps.shape)]
+        in_specs=[by_group(model), by_group(width), side_block, whole(w_o.shape), whole(up_maps.shape)]
         + [by_group(AHD)] * 6,
         out_specs=[by_group(AHD)] * 3
         + [by_group(3 * rank)]
@@ -1895,7 +1944,7 @@
         scratch_shapes=[pltpu.VMEM((3 * AHD, width), f32), pltpu.VMEM((AHD, model), f32)],
         compiler_params=pltpu.CompilerParams(vmem_limit_bytes=60 * 2**20),
         name="attention_backward",
-    )(d_attn, xa, w_o, up_maps, *kept)
+    )(d_attn, xa, xa, w_o, up_maps, *kept)
 
 
 def per_device_split(
@@ -1940,30 +1989,31 @@
     def own_rows(values):
         return lax.dynamic_slice_in_dim(values, start, mine, 0)
 
-    def own_part(values, axis=0):
-        width = values.shape[axis] // plane_size
-        return lax.dynamic_slice_in_dim(values, plane_index * width, width, axis)
-
     width = hidden.shape[1]
     own_shape = (mine, width)
     cot_low = own_rows(cotangent)
 
-    up_maps = own_part(adapter_up_maps, 2)
-    w_step = own_part(step_size_weight, 1)
-    taps, tap_bias = own_part(mixer_input_taps, 1), own_part(mixer_input_tap_bias)
-    step_bias, decay_rate = own_part(step_size_bias), own_part(log_decay_rate)
-    skip, gate_gain = own_part(head_skip_weight), own_part(gated_norm_gain)
-
     rank = adapter_down_maps.shape[2]
     width_a = adapter_down_maps.shape[1]
-    xa_wide, w_o, w_qkv = opening(
+    xa_wide, up_maps, w_step, small, w_o, w_qkv = opening(
         sizes,
         1,
         hidden,
         embeds,
+        cotangent,
         lengths,
         attention_norm_gain,
         adapter_down_maps,
+        [
+            adapter_up_maps,
+            step_size_weight,
+            mixer_input_taps,
+            mixer_input_tap_bias[None],
+            gated_norm_gain[None],
+            head_skip_weight[None],
+            step_size_bias[None],
+            log_decay_rate[None],
+        ],
         [(attention_output_weight, 0, 1), (query_key_value_weight, 2, 1)],
     )
     half = AHD // 2
@@ -1998,34 +2048,19 @@
         [own_shape],
         width,
         [(mixer_gate_input_weight, 2, 1), (mixer_output_weight, 0, 1)],
-        plan=(),
-        also_gather=cot_low,
-    )
-    xn, cot, (after_mlp,) = found["gathered"], found["also"], found["finish"]
+        plan=(6,),
+    )
+    xn, (after_mlp,) = found["gathered"], found["finish"]
     w_zx, w_out = found["moves"]
-    few = step_bias.shape[0]
-    lanes = ((0, 0), (0, 128 - few))
-    row_of = lambda part: jnp.pad(part[None], lanes)
-    small = jnp.concatenate(
-        [
-            taps,
-            tap_bias[None],
-            jnp.repeat(skip, MIXER_HEAD_SIZE)[None],
-            gate_gain[None],
-            jnp.zeros((1, 128), f32),
-            row_of(step_bias),
-            row_of(decay_rate),
-        ]
-    )
-    bc_small = jnp.concatenate([state_map_taps, state_map_tap_bias[None]])
-    mark_block = (width_a + 3 * rank) // 128
-    w_step = jnp.pad(w_step, lanes)
+    few = step_size_weight.shape[1] // plane_size
+    bc_bias = state_map_tap_bias[None]
+    mark_block = (3 * width + 3 * rank) // 128
     *kept, sums = mixer_forward(
-        xn, cot, xa_wide, mark_block, w_zx, w_step, state_map_weight, w_out, small, bc_small, groups
+        xn, xa_wide, mark_block, w_zx, w_step, state_map_weight, w_out, small, state_map_taps, bc_bias, groups
     )
     sums = sum_small(sizes, 4, sums)
     d_z, d_xs, d_step, d_bc_part, yn_low, grad_w_zx, grad_w_dt, grad_w_out, few_x, few_bc = (
-        mixer_backward(xn, cot, xa_wide, mark_block, kept, sums, small, bc_small, groups)
+        mixer_backward(xn, xa_wide, mark_block, kept, sums, small, state_map_taps, bc_bias, groups)
     )
     grad_conv_bc, grad_conv_bc_bias = few_bc[:4], few_bc[4]
     found = exchange(

time: 972 us -> 961 us (0.989)
    pallas_call x1, Pallas kernels: 125 us -> 152 us  [opening(): pl.pallas_call(kernel, out_shape=[S((groups, ctx, tp // 2, 2, rows, width...]
    pallas_call x5, Pallas kernels: 641 us -> 614 us  [exchange(): pl.pallas_call(kernel, out_shape=out_shape, in_specs=in_specs, out_specs=...]
where the time goes in v6:
time: 961 us; the launch traced here: 951 us
  Pallas kernels  889 us (93%)
  matrix products  24.9 us (3%)
  other arithmetic  20.7 us (2%)
  local copies, waits for them, and re-layouts  14.4 us (1%)
    pallas_call x5, Pallas kernels, exchange(): pl.pallas_call(kernel, out_shape=out_shape, in_specs=in_specs, out_specs=...  614 us
    pallas_call x1, Pallas kernels, opening(): pl.pallas_call(kernel, out_shape=[S((groups, ctx, tp // 2, 2, rows, width...  152 us
    pallas_call x1, Pallas kernels, mixer_backward(): pl.pallas_call(kernel, grid=(groups,), in_specs=[by_group(width), pl.Bloc...  30.5 us
    pallas_call x1, Pallas kernels, attention_backward(): pl.pallas_call(kernel, grid=(groups,), in_specs=[by_group(model), by_grou...  26.1 us
    pallas_call x1, Pallas kernels, mixer_forward(): pl.pallas_call(kernel, grid=(groups,), in_specs=[by_group(width), pl.Bloc...  24.6 us

profile of v6, /device:TPU:0, one launch (start us, length us, event | category | flops | bytes accessed | tf_op | source)
XLA Modules:
  0.0 950.7 jit_solution(5684296250690817565)
XLA Ops:
  0.7 0.6 maximum_bitcast_fusion.freq_r
  1.3 1.6 constant_dynamic-slice_fusion.refs_8_
  2.9 1.8 copy.51.refs_7_
  4.7 151.9 %opening_1.1 = (bf16[4,2,2,2,48,6656]{5,4,3,2,1,0:T(8,128)(2,1)}, bf16[3,128,128]{2,1,0:T(8,128)(2,1)}, bf16[2048,128]{1,0:T(8,128)(2,1)}, f32[16,128]{1,0:T(8,1...) custom-call(bf16[192,2048]{1,0:T(8,128)(2,1)} %refs_5_.7, bf16[192,2048]{1,0:T(8,128)(2,1)} %refs_6_.3, ...), custom_call_target="tpu_custom_call" | custom-call | tf_op jit(solution)/shard_map/opening_1/pallas_call | solution.py:1353
  156.7 16.3 %attention_forward.1 = (bf16[1536,128]{1,0:T(8,128)(2,1)}, bf16[1536,128]{1,0:T(8,128)(2,1)}, bf16[1536,128]{1,0:T(8,128)(2,1)}, bf16[1536,128]{1,0:T(8,128)(2,1...) custom-call(bf16[1536,6656]{1,0:T(8,128)(2,1)} %bitcast.82, bf16[1536,6656]{1,0:T(8,128)(2,1)} %bitcast.83, ...), custom_call_target="tpu_custom_call" | custom-call | tf_op jit(solution)/shard_map/attention_forward/pallas_call | solution.py:1853
  173.0 120.4 %exchange_2.1 = (bf16[4,2,2,2,48,2048]{5,4,3,2,1,0:T(8,128)(2,1)}, f32[48,2048]{1,0:T(8,128)}, bf16[2,2048,256]{2,1,0:T(8,128)(2,1)}, bf16[256,2048]{1,0:T(8,128)(2,1)}) custom-call(bf16[4,2,2,2,48,128]{5,4,3,2,1,0:T(8,128)(2,1)} %bitcast.96, bf16[128,2048]{1,0:T(8,128)(2,1)} %get-tuple-element.90.refs_1_.wo_r, bf16[192,2048]{1,0:T(8,128)(2,1)} %refs_5_.7, ...), custom_call_target="tpu_custom_call" | custom-call | tf_op jit(solution)/shard_map/exchange_2/pallas_call | solution.py:1226
  293.4 5.1 fusion.18
  298.5 0.0 copy-done.3
  298.5 0.4 copy-done.17
  299.0 3.6 multiply_convert_fusion.1
  302.6 95.0 %exchange_3.1 = (bf16[4,2,2,2,48,2048]{5,4,3,2,1,0:T(8,128)(2,1)}, f32[48,2048]{1,0:T(8,128)}, bf16[2,2048,128]{2,1,0:T(8,128)(2,1)}, bf16[128,2048]{1,0:T(8,128)(2,1)}) custom-call(bf16[4,2,2,2,48,256]{5,4,3,2,1,0:T(8,128)(2,1)} %bitcast.102, bf16[256,2048]{1,0:T(8,128)(2,1)} %get-tuple-element.93.refs_1_, f32[48,2048]{1,0:T(8,128)} %get-tuple-element.94.refs_2_.refs_3_, ...), custom_call_target="tpu_custom_call" | custom-call | tf_op jit(solution)/shard_map/exchange_3/pallas_call | solution.py:1226
  397.5 24.6 %mixer_forward.1 = (f32[1536,128]{1,0:T(8,128)}, bf16[1536,128]{1,0:T(8,128)(2,1)}, bf16[1536,128]{1,0:T(8,128)(2,1)}, bf16[1536,256]{1,0:T(8,128)(2,1)}, bf16[1...) custom-call(bf16[1536,2048]{1,0:T(8,128)(2,1)} %bitcast.91, bf16[1536,6656]{1,0:T(8,128)(2,1)} %bitcast.84, ...), custom_call_target="tpu_custom_call" | custom-call | tf_op jit(solution)/shard_map/mixer_forward/pallas_call | solution.py:1639
  422.2 14.3 %sum_small_4.1.sums_r = f32[4,2,384]{2,1,0:T(2,128)} custom-call(f32[4,2,384]{2,1,0:T(2,128)} %get-tuple-element.106.x), custom_call_target="tpu_custom_call" | custom-call | tf_op jit(solution)/shard_map/sum_small_4/pallas_call | solution.py:1389
  436.5 30.5 %mixer_backward.1 = (bf16[1536,128]{1,0:T(8,128)(2,1)}, bf16[1536,128]{1,0:T(8,128)(2,1)}, bf16[1536,128]{1,0:T(8,128)(2,1)}, bf16[1536,256]{1,0:T(8,128)(2,1)},...) custom-call(bf16[1536,2048]{1,0:T(8,128)(2,1)} %bitcast.92, ...), custom_call_target="tpu_custom_call" | custom-call | tf_op jit(solution)/shard_map/mixer_backward/pallas_call | solution.py:1766
  466.9 0.7 slice.91
  467.6 0.7 slice_bitcast_fusion.1
  468.3 0.7 convert.8
  469.0 0.8 slice.149
  469.9 0.6 pad_maximum_fusion.2.refs_15_
  470.5 130.2 %exchange_5.1 = (bf16[4,2,2,2,48,2304]{5,4,3,2,1,0:T(8,128)(2,1)}, f32[48,2048]{1,0:T(8,128)}, f32[1,2048]{1,0:T(1,128)}, bf16[48,2048]{1,0:T(8,128)(2,1)}, bf16...) custom-call(bf16[4,2,2,2,48,128]{5,4,3,2,1,0:T(8,128)(2,1)} %bitcast.105, bf16[4,2,2,2,48,128]{5,4,3,2,1,0:T(8,128)(2,1)} %bitcast.106, ...), custom_call_target="tpu_custom_call" | custom-call | tf_op jit(solution)/shard_map/exchange_5/pallas_call | solution.py:1226
  600.7 0.0 copy-start.18
  600.7 0.0 slice-start
  600.7 6.3 fusion.22
  607.1 0.0 copy-done.6
  607.1 0.0 copy-done.18
  607.1 0.0 copy-start.10
  607.1 0.0 slice-start.1
  607.1 3.1 multiply_convert_fusion
  610.3 0.0 copy-start.7
  610.3 0.0 copy-start.8
  610.3 2.8 fusion.4.refs_7_
  613.1 2.0 fusion.8
  615.1 2.0 fusion.7
  617.1 1.5 pad_maximum_fusion.refs_6_
  618.6 0.0 copy-done.11
  618.6 1.0 convert_element_type.68
  619.7 1.6 convert_element_type.66
  621.2 114.0 %exchange_6.1 = (bf16[4,2,2,2,48,2048]{5,4,3,2,1,0:T(8,128)(2,1)}, f32[48,2048]{1,0:T(8,128)}, f32[1,2048]{1,0:T(1,128)}, bf16[2,256,2048]{2,1,0:T(8,128)(2,1)}, bf16[2048,256]{1,0:T(8,128)(2,1)}) custom-call(bf16[4,2,2,2,48,256]{5,4,3,2,1,0:T(8,128)(2,1)} %bitcast.101, bf16[4,2,2,2,48,256]{5,4,3,2,1,0:T(8,128)(2,1)} %bitcast.100, ...), custom_call_target="tpu_custom_call" | custom-call | tf_op jit(solution)/shard_map/exchange_6/pallas_call | solution.py:1226
  735.2 26.1 %attention_backward.1 = (bf16[1536,128]{1,0:T(8,128)(2,1)}, bf16[1536,128]{1,0:T(8,128)(2,1)}, bf16[1536,128]{1,0:T(8,128)(2,1)}, bf16[1536,384]{1,0:T(8,128)(2,...) custom-call(bf16[1536,2048]{1,0:T(8,128)(2,1)} %bitcast.94, ...), custom_call_target="tpu_custom_call" | custom-call | tf_op jit(solution)/shard_map/attention_backward/pallas_call | solution.py:1929
  761.4 0.6 broadcast_in_dim.31.refs_11_
  762.0 1.6 convert_element_type.58.refs_14_
  763.6 154.8 %exchange_7.1 = (bf16[4,2,2,2,48,384]{5,4,3,2,1,0:T(8,128)(2,1)}, bf16[2,2,48,6144]{3,2,1,0:T(8,128)(2,1)}, f32[1,9472]{1,0:T(1,128)}, bf16[3,512,1024]{2,1,0:T(...) custom-call(bf16[4,2,2,2,48,128]{5,4,3,2,1,0:T(8,128)(2,1)} %bitcast.109, ...), custom_call_target="tpu_custom_call" | custom-call | tf_op jit(solution)/shard_map/exchange_7/pallas_call | solution.py:1226
  918.4 11.2 %adapter_products.1 = f32[3,4096,128]{2,1,0:T(8,128)} custom-call(bf16[1536,6656]{1,0:T(8,128)(2,1)} %bitcast.90, bf16[1536,384]{1,0:T(8,128)(2,1)} %bitcast.98), custom_call_target="tpu_custom_call" | custom-call | tf_op jit(solution)/shard_map/adapter_products/pallas_call | solution.py:1486
  929.6 0.6 slice.107
  930.1 0.6 fusion.25
  930.7 0.6 reshape.176
  931.3 0.6 slice.120
  932.0 0.6 slice.96
  932.6 0.6 fusion.26
  933.3 0.6 reshape_squeeze.10
  933.8 0.6 reshape_squeeze.9
  934.6 0.7 copy.58
  935.3 0.1 reshape_squeeze.11
  935.3 0.1 reduce_sum.9
  935.4 0.6 reshape.178
  936.0 2.1 convert_element_type.63
  938.1 1.3 convert_element_type.62
  939.4 0.0 copy-done.1
  939.4 2.1 slice_convert_fusion
  941.5 1.5 convert_element_type.65
  943.0 0.9 copy-done.2
  943.9 2.5 convert_element_type.64
  946.4 0.3 copy-done
  946.8 3.4 convert_element_type.61
  (41 shorter events, 0.3 us)
Async XLA Ops:
  293.4 5.1 copy-start.3
  293.4 5.5 copy-start.17
  600.7 6.4 copy-start.6
  600.7 6.4 copy-start.16
  600.7 6.4 copy-start.18
  600.7 12.3 %slice-start = ((s8[6291456]{0:T(1024)(128)(4,1)}), s8[4194304]{0:T(1024)(128)(4,1)S(1)}, s32[]{:S(2)}) async-start(s8[6291456]{0:T(1024)(128)(4,1)} %bitcast.142), calls=%async_computation | async-start | bytes 8388608
  607.1 3.2 copy-start.10
  607.1 6.0 slice-start.1
  610.3 2.8 copy-start.7
  610.3 4.8 copy-start.8
  617.1 1.5 copy-start.11
  617.1 2.6 copy-start.5
  735.2 26.2 %copy-start.14 = (f32[1,2048]{1,0:T(1,128)S(1)}, f32[1,2048]{1,0:T(1,128)}, u32[]{:S(2)}) copy-start(f32[1,2048]{1,0:T(1,128)} %get-tuple-element.130) | copy-start | bytes 24580
  735.2 26.2 %copy-start.15 = (f32[1,2048]{1,0:T(1,128)S(1)}, f32[1,2048]{1,0:T(1,128)}, u32[]{:S(2)}) copy-start(f32[1,2048]{1,0:T(1,128)} %get-tuple-element.129) | copy-start | bytes 24580
  918.4 11.2 %copy-start.13 = (f32[1,9472]{1,0:T(1,128)S(1)}, f32[1,9472]{1,0:T(1,128)}, u32[]{:S(2)}) copy-start(f32[1,9472]{1,0:T(1,128)} %get-tuple-element.138) | copy-start | bytes 113668
  918.4 11.8 %copy-start.12 = (bf16[48,1024]{1,0:T(8,128)(2,1)S(1)}, bf16[48,1024]{1,0:T(8,128)(2,1)}, u32[]{:S(2)}) copy-start(bf16[48,1024]{1,0:T(8,128)(2,1)} %get-tuple-element.146) | copy-start | bytes 294916
  929.6 8.5 copy-start.9
  934.6 4.9 copy-start.1
  939.4 2.1 copy-start.4
  941.5 2.3 copy-start.2
  943.9 2.9 copy-start

commit v7 on v6

--- a/solution.py
+++ b/solution.py
@@ -801,6 +801,39 @@
             copy.wait_send()
 
 
+class PlaneGather:
+    def __init__(self, place, x, o, zs, zr, ss, sr, own_sem):
+        self.place, self.x, self.o, self.zs, self.zr = place, x, o, zs, zr
+        self.ss, self.sr, self.own_sem = ss, sr, own_sem
+
+    def line_copy(self, d, owner):
+        place = self.place
+        to = self.o.at[owner, place.c]
+        return remote(self.x, to, self.zs.at[d], self.zr.at[d], place.line[d])
+
+    def begin(self):
+        place = self.place
+        self.own = pltpu.make_async_copy(self.x, self.o.at[place.g, place.c], self.own_sem)
+        self.own.start()
+        for d in range(place.groups - 1):
+            self.line_copy(d, place.g).start()
+
+    def step(self):
+        place = self.place
+        self.own.wait()
+        for d in range(place.groups - 1):
+            self.line_copy(d, lax.rem(place.g + place.groups - d - 1, place.groups)).wait_recv()
+        part = self.o.at[:, place.c]
+        self.onward = remote(part, part, self.ss, self.sr, place.side_x)
+        self.onward.start()
+
+    def end(self):
+        self.onward.wait_recv()
+        self.onward.wait_send()
+        for d in range(self.place.groups - 1):
+            self.line_copy(d, self.place.g).wait_send()
+
+
 def pipelined(count, stages, lags):
     def step(at):
         for stage, lag in zip(stages, lags):
@@ -1085,6 +1118,7 @@
     also_sum=None,
     tail=0,
     small=0,
+    spread=None,
 ):
     groups, ctx, tp = sizes
     f32, bf16 = jnp.float32, jnp.bfloat16
@@ -1138,6 +1172,10 @@
     if small:
         o_small = add_out([S((1, small), f32)])
         s_small = add_scratch([pltpu.VMEM((1, small), f32)] + small_scratch((1, small), groups))
+    if spread is not None:
+        in_spread = add_in([spread])
+        o_spread = add_out([S((groups, ctx, *spread.shape), spread.dtype)])
+        s_spread = add_scratch([DMA((groups - 1,)), DMA((groups - 1,)), DMA, DMA, DMA])
     in_moves = add_in([array for array, _, _ in moves], IN_HBM)
     o_moves = add_out(move_outs, IN_HBM)
     s_moves = add_scratch(move_scratch)
@@ -1170,6 +1208,11 @@
             side_gather.begin()
             streams.append((start_also, side_gather.steps()))
             ends.append(side_gather)
+        if spread is not None:
+            plane = PlaneGather(place, ins[in_spread][0], outs[o_spread][0], *scr[s_spread])
+            plane.begin()
+            streams.append((6, [plane.step]))
+            ends.append(plane)
         later = []
         if also_sum is not None:
             side_sum = second.stage(place, ins[in_second], scr[s_second])
@@ -1243,6 +1286,8 @@
         found["tail"] = results[o_tail][0].reshape(-1, tail)
     if small:
         found["small"] = results[o_small][0]
+    if spread is not None:
+        found["spread"] = results[o_spread][0]
     found["moves"] = results[o_moves]
     return found
 
@@ -2137,15 +2182,18 @@
         [
             (grad_w_qkv, 1, 2),
             (grad_w_o, 1, 0),
-            (adapter_up_gradient.astype(bf16), None, 2),
-            (shares, None, 1),
         ],
         plan=(5,),
         tail=3 * width,
         small=width_a + row.shape[1],
+        spread=jnp.concatenate([adapter_up_gradient.reshape(-1, 128).astype(bf16), shares]),
     )
     dmid, back, row = found["gathered"], found["tail"], found["small"][0]
-    grad_w_qkv, grad_w_o, adapter_up_gradient, shared = found["moves"]
+    grad_w_qkv, grad_w_o = found["moves"]
+    shared = found["spread"].reshape(plane_size, -1, 128)
+    adapter_up_gradient = shared[:, : 3 * rank].reshape(plane_size, 3, rank, 128)
+    adapter_up_gradient = adapter_up_gradient.transpose(1, 2, 0, 3).reshape(3, rank, -1)
+    shared = shared[:, 3 * rank :].transpose(1, 0, 2).reshape(-1, plane_size * 128)
     adapter_down_gradient = adapter_products(xa_wide, dmid, width_a)
     result = back[:, :width]
     d_hidden = back[:, width : 2 * width].astype(f32)

time: 961 us -> 953 us (level)
  no operation moved by 1% of the time
where the time goes in v7:
time: 953 us; the launch traced here: 943 us
  Pallas kernels  880 us (92%)
  matrix products  24.9 us (3%)
  other arithmetic  19.4 us (2%)
  local copies, waits for them, and re-layouts  16.7 us (2%)
    pallas_call x5, Pallas kernels, exchange(): pl.pallas_call(kernel, out_shape=out_shape, in_specs=in_specs, out_specs=...  605 us
    pallas_call x1, Pallas kernels, opening(): pl.pallas_call(kernel, out_shape=[S((groups, ctx, tp // 2, 2, rows, width...  152 us
    pallas_call x1, Pallas kernels, mixer_backward(): pl.pallas_call(kernel, grid=(groups,), in_specs=[by_group(width), pl.Bloc...  30.5 us
    pallas_call x1, Pallas kernels, attention_backward(): pl.pallas_call(kernel, grid=(groups,), in_specs=[by_group(model), by_grou...  26.1 us
    pallas_call x1, Pallas kernels, mixer_forward(): pl.pallas_call(kernel, grid=(groups,), in_specs=[by_group(width), pl.Bloc...  24.6 us

profile of v7, /device:TPU:0, one launch (start us, length us, event | category | flops | bytes accessed | tf_op | source)
XLA Modules:
  0.0 942.7 jit_solution(9308795502904165545)
XLA Ops:
  0.7 0.6 maximum_bitcast_fusion.freq_r
  1.3 1.6 constant_dynamic-slice_fusion.refs_8_
  2.9 1.8 copy.53.refs_7_
  4.7 152.0 %opening_1.1 = (bf16[4,2,2,2,48,6656]{5,4,3,2,1,0:T(8,128)(2,1)}, bf16[3,128,128]{2,1,0:T(8,128)(2,1)}, bf16[2048,128]{1,0:T(8,128)(2,1)}, f32[16,128]{1,0:T(8,1...) custom-call(bf16[192,2048]{1,0:T(8,128)(2,1)} %refs_5_.7, bf16[192,2048]{1,0:T(8,128)(2,1)} %refs_6_.3, ...), custom_call_target="tpu_custom_call" | custom-call | tf_op jit(solution)/shard_map/opening_1/pallas_call | solution.py:1398
  156.7 16.3 %attention_forward.1 = (bf16[1536,128]{1,0:T(8,128)(2,1)}, bf16[1536,128]{1,0:T(8,128)(2,1)}, bf16[1536,128]{1,0:T(8,128)(2,1)}, bf16[1536,128]{1,0:T(8,128)(2,1...) custom-call(bf16[1536,6656]{1,0:T(8,128)(2,1)} %bitcast.91, bf16[1536,6656]{1,0:T(8,128)(2,1)} %bitcast.92, ...), custom_call_target="tpu_custom_call" | custom-call | tf_op jit(solution)/shard_map/attention_forward/pallas_call | solution.py:1898
  173.0 120.5 %exchange_2.1 = (bf16[4,2,2,2,48,2048]{5,4,3,2,1,0:T(8,128)(2,1)}, f32[48,2048]{1,0:T(8,128)}, bf16[2,2048,256]{2,1,0:T(8,128)(2,1)}, bf16[256,2048]{1,0:T(8,128)(2,1)}) custom-call(bf16[4,2,2,2,48,128]{5,4,3,2,1,0:T(8,128)(2,1)} %bitcast.107, bf16[128,2048]{1,0:T(8,128)(2,1)} %get-tuple-element.89.refs_1_.wo_r, bf16[192,2048]{1,0:T(8,128)(2,1)} %refs_5_.7, ...), custom_call_target="tpu_custom_call" | custom-call | tf_op jit(solution)/shard_map/exchange_2/pallas_call | solution.py:1269
  293.5 0.0 copy-start.2
  293.5 0.0 copy-start.16
  293.5 5.1 fusion.18
  298.6 0.4 copy-done.16
  299.0 3.6 multiply_convert_fusion.1
  302.6 94.9 %exchange_3.1 = (bf16[4,2,2,2,48,2048]{5,4,3,2,1,0:T(8,128)(2,1)}, f32[48,2048]{1,0:T(8,128)}, bf16[2,2048,128]{2,1,0:T(8,128)(2,1)}, bf16[128,2048]{1,0:T(8,128)(2,1)}) custom-call(bf16[4,2,2,2,48,256]{5,4,3,2,1,0:T(8,128)(2,1)} %bitcast.115, bf16[256,2048]{1,0:T(8,128)(2,1)} %get-tuple-element.92.refs_1_, f32[48,2048]{1,0:T(8,128)} %get-tuple-element.93.refs_2_.refs_3_, ...), custom_call_target="tpu_custom_call" | custom-call | tf_op jit(solution)/shard_map/exchange_3/pallas_call | solution.py:1269
  397.5 24.6 %mixer_forward.1 = (f32[1536,128]{1,0:T(8,128)}, bf16[1536,128]{1,0:T(8,128)(2,1)}, bf16[1536,128]{1,0:T(8,128)(2,1)}, bf16[1536,256]{1,0:T(8,128)(2,1)}, bf16[1...) custom-call(bf16[1536,2048]{1,0:T(8,128)(2,1)} %bitcast.100, bf16[1536,6656]{1,0:T(8,128)(2,1)} %bitcast.93, ...), custom_call_target="tpu_custom_call" | custom-call | tf_op jit(solution)/shard_map/mixer_forward/pallas_call | solution.py:1684
  422.2 14.3 %sum_small_4.1.sums_r = f32[4,2,384]{2,1,0:T(2,128)} custom-call(f32[4,2,384]{2,1,0:T(2,128)} %get-tuple-element.105.x), custom_call_target="tpu_custom_call" | custom-call | tf_op jit(solution)/shard_map/sum_small_4/pallas_call | solution.py:1434
  436.5 30.5 %mixer_backward.1 = (bf16[1536,128]{1,0:T(8,128)(2,1)}, bf16[1536,128]{1,0:T(8,128)(2,1)}, bf16[1536,128]{1,0:T(8,128)(2,1)}, bf16[1536,256]{1,0:T(8,128)(2,1)},...) custom-call(bf16[1536,2048]{1,0:T(8,128)(2,1)} %bitcast.101, ...), custom_call_target="tpu_custom_call" | custom-call | tf_op jit(solution)/shard_map/mixer_backward/pallas_call | solution.py:1811
  467.0 0.7 slice.104
  467.7 0.7 slice_bitcast_fusion.3
  468.4 0.7 convert.13
  469.1 0.8 slice.168
  470.0 130.1 %exchange_5.1 = (bf16[4,2,2,2,48,2304]{5,4,3,2,1,0:T(8,128)(2,1)}, f32[48,2048]{1,0:T(8,128)}, f32[1,2048]{1,0:T(1,128)}, bf16[48,2048]{1,0:T(8,128)(2,1)}, bf16...) custom-call(bf16[4,2,2,2,48,128]{5,4,3,2,1,0:T(8,128)(2,1)} %bitcast.118, bf16[4,2,2,2,48,128]{5,4,3,2,1,0:T(8,128)(2,1)} %bitcast.119, ...), custom_call_target="tpu_custom_call" | custom-call | tf_op jit(solution)/shard_map/exchange_5/pallas_call | solution.py:1269
  600.1 0.0 copy-start.17
  600.1 0.0 slice-start
  600.1 6.3 fusion.22
  606.5 0.0 copy-start.9
  606.5 0.0 slice-start.1
  606.5 3.1 multiply_convert_fusion
  609.7 0.0 copy-start.7
  609.7 0.0 copy-start.8
  609.7 2.8 fusion.4.refs_7_
  612.5 2.0 fusion.8
  614.5 2.0 fusion.7
  616.5 1.5 pad_maximum_fusion.refs_6_
  618.0 1.0 convert_element_type.91
  619.1 0.6 copy-done.4
  619.6 1.6 convert_element_type.88
  621.2 114.0 %exchange_6.1 = (bf16[4,2,2,2,48,2048]{5,4,3,2,1,0:T(8,128)(2,1)}, f32[48,2048]{1,0:T(8,128)}, f32[1,2048]{1,0:T(1,128)}, bf16[2,256,2048]{2,1,0:T(8,128)(2,1)}, bf16[2048,256]{1,0:T(8,128)(2,1)}) custom-call(bf16[4,2,2,2,48,256]{5,4,3,2,1,0:T(8,128)(2,1)} %bitcast.114, bf16[4,2,2,2,48,256]{5,4,3,2,1,0:T(8,128)(2,1)} %bitcast.113, ...), custom_call_target="tpu_custom_call" | custom-call | tf_op jit(solution)/shard_map/exchange_6/pallas_call | solution.py:1269
  735.2 26.1 %attention_backward.1 = (bf16[1536,128]{1,0:T(8,128)(2,1)}, bf16[1536,128]{1,0:T(8,128)(2,1)}, bf16[1536,128]{1,0:T(8,128)(2,1)}, bf16[1536,384]{1,0:T(8,128)(2,...) custom-call(bf16[1536,2048]{1,0:T(8,128)(2,1)} %bitcast.104, ...), custom_call_target="tpu_custom_call" | custom-call | tf_op jit(solution)/shard_map/attention_backward/pallas_call | solution.py:1974
  761.3 0.6 broadcast_in_dim.31.refs_11_
  762.0 0.9 convert_element_type.76
  762.9 0.7 pad_maximum_fusion.1.refs_12_
  763.6 145.6 %exchange_7.1 = (bf16[4,2,2,2,48,384]{5,4,3,2,1,0:T(8,128)(2,1)}, bf16[2,2,48,6144]{3,2,1,0:T(8,128)(2,1)}, f32[1,9472]{1,0:T(1,128)}, bf16[4,2,432,128]{3,2,1,0...) custom-call(bf16[4,2,2,2,48,128]{5,4,3,2,1,0:T(8,128)(2,1)} %bitcast.123, ...), custom_call_target="tpu_custom_call" | custom-call | tf_op jit(solution)/shard_map/exchange_7/pallas_call | solution.py:1269
  909.2 11.2 %adapter_products.1 = f32[3,4096,128]{2,1,0:T(8,128)} custom-call(bf16[1536,6656]{1,0:T(8,128)(2,1)} %bitcast.99, bf16[1536,384]{1,0:T(8,128)(2,1)} %bitcast.109), custom_call_target="tpu_custom_call" | custom-call | tf_op jit(solution)/shard_map/adapter_products/pallas_call | solution.py:1531
  920.4 0.6 slice.123
  921.0 0.6 reshape.197
  921.6 0.6 slice.109
  922.2 0.6 fusion.25
  922.8 0.1 slice.134
  922.9 0.6 reshape_squeeze.10
  923.5 0.6 reshape_squeeze.9
  924.1 0.6 slice_bitcast_fusion.1
  924.7 0.1 reshape_squeeze.11
  924.7 0.1 reduce_sum.9
  924.8 0.6 reshape.198
  925.5 0.7 copy.66
  926.2 0.6 copy.67
  926.8 0.5 copy.65
  927.3 1.4 reshape.199
  928.6 1.0 convert_element_type.85
  929.7 3.8 slice_convert_fusion
  933.5 1.5 convert_element_type.87
  935.0 0.9 copy-done.1
  935.8 2.5 convert_element_type.86
  938.4 0.3 copy-done
  938.7 3.4 convert_element_type.80
  (40 shorter events, 0.2 us)
Async XLA Ops:
  293.5 5.1 copy-start.2
  293.5 5.5 copy-start.16
  600.1 6.4 copy-start.5
  600.1 6.4 copy-start.15
  600.1 6.4 copy-start.17
  600.1 12.3 %slice-start = ((s8[6291456]{0:T(1024)(128)(4,1)}), s8[4194304]{0:T(1024)(128)(4,1)S(1)}, s32[]{:S(2)}) async-start(s8[6291456]{0:T(1024)(128)(4,1)} %bitcast.154), calls=%async_computation | async-start | bytes 8388608
  606.5 3.2 copy-start.9
  606.5 6.0 slice-start.1
  609.7 2.8 copy-start.7
  609.7 4.8 copy-start.8
  616.5 1.5 copy-start.11
  618.0 1.6 copy-start.4
  735.2 26.2 %copy-start.13 = (f32[1,2048]{1,0:T(1,128)S(1)}, f32[1,2048]{1,0:T(1,128)}, u32[]{:S(2)}) copy-start(f32[1,2048]{1,0:T(1,128)} %get-tuple-element.129) | copy-start | bytes 24580
  735.2 26.2 %copy-start.14 = (f32[1,2048]{1,0:T(1,128)S(1)}, f32[1,2048]{1,0:T(1,128)}, u32[]{:S(2)}) copy-start(f32[1,2048]{1,0:T(1,128)} %get-tuple-element.128) | copy-start | bytes 24580
  909.1 11.2 %copy-start.12 = (f32[1,9472]{1,0:T(1,128)S(1)}, f32[1,9472]{1,0:T(1,128)}, u32[]{:S(2)}) copy-start(f32[1,9472]{1,0:T(1,128)} %get-tuple-element.137) | copy-start | bytes 113668
  909.1 13.6 %copy-start.6 = (bf16[4,2,432,128]{3,2,1,0:T(8,128)(2,1)S(1)}, bf16[4,2,432,128]{3,2,1,0:T(8,128)(2,1)}, u32[]{:S(2)}) copy-start(bf16[4,2,432,128]{3,2,1,0:T(8,128)(2,1)} %get-tuple-element.140) | copy-start | bytes 2654212
  927.3 1.4 copy-start.10
  929.7 3.8 copy-start.3
  933.5 2.3 copy-start.1
  935.8 2.9 copy-start

commit v8 on v7

--- a/solution.py
+++ b/solution.py
@@ -1367,14 +1367,14 @@
         lanes = pl.ds(pl.multiple_of(place.index * 128, 128), 128)
         for j in range(up_o.shape[0]):
             up_o[j] = up_ref[j, :, lanes]
-        heads = step_ref.shape[1]
+        heads = step_ref.shape[0]
         few = heads // place.plane
         row = lax.broadcasted_iota(jnp.int32, (heads, 128), 0) - place.index * few
         col = lax.broadcasted_iota(jnp.int32, (heads, 128), 1)
         pick = (row == col) & (col < few)
         wide = row == col // (128 // few)
         step_o[...] = lax.dot_general(
-            step_ref[...], pick.astype(bf16), NN, preferred_element_type=f32
+            step_ref[...], pick.astype(bf16), TN, preferred_element_type=f32
         ).astype(bf16)
         small_o[...] = jnp.zeros_like(small_o)
         small_o[0:4, :] = taps_ref[:, lanes]
@@ -1400,7 +1400,7 @@
         out_shape=[
             S((groups, ctx, tp // 2, 2, rows, width), bf16),
             S((*shard[0].shape[:2], 128), bf16),
-            S((shard[1].shape[0], 128), bf16),
+            S((shard[1].shape[1], 128), bf16),
             S((16, 128), f32),
         ]
         + move_outs,
@@ -2051,7 +2051,7 @@
         adapter_down_maps,
         [
             adapter_up_maps,
-            step_size_weight,
+            step_size_weight.T,
             mixer_input_taps,
             mixer_input_tap_bias[None],
             gated_norm_gain[None],

time: 953 us -> 955 us (level)
  no operation moved by 1% of the time
where the time goes in v8:
time: 955 us; the launch traced here: 945 us
  Pallas kernels  884 us (93%)
  matrix products  24.9 us (3%)
  other arithmetic  19.4 us (2%)
  local copies, waits for them, and re-layouts  14.9 us (2%)
    pallas_call x5, Pallas kernels, exchange(): pl.pallas_call(kernel, out_shape=out_shape, in_specs=in_specs, out_specs=...  610 us
    pallas_call x1, Pallas kernels, opening(): pl.pallas_call(kernel, out_shape=[S((groups, ctx, tp // 2, 2, rows, width...  152 us
    pallas_call x1, Pallas kernels, mixer_backward(): pl.pallas_call(kernel, grid=(groups,), in_specs=[by_group(width), pl.Bloc...  30.5 us
    pallas_call x1, Pallas kernels, attention_backward(): pl.pallas_call(kernel, grid=(groups,), in_specs=[by_group(model), by_grou...  26.1 us
    pallas_call x1, Pallas kernels, mixer_forward(): pl.pallas_call(kernel, grid=(groups,), in_specs=[by_group(width), pl.Bloc...  24.6 us

profile of v8, /device:TPU:0, one launch (start us, length us, event | category | flops | bytes accessed | tf_op | source)
XLA Modules:
  0.0 945.0 jit_solution(12944719838529698143)
XLA Ops:
  0.7 0.6 maximum_bitcast_fusion.freq_r
  1.3 1.6 constant_dynamic-slice_fusion.refs_8_
  2.9 151.9 %opening_1.1 = (bf16[4,2,2,2,48,6656]{5,4,3,2,1,0:T(8,128)(2,1)}, bf16[3,128,128]{2,1,0:T(8,128)(2,1)}, bf16[2048,128]{1,0:T(8,128)(2,1)}, f32[16,128]{1,0:T(8,1...) custom-call(bf16[192,2048]{1,0:T(8,128)(2,1)} %refs_5_.7, bf16[192,2048]{1,0:T(8,128)(2,1)} %refs_6_.3, ...), custom_call_target="tpu_custom_call" | custom-call | tf_op jit(solution)/shard_map/opening_1/pallas_call | solution.py:1398
  154.8 16.3 %attention_forward.1 = (bf16[1536,128]{1,0:T(8,128)(2,1)}, bf16[1536,128]{1,0:T(8,128)(2,1)}, bf16[1536,128]{1,0:T(8,128)(2,1)}, bf16[1536,128]{1,0:T(8,128)(2,1...) custom-call(bf16[1536,6656]{1,0:T(8,128)(2,1)} %bitcast.92, bf16[1536,6656]{1,0:T(8,128)(2,1)} %bitcast.93, ...), custom_call_target="tpu_custom_call" | custom-call | tf_op jit(solution)/shard_map/attention_forward/pallas_call | solution.py:1898
  171.1 120.5 %exchange_2.1 = (bf16[4,2,2,2,48,2048]{5,4,3,2,1,0:T(8,128)(2,1)}, f32[48,2048]{1,0:T(8,128)}, bf16[2,2048,256]{2,1,0:T(8,128)(2,1)}, bf16[256,2048]{1,0:T(8,128)(2,1)}) custom-call(bf16[4,2,2,2,48,128]{5,4,3,2,1,0:T(8,128)(2,1)} %bitcast.108, bf16[128,2048]{1,0:T(8,128)(2,1)} %get-tuple-element.89.refs_1_.wo_r, bf16[192,2048]{1,0:T(8,128)(2,1)} %refs_5_.7, ...), custom_call_target="tpu_custom_call" | custom-call | tf_op jit(solution)/shard_map/exchange_2/pallas_call | solution.py:1269
  291.6 5.1 fusion.18
  296.6 0.4 copy-done.16
  297.1 3.6 multiply_convert_fusion.1
  300.7 95.3 %exchange_3.1 = (bf16[4,2,2,2,48,2048]{5,4,3,2,1,0:T(8,128)(2,1)}, f32[48,2048]{1,0:T(8,128)}, bf16[2,2048,128]{2,1,0:T(8,128)(2,1)}, bf16[128,2048]{1,0:T(8,128)(2,1)}) custom-call(bf16[4,2,2,2,48,256]{5,4,3,2,1,0:T(8,128)(2,1)} %bitcast.116, bf16[256,2048]{1,0:T(8,128)(2,1)} %get-tuple-element.92.refs_1_, f32[48,2048]{1,0:T(8,128)} %get-tuple-element.93.refs_2_.refs_3_, ...), custom_call_target="tpu_custom_call" | custom-call | tf_op jit(solution)/shard_map/exchange_3/pallas_call | solution.py:1269
  396.0 24.6 %mixer_forward.1 = (f32[1536,128]{1,0:T(8,128)}, bf16[1536,128]{1,0:T(8,128)(2,1)}, bf16[1536,128]{1,0:T(8,128)(2,1)}, bf16[1536,256]{1,0:T(8,128)(2,1)}, bf16[1...) custom-call(bf16[1536,2048]{1,0:T(8,128)(2,1)} %bitcast.101, bf16[1536,6656]{1,0:T(8,128)(2,1)} %bitcast.94, ...), custom_call_target="tpu_custom_call" | custom-call | tf_op jit(solution)/shard_map/mixer_forward/pallas_call | solution.py:1684
  420.7 14.0 %sum_small_4.1.sums_r = f32[4,2,384]{2,1,0:T(2,128)} custom-call(f32[4,2,384]{2,1,0:T(2,128)} %get-tuple-element.105.x), custom_call_target="tpu_custom_call" | custom-call | tf_op jit(solution)/shard_map/sum_small_4/pallas_call | solution.py:1434
  434.7 30.5 %mixer_backward.1 = (bf16[1536,128]{1,0:T(8,128)(2,1)}, bf16[1536,128]{1,0:T(8,128)(2,1)}, bf16[1536,128]{1,0:T(8,128)(2,1)}, bf16[1536,256]{1,0:T(8,128)(2,1)},...) custom-call(bf16[1536,2048]{1,0:T(8,128)(2,1)} %bitcast.102, ...), custom_call_target="tpu_custom_call" | custom-call | tf_op jit(solution)/shard_map/mixer_backward/pallas_call | solution.py:1811
  465.2 0.7 slice.104
  465.9 0.7 slice_bitcast_fusion.3
  466.6 0.7 convert.13
  467.3 0.8 slice.168
  468.1 128.8 %exchange_5.1 = (bf16[4,2,2,2,48,2304]{5,4,3,2,1,0:T(8,128)(2,1)}, f32[48,2048]{1,0:T(8,128)}, f32[1,2048]{1,0:T(1,128)}, bf16[48,2048]{1,0:T(8,128)(2,1)}, bf16...) custom-call(bf16[4,2,2,2,48,128]{5,4,3,2,1,0:T(8,128)(2,1)} %bitcast.119, bf16[4,2,2,2,48,128]{5,4,3,2,1,0:T(8,128)(2,1)} %bitcast.120, ...), custom_call_target="tpu_custom_call" | custom-call | tf_op jit(solution)/shard_map/exchange_5/pallas_call | solution.py:1269
  597.0 0.0 copy-start.17
  597.0 0.0 slice-start
  597.0 6.3 fusion.22
  603.3 0.0 copy-done.5
  603.3 0.0 copy-done.17
  603.4 0.0 copy-start.9
  603.4 0.0 slice-start.1
  603.4 3.1 multiply_convert_fusion
  606.5 0.0 copy-start.7
  606.6 0.0 copy-start.8
  606.6 2.8 fusion.4.refs_7_
  609.3 0.0 slice-done
  609.4 2.0 fusion.8
  611.4 2.0 fusion.7
  613.4 1.5 pad_maximum_fusion.refs_6_
  614.9 1.0 convert_element_type.91
  615.9 0.6 copy-done.4
  616.5 1.6 convert_element_type.88
  618.1 116.1 %exchange_6.1 = (bf16[4,2,2,2,48,2048]{5,4,3,2,1,0:T(8,128)(2,1)}, f32[48,2048]{1,0:T(8,128)}, f32[1,2048]{1,0:T(1,128)}, bf16[2,256,2048]{2,1,0:T(8,128)(2,1)}, bf16[2048,256]{1,0:T(8,128)(2,1)}) custom-call(bf16[4,2,2,2,48,256]{5,4,3,2,1,0:T(8,128)(2,1)} %bitcast.115, bf16[4,2,2,2,48,256]{5,4,3,2,1,0:T(8,128)(2,1)} %bitcast.114, ...), custom_call_target="tpu_custom_call" | custom-call | tf_op jit(solution)/shard_map/exchange_6/pallas_call | solution.py:1269
  734.2 26.1 %attention_backward.1 = (bf16[1536,128]{1,0:T(8,128)(2,1)}, bf16[1536,128]{1,0:T(8,128)(2,1)}, bf16[1536,128]{1,0:T(8,128)(2,1)}, bf16[1536,384]{1,0:T(8,128)(2,...) custom-call(bf16[1536,2048]{1,0:T(8,128)(2,1)} %bitcast.105, ...), custom_call_target="tpu_custom_call" | custom-call | tf_op jit(solution)/shard_map/attention_backward/pallas_call | solution.py:1974
  760.4 0.6 broadcast_in_dim.31.refs_11_
  761.0 0.9 convert_element_type.76
  761.9 0.7 pad_maximum_fusion.1.refs_12_
  762.6 148.9 %exchange_7.1 = (bf16[4,2,2,2,48,384]{5,4,3,2,1,0:T(8,128)(2,1)}, bf16[2,2,48,6144]{3,2,1,0:T(8,128)(2,1)}, f32[1,9472]{1,0:T(1,128)}, bf16[4,2,432,128]{3,2,1,0...) custom-call(bf16[4,2,2,2,48,128]{5,4,3,2,1,0:T(8,128)(2,1)} %bitcast.124, ...), custom_call_target="tpu_custom_call" | custom-call | tf_op jit(solution)/shard_map/exchange_7/pallas_call | solution.py:1269
  911.5 11.2 %adapter_products.1 = f32[3,4096,128]{2,1,0:T(8,128)} custom-call(bf16[1536,6656]{1,0:T(8,128)(2,1)} %bitcast.100, bf16[1536,384]{1,0:T(8,128)(2,1)} %bitcast.110), custom_call_target="tpu_custom_call" | custom-call | tf_op jit(solution)/shard_map/adapter_products/pallas_call | solution.py:1531
  922.7 0.6 slice.123
  923.3 0.6 reshape.197
  923.9 0.6 slice.109
  924.5 0.6 fusion.25
  925.1 0.1 slice.134
  925.2 0.6 reshape_squeeze.10
  925.8 0.6 reshape_squeeze.9
  926.4 0.6 slice_bitcast_fusion.1
  927.0 0.1 reshape_squeeze.11
  927.1 0.1 reduce_sum.9
  927.2 0.6 reshape.198
  927.8 0.7 copy.64
  928.5 0.6 copy.65
  929.1 0.5 copy.63
  929.6 1.4 reshape.199
  931.0 1.0 convert_element_type.85
  932.0 3.8 slice_convert_fusion
  935.8 1.5 convert_element_type.87
  937.3 0.9 copy-done.1
  938.2 2.5 convert_element_type.86
  940.7 0.3 copy-done
  941.1 3.4 convert_element_type.80
  (39 shorter events, 0.2 us)
Async XLA Ops:
  291.6 5.1 copy-start.2
  291.6 5.5 copy-start.16
  597.0 6.4 copy-start.5
  597.0 6.4 copy-start.15
  597.0 6.4 copy-start.17
  597.0 12.3 %slice-start = ((s8[6291456]{0:T(1024)(128)(4,1)}), s8[4194304]{0:T(1024)(128)(4,1)S(1)}, s32[]{:S(2)}) async-start(s8[6291456]{0:T(1024)(128)(4,1)} %bitcast.156), calls=%async_computation | async-start | bytes 8388608
  603.4 3.2 copy-start.9
  603.4 6.0 slice-start.1
  606.5 2.8 copy-start.7
  606.6 4.8 copy-start.8
  613.4 1.5 copy-start.11
  614.9 1.6 copy-start.4
  734.2 26.2 %copy-start.13 = (f32[1,2048]{1,0:T(1,128)S(1)}, f32[1,2048]{1,0:T(1,128)}, u32[]{:S(2)}) copy-start(f32[1,2048]{1,0:T(1,128)} %get-tuple-element.129) | copy-start | bytes 24580
  734.2 26.2 %copy-start.14 = (f32[1,2048]{1,0:T(1,128)S(1)}, f32[1,2048]{1,0:T(1,128)}, u32[]{:S(2)}) copy-start(f32[1,2048]{1,0:T(1,128)} %get-tuple-element.128) | copy-start | bytes 24580
  911.5 11.2 %copy-start.12 = (f32[1,9472]{1,0:T(1,128)S(1)}, f32[1,9472]{1,0:T(1,128)}, u32[]{:S(2)}) copy-start(f32[1,9472]{1,0:T(1,128)} %get-tuple-element.137) | copy-start | bytes 113668
  911.5 13.6 %copy-start.6 = (bf16[4,2,432,128]{3,2,1,0:T(8,128)(2,1)S(1)}, bf16[4,2,432,128]{3,2,1,0:T(8,128)(2,1)}, u32[]{:S(2)}) copy-start(bf16[4,2,432,128]{3,2,1,0:T(8,128)(2,1)} %get-tuple-element.140) | copy-start | bytes 2654212
  929.6 1.4 copy-start.10
  932.0 3.8 copy-start.3
  935.8 2.3 copy-start.1
  938.2 2.9 copy-start
